TPU v7x, 32 devices: a whole 2x2x4 slice. The times are simulated.
32 devices in a mesh: tp: 4 (over z), cp: 2 (over y), fsdp: 4 (over x, core).
Axes of the slice: x: 2, y: 2, z: 4, core: 2. Of those that a mesh axis runs over, the one named last changes fastest.
Arguments:
- hidden: bfloat16 [4, 2048, 4096], P('fsdp', 'cp')
- cotangent: bfloat16 [4, 2048, 4096], P('fsdp', 'cp')
- positions: int32 [2048], P('cp')
- gain: bfloat16 [4096], P('fsdp')
- w_query: bfloat16 [4096, 32, 128], P('fsdp', 'tp')
- w_key: bfloat16 [4096, 8, 128], P('fsdp', 'tp')
- w_value: bfloat16 [4096, 8, 128], P('fsdp', 'tp')
- w_out: bfloat16 [32, 128, 4096], P('tp', None, 'fsdp')
Outputs:
- output 1: bfloat16 [4, 2048, 4096], P('fsdp', 'cp')
- output 2: bfloat16 [4, 2048, 4096], P('fsdp', 'cp')
- output 3: float32 [4096], P('fsdp')
- output 4: float32 [4096, 32, 128], P('fsdp', 'tp')
- output 5: float32 [4096, 8, 128], P('fsdp', 'tp')
- output 6: float32 [4096, 8, 128], P('fsdp', 'tp')
- output 7: float32 [32, 128, 4096], P('tp', None, 'fsdp')
All inputs are finite; a program needn't handle non-finite values.
Results may differ from a plain program's by a relative error of at most 0.0138206.
Values are sent between devices in bfloat16 or wider.
A program may use at most 1 GiB of HBM per device.

v0:
```python
import math
import jax
import jax.numpy as jnp
from jax import lax
from jax.sharding import PartitionSpec as P

WINDOW_LEN = 4096
ROPE_BASE = 10000.0
NORM_EPS = 1e-5
NEG_BIG = -1e30


def rope_tables(positions, head_dim):
    inv_freq = ROPE_BASE ** (-jnp.arange(0, head_dim, 2).astype(jnp.float32) / head_dim)
    angles = positions.astype(jnp.float32)[:, None] * inv_freq[None, :]
    return jnp.cos(angles), jnp.sin(angles)


def rope_apply(head_vals, cosines, sines, sign):
    half_dim = head_vals.shape[-1] // 2
    first_half = head_vals[..., :half_dim]
    second_half = head_vals[..., half_dim:]
    cos_b = cosines[:, None, :]
    sin_b = sines[:, None, :] * sign
    return jnp.concatenate([first_half * cos_b - second_half * sin_b, second_half * cos_b + first_half * sin_b], axis=-1)


def tile_layout(q_len, key_len):
    q_tile = math.gcd(q_len, 512)
    return q_tile, min(q_tile + WINDOW_LEN, key_len), q_len // q_tile


def tile_scores(q_blk, k_blk, q_start, k_start, score_scale):
    scores = jnp.einsum("qkgd,skd->kgqs", q_blk, k_blk, preferred_element_type=jnp.float32) * score_scale
    q_idx = q_start + jnp.arange(q_blk.shape[0])
    k_idx = k_start + jnp.arange(k_blk.shape[0])
    allowed = (k_idx[None, :] <= q_idx[:, None]) & (k_idx[None, :] > q_idx[:, None] - WINDOW_LEN) & (k_idx[None, :] >= 0)
    return jnp.where(allowed, scores, NEG_BIG)


def tile_inputs(tile_id, q_grp, k_span, v_span, q_origin, k_origin):
    num_rows, q_len, kv_heads, group_size, head_dim = q_grp.shape
    key_len = k_span.shape[1]
    q_tile, span_len, n_tiles = tile_layout(q_len, key_len)
    row_idx = tile_id // n_tiles
    q_off = (tile_id % n_tiles) * q_tile
    k_off = jnp.clip(q_origin - k_origin + q_off + q_tile - span_len, 0, key_len - span_len)
    q_blk = lax.dynamic_slice(q_grp, (row_idx, q_off, 0, 0, 0), (1, q_tile, kv_heads, group_size, head_dim))[0]
    k_blk = lax.dynamic_slice(k_span, (row_idx, k_off, 0, 0), (1, span_len, kv_heads, head_dim))[0]
    v_blk = lax.dynamic_slice(v_span, (row_idx, k_off, 0, 0), (1, span_len, kv_heads, head_dim))[0]
    return row_idx, q_off, k_off, q_blk, k_blk, v_blk


def attn_forward(q_grp, k_span, v_span, q_origin, k_origin):
    num_rows, q_len, kv_heads, group_size, head_dim = q_grp.shape
    q_tile, span_len, n_tiles = tile_layout(q_len, k_span.shape[1])
    score_scale = head_dim ** -0.5

    def one_tile(tile_id):
        row_idx, q_off, k_off, q_blk, k_blk, v_blk = tile_inputs(tile_id, q_grp, k_span, v_span, q_origin, k_origin)
        scores = tile_scores(q_blk, k_blk, q_origin + q_off, k_origin + k_off, score_scale)
        row_max = jnp.max(scores, axis=-1, keepdims=True)
        exp_scores = jnp.exp(scores - row_max)
        row_total = jnp.sum(exp_scores, axis=-1, keepdims=True)
        prob_bf = (exp_scores / row_total).astype(jnp.bfloat16)
        out_blk = jnp.einsum("kgqs,skd->qkgd", prob_bf, v_blk, preferred_element_type=jnp.float32).astype(jnp.bfloat16)
        return out_blk, row_max + jnp.log(row_total)

    attn_tiles, log_norm = lax.map(one_tile, jnp.arange(num_rows * n_tiles))
    return attn_tiles.reshape(num_rows, q_len, kv_heads * group_size, head_dim), log_norm


def attn_backward(q_grp, k_span, v_span, d_attn, log_norm, q_origin, k_origin):
    num_rows, q_len, kv_heads, group_size, head_dim = q_grp.shape
    key_len = k_span.shape[1]
    q_tile, span_len, n_tiles = tile_layout(q_len, key_len)
    score_scale = head_dim ** -0.5
    d_grp = d_attn.reshape(num_rows, q_len, kv_heads, group_size, head_dim)

    def one_tile(acc_pair, tile_id):
        dk_acc, dv_acc = acc_pair
        row_idx, q_off, k_off, q_blk, k_blk, v_blk = tile_inputs(tile_id, q_grp, k_span, v_span, q_origin, k_origin)
        d_blk = lax.dynamic_slice(d_grp, (row_idx, q_off, 0, 0, 0), (1, q_tile, kv_heads, group_size, head_dim))[0]
        scores = tile_scores(q_blk, k_blk, q_origin + q_off, k_origin + k_off, score_scale)
        prob_vals = jnp.exp(scores - lax.dynamic_index_in_dim(log_norm, tile_id, 0, keepdims=False))
        dv_blk = jnp.einsum("kgqs,qkgd->skd", prob_vals.astype(jnp.bfloat16), d_blk, preferred_element_type=jnp.float32)
        d_probs = jnp.einsum("qkgd,skd->kgqs", d_blk, v_blk, preferred_element_type=jnp.float32)
        row_dot = jnp.sum(prob_vals * d_probs, axis=-1, keepdims=True)
        d_scores = (prob_vals * (d_probs - row_dot) * score_scale).astype(jnp.bfloat16)
        dq_blk = jnp.einsum("kgqs,skd->qkgd", d_scores, k_blk, preferred_element_type=jnp.float32)
        dk_blk = jnp.einsum("kgqs,qkgd->skd", d_scores, q_blk, preferred_element_type=jnp.float32)
        where_k = (row_idx, k_off, 0, 0)
        acc_shape = (1, span_len, kv_heads, head_dim)
        dk_acc = lax.dynamic_update_slice(dk_acc, lax.dynamic_slice(dk_acc, where_k, acc_shape) + dk_blk[None], where_k)
        dv_acc = lax.dynamic_update_slice(dv_acc, lax.dynamic_slice(dv_acc, where_k, acc_shape) + dv_blk[None], where_k)
        return (dk_acc, dv_acc), dq_blk

    zero_acc = jnp.zeros((num_rows, key_len, kv_heads, head_dim), jnp.float32)
    acc_pair, dq_tiles = lax.scan(one_tile, (zero_acc, zero_acc), jnp.arange(num_rows * n_tiles))
    return dq_tiles.reshape(num_rows, q_len, kv_heads * group_size, head_dim), acc_pair[0], acc_pair[1]


def reduce_grad(full_grad, dim):
    return lax.psum(lax.psum_scatter(full_grad, "fsdp", scatter_dimension=dim, tiled=True), "cp")


def solution(mesh):
    act_spec = P("fsdp", "cp", None)
    proj_spec = P("fsdp", "tp", None)
    wout_spec = P("tp", None, "fsdp")

    def device_step(hidden, cotangent, positions, gain, w_query, w_key, w_value, w_out):
        num_rows, q_len = hidden.shape[0], hidden.shape[1]
        gain_full = lax.all_gather(gain, "fsdp", axis=0, tiled=True).astype(jnp.float32)
        wq_full = lax.all_gather(w_query, "fsdp", axis=0, tiled=True)
        wk_full = lax.all_gather(w_key, "fsdp", axis=0, tiled=True)
        wv_full = lax.all_gather(w_value, "fsdp", axis=0, tiled=True)
        wo_full = lax.all_gather(w_out, "fsdp", axis=2, tiled=True)
        q_heads, head_dim = wq_full.shape[1], wq_full.shape[2]
        kv_heads = wk_full.shape[1]
        cosines, sines = rope_tables(positions, head_dim)
        q_origin = lax.axis_index("cp") * q_len

        hidden_f = hidden.astype(jnp.float32)
        inv_rms = lax.rsqrt(jnp.mean(hidden_f * hidden_f, axis=-1, keepdims=True) + NORM_EPS)
        x_hat = hidden_f * inv_rms
        normed = (x_hat * gain_full).astype(jnp.bfloat16)
        q_rot = rope_apply(jnp.einsum("duo,ojf->dujf", normed, wq_full, preferred_element_type=jnp.float32), cosines, sines, 1.0).astype(jnp.bfloat16)
        k_rot = rope_apply(jnp.einsum("duo,ojf->dujf", normed, wk_full, preferred_element_type=jnp.float32), cosines, sines, 1.0).astype(jnp.bfloat16)
        v_loc = jnp.einsum("duo,ojf->dujf", normed, wv_full, preferred_element_type=jnp.float32).astype(jnp.bfloat16)
        k_all = lax.all_gather(k_rot, "cp", axis=1, tiled=True)
        v_all = lax.all_gather(v_loc, "cp", axis=1, tiled=True)
        q_grp = q_rot.reshape(num_rows, q_len, kv_heads, q_heads // kv_heads, head_dim)
        attn_out, log_norm = attn_forward(q_grp, k_all, v_all, q_origin, 0)
        mixed_out = lax.psum(jnp.einsum("bshd,hdm->bsm", attn_out, wo_full, preferred_element_type=jnp.float32), "tp")
        block_out = (hidden_f + mixed_out).astype(jnp.bfloat16)

        grad_wout = jnp.einsum("bshd,bsm->hdm", attn_out, cotangent, preferred_element_type=jnp.float32)
        d_attn = jnp.einsum("bsm,hdm->bshd", cotangent, wo_full, preferred_element_type=jnp.float32).astype(jnp.bfloat16)
        dq_rot, dk_all, dv_all = attn_backward(q_grp, k_all, v_all, d_attn, log_norm, q_origin, 0)
        dk_rot = lax.psum_scatter(dk_all, "cp", scatter_dimension=1, tiled=True)
        dv_loc = lax.psum_scatter(dv_all, "cp", scatter_dimension=1, tiled=True).astype(jnp.bfloat16)
        dq_lin = rope_apply(dq_rot, cosines, sines, -1.0).astype(jnp.bfloat16)
        dk_lin = rope_apply(dk_rot, cosines, sines, -1.0).astype(jnp.bfloat16)
        grad_query = jnp.einsum("duo,dujf->ojf", normed, dq_lin, preferred_element_type=jnp.float32)
        grad_key = jnp.einsum("duo,dujf->ojf", normed, dk_lin, preferred_element_type=jnp.float32)
        grad_value = jnp.einsum("duo,dujf->ojf", normed, dv_loc, preferred_element_type=jnp.float32)
        d_part = jnp.einsum("dujf,ojf->duo", dq_lin, wq_full, preferred_element_type=jnp.float32) + jnp.einsum("dujf,ojf->duo", dk_lin, wk_full, preferred_element_type=jnp.float32) + jnp.einsum("dujf,ojf->duo", dv_loc, wv_full, preferred_element_type=jnp.float32)
        d_normed = lax.psum(d_part, "tp")
        grad_gain = jnp.sum(d_normed * x_hat, axis=(0, 1))
        value_a6 = d_normed * gain_full
        grad_hidden = (cotangent.astype(jnp.float32) + inv_rms * (value_a6 - x_hat * jnp.mean(value_a6 * x_hat, axis=-1, keepdims=True))).astype(jnp.bfloat16)
        return (block_out, grad_hidden, reduce_grad(grad_gain, 0), reduce_grad(grad_query, 0), reduce_grad(grad_key, 0), reduce_grad(grad_value, 0), reduce_grad(grad_wout, 2))

    return jax.shard_map(device_step, mesh=mesh, in_specs=(act_spec, act_spec, P("cp"), P("fsdp"), proj_spec, proj_spec, proj_spec, wout_spec), out_specs=(act_spec, act_spec, P("fsdp"), proj_spec, proj_spec, proj_spec, wout_spec), check_vma=False)
```

profile of v0, /device:TPU:0, one launch (start us, length us, event | category | flops | bytes accessed | tf_op | source)
XLA Modules:
  0.0 2370.8 jit_solution(145926162370201299)
XLA Ops:
  84.5 58.9 %all-gather.8.cloned.1.call-done = bf16[4096,8,128]{0,2,1:T(8,128)(2,1)} async-done(((bf16[1024,8,128]{0,2,1:T(8,128)(2,1)}), bf16[4096,8,128]{0,2,1:T(8,128)(2,1)}) %all-gather.8.cloned.1.call-update) | async-done | bytes 8388624 | tf_op jit(solution)/shard_map/all_gather | solution.py:115
  167.1 98.5 %while.35 = (s32[]{:T(128)}, bf16[2,512,2,4,128]{4,1,0,3,2:T(8,128)(2,1)}, f32[2,2,4,512,1]{3,2,1,4,0:T(4,128)S(1)}, s32[2]{0:T(128)S(1)}, s32[]{:T(128)}, /*ind...) while((s32[]{:T(128)}, ...), condition=%wide.region_4.5_spmd, body=%wide.region_1.4_spmd.sunk | while | flops 4400352256 | bytes 113406856 | solution.py:69
  170.9 15.1 bitcast_reduce_fusion.2
  201.2 15.3 fusion.200
  250.3 15.3 fusion.200
  280.5 310.6 %while.36 = (s32[]{:T(128)}, f32[1,2048,2,128]{1,3,2,0:T(8,128)}, f32[1,2048,2,128]{1,3,2,0:T(8,128)}, f32[2,512,2,4,128]{1,0,4,3,2:T(2,128)}, s32[2]{0:T(128)S(...) while((s32[]{:T(128)}, f32[1,2048,2,128]{1,3,2,0:T(8,128)}, ...), condition=%wide.region_8.9_spmd.clone, body=%wide.region_6.8_spmd.clone.sunk | while | flops 17404284928 | bytes 252853744 | solution.py:99
  299.0 38.0 %fusion.220 = f32[1,512,2,4,128]{4,1,3,2,0:T(8,128)} fusion(f32[2,512,4,2048]{3,1,2,0:T(8,128)} %fusion.217, f32[2,4,512]{2,1,0:T(4,128)S(1)} %dynamic-slice_bitcast_fusion.2, pred[512,2048]{1,0:T(8,128)(4,1)S(1)} %and_and_fusion.5, bf16[1,2048,2,128]{3,1,2,0:T(8,128)(2,1)} %get-tuple-element.791, ...), kind=kOutput, calls=%fused_computation.44.clone.1 | convolution fusion | flops 6534731776 | bytes 76579840 | tf_op jit(solution)/shard_map/while/body/eval_jaxpr/kgqs,skd->qkgd/dot_general | solution.py:90
  341.6 38.1 %dynamic_update_slice.40 = f32[2,512,2,4,128]{1,0,4,3,2:T(2,128)} dynamic-update-slice(f32[2,512,2,4,128]{1,0,4,3,2:T(2,128)} %get-tuple-element.767, f32[1,512,2,4,128]{1,0,4,3,2:T(1,128)S(1)} %copy.123, s32[]{:T(128)} %get-tuple-element.764, s32[]{:T(128)} %constant.251.clone.1..sunk.1, s32[]{:T(128)} %constant.251.clone.1..sunk.1, s32[]{:T(128)} %constant.251.clone.1..sunk.1, ...) | dynamic-update-slice | bytes 4194308 | tf_op jit(solution)/shard_map/while/body/jit(dynamic_update_index_in_dim)/dynamic_update_slice | solution.py:99
  379.7 17.2 fusion.219
  396.9 37.5 %fusion.218 = f32[1,2048,2,128]{1,3,2,0:T(8,128)} fusion(f32[2,512,4,2048]{3,1,2,0:T(8,128)} %fusion.217, f32[2,4,512]{2,1,0:T(4,128)S(1)} %dynamic-slice_bitcast_fusion.2, pred[512,2048]{1,0:T(8,128)(4,1)} %copy-done, f32[1,2048,2,128]{1,3,2,0:T(8,128)} %get-tuple-element.765, bf16[1,2048,2,128]{3,1,2,0:T(8,128)(2,1)} %get-tuple-element.791, ...), kind=kOutput, calls=%fused_computation.42.clone.1 | convolution fusion | flops 6535780352 | bytes 78678016 | tf_op jit(solution)/shard_map/while/body/eval_jaxpr/kgqs,qkgd->skd/dot_general | solution.py:91
  452.4 37.9 %fusion.220 = f32[1,512,2,4,128]{4,1,3,2,0:T(8,128)} fusion(f32[2,512,4,2048]{3,1,2,0:T(8,128)} %fusion.217, f32[2,4,512]{2,1,0:T(4,128)S(1)} %dynamic-slice_bitcast_fusion.2, pred[512,2048]{1,0:T(8,128)(4,1)S(1)} %and_and_fusion.5, bf16[1,2048,2,128]{3,1,2,0:T(8,128)(2,1)} %get-tuple-element.791, ...), kind=kOutput, calls=%fused_computation.44.clone.1 | convolution fusion | flops 6534731776 | bytes 76579840 | tf_op jit(solution)/shard_map/while/body/eval_jaxpr/kgqs,skd->qkgd/dot_general | solution.py:90
  495.0 38.1 %dynamic_update_slice.40 = f32[2,512,2,4,128]{1,0,4,3,2:T(2,128)} dynamic-update-slice(f32[2,512,2,4,128]{1,0,4,3,2:T(2,128)} %get-tuple-element.767, f32[1,512,2,4,128]{1,0,4,3,2:T(1,128)S(1)} %copy.123, s32[]{:T(128)} %get-tuple-element.764, s32[]{:T(128)} %constant.251.clone.1..sunk.1, s32[]{:T(128)} %constant.251.clone.1..sunk.1, s32[]{:T(128)} %constant.251.clone.1..sunk.1, ...) | dynamic-update-slice | bytes 4194308 | tf_op jit(solution)/shard_map/while/body/jit(dynamic_update_index_in_dim)/dynamic_update_slice | solution.py:99
  533.1 17.8 fusion.219
  550.9 40.1 %fusion.218 = f32[1,2048,2,128]{1,3,2,0:T(8,128)} fusion(f32[2,512,4,2048]{3,1,2,0:T(8,128)} %fusion.217, f32[2,4,512]{2,1,0:T(4,128)S(1)} %dynamic-slice_bitcast_fusion.2, pred[512,2048]{1,0:T(8,128)(4,1)} %copy-done, f32[1,2048,2,128]{1,3,2,0:T(8,128)} %get-tuple-element.765, bf16[1,2048,2,128]{3,1,2,0:T(8,128)(2,1)} %get-tuple-element.791, ...), kind=kOutput, calls=%fused_computation.42.clone.1 | convolution fusion | flops 6535780352 | bytes 78678016 | tf_op jit(solution)/shard_map/while/body/eval_jaxpr/kgqs,qkgd->skd/dot_general | solution.py:91
  591.9 31.2 %reduce-scatter.7.cloned.1.call-done = f32[1,1024,2,128]{1,3,2,0:T(8,128)} async-done(((f32[1,2048,2,128]{1,3,2,0:T(8,128)}), f32[1,1024,2,128]{1,3,2,0:T(8,128)}) %reduce-scatter.7.cloned.1.call-update) | async-done | bytes 1048592 | tf_op jit(solution)/shard_map/reduce_scatter | solution.py:141
  635.0 22.2 reduce-scatter.9.cloned.1.call-done
  691.4 16.2 fusion.123
  707.6 15.1 fusion.142
  745.7 18.5 fusion.122
  764.3 113.6 %reduce-scatter.11.cloned.1.call-done = f32[1024,8,128]{2,0,1:T(8,128)} async-done(((f32[4096,8,128]{2,0,1:T(8,128)}), f32[1024,8,128]{2,0,1:T(8,128)}) %reduce-scatter.11.cloned.1.call-update) | async-done | bytes 4194320 | tf_op jit(solution)/shard_map/reduce_scatter | solution.py:104
  877.9 126.8 %reduce-scatter.17.cloned.1.call-done = f32[8,128,1024]{2,1,0:T(8,128)} async-done(((f32[8,128,4096]{2,1,0:T(8,128)}), f32[8,128,1024]{2,1,0:T(8,128)}) %reduce-scatter.17.cloned.1.call-update) | async-done | bytes 4194320 | tf_op jit(solution)/shard_map/reduce_scatter | solution.py:104
  1005.9 1101.1 %all-reduce.6.cloned.1.call-done = (f32[1,1024,4096]{2,1,0:T(8,128)}, f32[1,1024,4096]{2,1,0:T(8,128)}) async-done(((f32[1,1024,4096]{2,1,0:T(8,128)}, f32[1,1024,4096]{2,1,0:T(8,128)}), (f32[1,1024,4096]{2,1,0:T(8,128)}, f32[1,1024,4096]{2,1,0:T(8,128)})) %all-reduce.6.cloned.1.call-update) | async-done | bytes 33554448 | tf_op jit(solution)/shard_map/psum | solution.py:135
  2134.1 24.0 %fusion.118 = (bf16[1,1024,4096]{2,1,0:T(8,128)(2,1)}, bf16[1,1024,4096]{2,1,0:T(8,128)(2,1)}) fusion(bf16[1,1024,4096]{2,1,0:T(8,128)(2,1)} %param.12, bf16[1,1024,4096]{2,1,0:T(8,128)(2,1)} %param.13, f32[1,1024,4096]{2,1,0:T(8,128)} %get-tuple-element.553, f32[1024]{0:T(1024)S(1)} %broadcast_multiply_fusion.1, f32[4096]{0:T(1024)S(1)} %copy-done.14, ...), kind=kLoop, calls=%fused_computation.94 | loop fusion | flops 46137344 | bytes 67133440 | tf_op jit(solution)/shard_map/convert_element_type | solution.py:152
  2158.1 193.3 %all-reduce.8.cloned.1.call-done = (f32[1024,8,128]{2,0,1:T(8,128)}, f32[1024,2,128]{2,0,1:T(8,128)}, f32[1024,2,128]{2,0,1:T(8,128)}, f32[8,128,1024]{2,1,0:T(8,128)}) async-done(((f32[1024,8,128]{2,0,1:T(8,128)}, f32[1024,2,128]{2,0,1:T(8,128)}, f32[1024,2,128]{2,0,1:T(8,128)}, f32[8,128,1024]{2,1,0:T(8,128)}), (f32[1024,8,128]{2,0,1:T(8,128)}, f32[1024,2,128]{2,0,1:T(8,128)}, f32[1024,2,128]{2,0,1:T(8,128)}, ...) | async-done | bytes 10485776 | tf_op jit(solution)/shard_map/psum | solution.py:104
  (156 shorter events, 313.1 us)
Async XLA Ops:
  7.2 28.0 %all-gather.10.cloned.1.call-start = ((), (), s32[]{:S(2)}) async-start(), calls=%async_computation.7 | async-start | bytes 2621440 | tf_op jit(solution)/shard_map/all_gather | solution.py:116
  9.2 50.5 %all-gather.14.cloned.1.call-start = ((), (), s32[]{:S(2)}) async-start(), calls=%async_computation.9 | async-start | bytes 2621440 | tf_op jit(solution)/shard_map/all_gather | solution.py:117
  11.2 71.7 %all-gather.12.cloned.1.call-start = ((), (), s32[]{:S(2)}) async-start(), calls=%async_computation.8 | async-start | bytes 1572864 | tf_op jit(solution)/shard_map/all_gather | solution.py:131
  17.4 126.0 %copy-start.13 = (f32[4096]{0:T(1024)}, f32[4096]{0:T(1024)S(1)}, u32[]{:S(2)}) copy-start(f32[4096]{0:T(1024)S(1)} %convert_element_type.110) | copy-start | bytes 49156
  23.2 120.2 %copy-start.15 = (f32[1024]{0:T(1024)}, f32[1024]{0:T(1024)S(1)}, u32[]{:S(2)}) copy-start(f32[1024]{0:T(1024)S(1)} %add_rsqrt_fusion) | copy-start | bytes 12292
  25.0 131.2 %copy-start.3 = (f32[1024,64]{0,1:T(8,128)}, f32[1024,64]{0,1:T(8,128)S(1)}, u32[]{:S(2)}) copy-start(f32[1024,64]{0,1:T(8,128)S(1)} %get-tuple-element.576) | copy-start | bytes 786436
  42.8 100.6 %all-gather.8.cloned.1.call-start = ((), (), s32[]{:S(2)}) async-start(), calls=%async_computation.6 | async-start | bytes 10485760 | tf_op jit(solution)/shard_map/all_gather | solution.py:115
  45.8 121.3 %all-gather.18.cloned.1.call-start = ((), (), s32[]{:S(2)}) async-start(), calls=%async_computation.17 | async-start | bytes 1572864 | tf_op jit(solution)/shard_map/all_gather | solution.py:132
  66.9 198.7 %all-gather.16.cloned.1.call-start = ((), (), s32[]{:S(2)}) async-start(), calls=%async_computation.10 | async-start | bytes 10485760 | tf_op jit(solution)/shard_map/all_gather | solution.py:118
  67.5 555.7 %reduce-scatter.7.cloned.1.call-start = ((), (), s32[]{:S(2)}) async-start(), calls=%async_computation.11 | async-start | bytes 3145728 | tf_op jit(solution)/shard_map/reduce_scatter | solution.py:141
  186.0 15.1 copy-start.17
  280.4 342.7 %copy-start.4 = (f32[1024,64]{0,1:T(8,128)S(1)}, f32[1024,64]{0,1:T(8,128)}, u32[]{:S(2)}) copy-start(f32[1024,64]{0,1:T(8,128)} %copy-done.3) | copy-start | bytes 786436
  280.5 344.1 %copy-start.14 = (f32[4096]{0:T(1024)S(1)}, f32[4096]{0:T(1024)}, u32[]{:S(2)}) copy-start(f32[4096]{0:T(1024)} %copy-done.13) | copy-start | bytes 49156
  280.5 344.1 %copy-start.16 = (f32[1024]{0:T(1024)S(1)}, f32[1024]{0:T(1024)}, u32[]{:S(2)}) copy-start(f32[1024]{0:T(1024)} %copy-done.15) | copy-start | bytes 12292
  379.7 17.2 copy-start.2
  533.1 17.8 copy-start.2
  591.1 66.0 %reduce-scatter.9.cloned.1.call-start = ((), (), s32[]{:S(2)}) async-start(), calls=%async_computation.12 | async-start | bytes 3145728 | tf_op jit(solution)/shard_map/reduce_scatter | solution.py:142
  591.9 172.4 %reduce-scatter.13.cloned.1.call-start = ((), (), s32[]{:S(2)}) async-start(), calls=%async_computation.14 | async-start | bytes 5242880 | tf_op jit(solution)/shard_map/reduce_scatter | solution.py:104
  635.0 129.3 %reduce-scatter.15.cloned.1.call-start = ((), (), s32[]{:S(2)}) async-start(), calls=%async_computation.15 | async-start | bytes 5242880 | tf_op jit(solution)/shard_map/reduce_scatter | solution.py:104
  665.9 211.9 %reduce-scatter.11.cloned.1.call-start = ((), (), s32[]{:S(2)}) async-start(), calls=%async_computation.13 | async-start | bytes 20971520 | tf_op jit(solution)/shard_map/reduce_scatter | solution.py:104
  691.3 313.3 %reduce-scatter.17.cloned.1.call-start = ((), (), s32[]{:S(2)}) async-start(), calls=%async_computation.16 | async-start | bytes 20971520 | tf_op jit(solution)/shard_map/reduce_scatter | solution.py:104
  707.6 1399.4 %all-reduce.6.cloned.1.call-start = ((), (), s32[]{:S(2)}) async-start(), calls=%async_computation.18 | async-start | bytes 67108864 | tf_op jit(solution)/shard_map/psum | solution.py:135
  764.2 240.5 %copy-start.18 = (u32[32]{0:T(128)S(1)}, u32[32]{0:T(128)}, u32[]{:S(2)}) copy-start(u32[32]{0:T(128)} %constant.269) | copy-start | bytes 388
  764.2 1587.2 %all-reduce.8.cloned.1.call-start = ((), (), s32[]{:S(2)}) async-start(), calls=%async_computation.19 | async-start | bytes 20971520 | tf_op jit(solution)/shard_map/psum | solution.py:104
  (12 other events, 96.6 us)
Sparse Core Ops, SparseCore 0:
  10.1 25.0 all-gather.9
  37.3 22.3 all-gather.13
  61.8 21.0 all-gather.11
  84.9 58.4 all-gather.7
  144.8 21.0 all-gather.17
  167.3 58.4 all-gather.15
  591.3 31.8 reduce-scatter.6
  625.4 31.7 reduce-scatter.8
  660.3 43.8 reduce-scatter.12
  707.1 43.8 reduce-scatter.14
  753.5 124.2 reduce-scatter.10
  880.3 124.2 reduce-scatter.16
  1007.3 1099.6 all-reduce.5
  2109.5 241.9 all-reduce.7
where the time goes:
time: 2380 us; the launch traced here: 2370 us
  waiting for transfers between devices  1690 us (71%)
  matrix products  423 us (18%)
  local copies, waits for them, and re-layouts  122 us (5%)
  other arithmetic  87.7 us (4%)
    psum x1, waiting for transfers between devices, device_step(): lax.psum(jnp.einsum('bshd,hdm->bsm', attn_out, wo_full, preferred_element...  1100 us
    reduce_scatter x4, waiting for transfers between devices, reduce_grad(): lax.psum_scatter(full_grad, 'fsdp', scatter_dimension=dim, tiled=True)  240 us
    psum x1, waiting for transfers between devices, reduce_grad(): lax.psum(lax.psum_scatter(full_grad, 'fsdp', scatter_dimension=dim, tiled...  193 us
    dynamic_update_slice x4, local copies, waits for them, and re-layouts, attn_backward(): lax.scan(one_tile, (zero_acc, zero_acc), jnp.arange(num_rows * n_tiles))  85.4 us
    dot_general x2, matrix products, one_tile(): jnp.einsum('kgqs,qkgd->skd', d_scores, q_blk, preferred_element_type=jnp....  77.6 us
    dot_general x2, matrix products, one_tile(): jnp.einsum('kgqs,skd->qkgd', d_scores, k_blk, preferred_element_type=jnp....  75.9 us
    all_gather x1, waiting for transfers between devices, device_step(): wq_full = lax.all_gather(w_query, 'fsdp', axis=0, tiled=True)  58.9 us
    dot_general x4, matrix products, tile_scores(): jnp.einsum('qkgd,skd->kgqs', q_blk, k_blk, preferred_element_type=jnp.flo...  56.5 us
  transfers between devices with their start and end apart: 14, of which 10 were waited for; matrix products, arithmetic and copies ran while one was open for 13% of the time, Pallas kernels for 0%

commit v1 on v0

v1 whole, which is shorter than its diff:
```python
import functools
import math

import jax
import jax.numpy as jnp
from jax import lax
from jax.experimental import pallas as pl
from jax.experimental.pallas import tpu as pltpu
from jax.sharding import PartitionSpec as P

WINDOW_LEN = 4096
ROPE_BASE = 10000.0
NORM_EPS = 1e-5
NEG_BIG = -1e30
LOG2E = math.log2(math.e)
TILES = 4
CHUNKS = 16
PIECES = 4
O_PIECES = 2
GRAD_CHUNKS = 8
FIRST_X = 5
EARLY = 6
VMEM_BYTES = 67043328

MESH = pl.DeviceIdType.MESH
ANY = pl.BlockSpec(memory_space=pl.ANY)
VMEM = pl.BlockSpec(memory_space=pltpu.VMEM)
DMA = pltpu.SemaphoreType.DMA
BF, F32 = jnp.bfloat16, jnp.float32

NT = (((1,), (1,)), ((), ()))
NN = (((1,), (0,)), ((), ()))
TN = (((0,), (0,)), ((), ()))


def dot(a, b, dims):
    return lax.dot_general(a, b, dims, preferred_element_type=F32)


def blk(k, n):
    return pl.ds(k * n if isinstance(k, int) else pl.multiple_of(k * n, n), n)


def lane_mean(vals):
    return jnp.mean(vals, axis=1, keepdims=True)


def row_sum(vals):
    return jnp.sum(vals, axis=0, keepdims=True)


def zero(ref):
    ref[...] = jnp.zeros_like(ref)


def remote(src, dst, send, recv, where):
    return pltpu.make_async_remote_copy(src_ref=src, dst_ref=dst, send_sem=send, recv_sem=recv, device_id=where, device_id_type=MESH)


def meet(peers):
    barrier = pltpu.get_barrier_semaphore()
    for where in peers:
        pl.semaphore_signal(barrier, inc=1, device_id=where, device_id_type=MESH)
    pl.semaphore_wait(barrier, len(peers))


def fsdp_peers(f):
    core = lax.rem(f, 2)
    other = f + 1 - 2 * core
    far = lax.rem(f + 2, 4)
    return other, far, lax.rem(other + 2, 4)


def others(axis, index, count):
    return [{axis: lax.rem(index + k, count)} for k in range(1, count)]


def rope(vals, cos, sin, half_dim):
    return vals * cos + pltpu.roll(vals, half_dim, 1) * sin


def causal(scores, tq):
    key_idx = lax.broadcasted_iota(jnp.int32, scores.shape, 0)
    q_idx = lax.rem(lax.broadcasted_iota(jnp.int32, scores.shape, 1), tq)
    return jnp.where(key_idx <= q_idx, scores, NEG_BIG)


def params(cid):
    return pltpu.CompilerParams(collective_id=cid, has_side_effects=True, vmem_limit_bytes=VMEM_BYTES)


def rope_tables(positions, head_dim):
    inv_freq = ROPE_BASE ** (-jnp.arange(0, head_dim, 2).astype(F32) / head_dim)
    angles = positions.astype(F32)[:, None] * inv_freq[None, :]
    cosines, sines = jnp.cos(angles), jnp.sin(angles)
    return jnp.concatenate([cosines, cosines], axis=1), jnp.concatenate([-sines, sines], axis=1)


def front_kernel(group, n_line, hid_ref, gain_ref, w_ref, wo_ref, cos_ref, sin_ref, o_ref, qr_ref, lse_ref, kl_ref, vl_ref, kp_ref, vp_ref, gfull_ref, n_out, w_out, wo_all, wbuf, nbuf, acc, hbuf, gbuf, qs, vt, m_all, l_all, acc_all, h_sem, g_send, g_recv, own_send, own_recv, x_send, x_recv, y_send, y_recv, d_send, d_recv, kv_send, kv_recv, ox_send, ox_recv, oy_send, oy_recv, od_send, od_recv, zw_send, zw_recv, out_sem):
    q_len, feat = hid_ref.shape[0], w_ref.shape[0]
    head_dim = cos_ref.shape[1]
    half_dim = head_dim // 2
    kv_width = kl_ref.shape[1]
    kv_heads = kv_width // head_dim
    q_width = qr_ref.shape[1]
    tq = q_len // TILES
    wide = group * tq
    scale = head_dim ** -0.5 * LOG2E
    half = feat // 2
    piece = half // PIECES
    o_rows = wo_ref.shape[0]
    o_half = o_rows // 2
    o_piece = o_half // O_PIECES
    flag, f, z = lax.axis_index("cp"), lax.axis_index("fsdp"), lax.axis_index("tp")
    wo_out = wo_all.at[z]
    far = 1 - flag
    f_core, f_x, f_diag = fsdp_peers(f)
    to_core, to_x, to_diag, to_y = {"fsdp": f_core}, {"fsdp": f_x}, {"fsdp": f_diag}, {"cp": far}

    def h_load(tile):
        slot = lax.rem(tile, 2)
        return pltpu.make_async_copy(hid_ref.at[blk(tile, tq)], hbuf.at[slot], h_sem.at[slot])

    h_load(0).start()
    h_load(1).start()
    meet([to_core, to_x, to_diag, to_y] + others("tp", z, n_line))

    def span(side, j):
        return blk(side * PIECES + j, piece)

    def x_copy(j):
        return remote(w_ref.at[span(flag, j)], wbuf.at[f, span(flag, j)], x_send.at[j], x_recv.at[j], to_x)

    def x_in(j):
        return remote(w_ref.at[span(flag, j)], wbuf.at[f_x, span(flag, j)], x_send.at[j], x_recv.at[j], to_x)

    def y_copy(j, side):
        return remote(wbuf.at[f_x, span(side, j)], wbuf.at[f_x, span(side, j)], y_send.at[j], y_recv.at[j], to_y)

    def d_copy(j, side, slot):
        return remote(wbuf.at[slot, span(side, j)], wbuf.at[slot, span(side, j)], d_send.at[side, j], d_recv.at[side, j], to_core)

    def g_copy(k, where, slot):
        return remote(gain_ref, gbuf.at[slot], g_send.at[k], g_recv.at[k], where)

    def own_copy(slot):
        return remote(w_ref, wbuf.at[slot], own_send, own_recv, to_core)

    def o_span(side, j):
        return blk(side * O_PIECES + j, o_piece)

    def ox_copy(j, slot):
        return remote(wo_ref.at[o_span(flag, j)], wo_out.at[slot, o_span(flag, j)], ox_send.at[j], ox_recv.at[j], to_x)

    def oy_copy(j, side):
        return remote(wo_out.at[f_x, o_span(side, j)], wo_out.at[f_x, o_span(side, j)], oy_send.at[j], oy_recv.at[j], to_y)

    def od_copy(k, src, slot, where):
        return remote(src, wo_out.at[slot, where], od_send.at[k], od_recv.at[k], to_core)

    def zw_copy(k, owner):
        mine = blk(flag, o_half)
        return remote(wo_ref.at[mine], wo_all.at[owner, f, mine], zw_send.at[k - 1], zw_recv.at[k - 1], {"tp": lax.rem(z + k, n_line)})

    for k in range(1, n_line):
        zw_copy(k, z).start()
    gains = [(k, where, where["fsdp"]) for k, where in enumerate((to_core, to_x, to_diag))]
    for k, where, _ in gains:
        g_copy(k, where, f).start()
    for j in range(PIECES):
        x_copy(j).start()
    own_copy(f).start()
    for j in range(O_PIECES):
        ox_copy(j, f).start()
    all_rows = pl.ds(0, o_rows)
    od_copy(0, wo_ref, f, all_rows).start()
    local_w = pltpu.make_async_copy(w_ref, wbuf.at[f], out_sem.at[0])
    local_w.start()
    local_o = pltpu.make_async_copy(wo_ref, wo_out.at[f], out_sem.at[1])
    local_o.start()
    gbuf[f] = gain_ref[...]
    for k, where, slot in gains:
        g_copy(k, where, slot).wait_recv()
    for k in range(gbuf.shape[0]):
        gfull_ref[:, blk(k, feat)] = gbuf[k]

    for tile in range(TILES):
        h_load(tile).wait()
        strip = min(32, tq)

        @pl.loop(0, tq // strip)
        def _(i):
            vals = hbuf[tile % 2, blk(i, strip), :].astype(F32)
            inv = lax.rsqrt(lane_mean(vals * vals) + NORM_EPS)
            nbuf[pl.ds(pl.multiple_of(tile * tq + i * strip, strip), strip), :] = (vals * inv * gfull_ref[...]).astype(BF)

        if tile + 2 < TILES:
            h_load(tile + 2).start()
    put_n = pltpu.make_async_copy(nbuf, n_out, out_sem.at[2])
    put_n.start()

    def project(slot, start, rows, first=False):
        cols = pl.ds(pl.multiple_of(slot * feat + start, 128), rows)

        @pl.loop(0, TILES)
        def _(tile):
            here = blk(tile, tq)
            part = dot(nbuf[here, cols], wbuf[slot, pl.ds(start, rows), :], NN)
            acc[here, :] = part if first else acc[here, :] + part

    def x_tick(j):
        x_in(j).wait_recv()
        y_copy(j, flag).start()
        d_copy(j, flag, f_x).start()

    def y_tick(j):
        y_copy(j, far).wait_recv()
        d_copy(j, 1 - flag, f_x).start()

    local_w.wait()
    project(f, 0, feat, first=True)
    x_tick(0)
    own_copy(f_core).wait_recv()
    project(f_core, 0, feat)
    x_tick(1)
    y_tick(0)
    x_tick(2)
    y_tick(1)
    x_tick(3)
    for j in range(PIECES):
        d_copy(j, flag, f_diag).wait_recv()
    first_half = pl.multiple_of(flag * half, half)
    project(f_x, first_half, half)
    y_tick(2)
    project(f_diag, first_half, half)
    y_tick(3)
    for j in range(PIECES):
        d_copy(j, 1 - flag, f_diag).wait_recv()
    second_half = pl.multiple_of((far) * half, half)
    project(f_x, second_half, half)
    project(f_diag, second_half, half)
    put_w = pltpu.make_async_copy(wbuf, w_out, out_sem.at[3])
    put_w.start()

    @pl.loop(0, TILES)
    def _(tile):
        here = blk(tile, tq)
        cos, sin = cos_ref[here, :], sin_ref[here, :]
        for h in range(kv_heads):
            k_at = q_width // head_dim + h
            kl_ref[here, blk(h, head_dim)] = rope(acc[here, blk(k_at, head_dim)], cos, sin, half_dim).astype(BF)
            vl_ref[here, blk(h, head_dim)] = acc[here, blk(k_at + kv_heads, head_dim)].astype(BF)

    kv_pairs = ((kl_ref, kp_ref), (vl_ref, vp_ref))

    def kv_copy(k):
        return remote(kv_pairs[k][0], kv_pairs[k][1], kv_send.at[k], kv_recv.at[k], {"cp": 1})

    @pl.loop(0, TILES)
    def _(tile):
        here = blk(tile, tq)
        cos, sin = cos_ref[here, :], sin_ref[here, :]
        for h in range(group * kv_heads):
            cols = blk(h, head_dim)
            qr_ref[here, cols] = rope(acc[here, cols], cos, sin, half_dim).astype(BF)

    @pl.when(flag == 0)
    def _():
        zero(kp_ref)
        zero(vp_ref)
        for k in range(len(kv_pairs)):
            kv_copy(k).start()

    def load_q(item):
        g, tile = item // TILES, lax.rem(item, TILES)
        rows = blk(tile, tq)
        for h in range(group):
            qs[blk(h, tq), :] = qr_ref[rows, blk(g * group + h, head_dim)]

    def key_piece(item, k_ref, side, start, masked):
        g = item // TILES
        scores = dot(k_ref[start, blk(g, head_dim)], qs[...], NT)
        if masked:
            scores = causal(scores, tq)
        m_old = m_all[item]
        m_new = jnp.maximum(m_old, jnp.max(scores, axis=0, keepdims=True))
        probs = jnp.exp2((scores - m_new) * scale)
        fade = jnp.exp2((m_old - m_new) * scale)
        m_all[item] = m_new
        l_all[item] = l_all[item] * fade + row_sum(probs)
        acc_all[item] = acc_all[item] * fade + dot(vt[g, side, :, start], probs.astype(BF), NN)

    for g in range(kv_heads):
        vt[g, 0] = vl_ref[:, blk(g, head_dim)].T

    @pl.loop(0, kv_heads * TILES)
    def _(item):
        tile = lax.rem(item, TILES)
        load_q(item)
        m_all[item] = jnp.full_like(m_all[item], NEG_BIG)
        l_all[item] = jnp.zeros_like(l_all[item])
        acc_all[item] = jnp.zeros_like(acc_all[item])
        key_piece(item, kl_ref, 0, blk(tile, tq), True)

        @pl.loop(0, tile)
        def _(i):
            key_piece(item, kl_ref, 0, blk(i, tq), False)

    for j in range(O_PIECES):
        ox_copy(j, f_x).wait_recv()
        oy_copy(j, flag).start()
        od_copy(1 + j, wo_out.at[f_x, o_span(flag, j)], f_x, o_span(flag, j)).start()

    @pl.when(flag == 1)
    def _():
        for k in range(len(kv_pairs)):
            kv_copy(k).wait_recv()
        for g in range(kv_heads):
            vt[g, 1] = vp_ref[:, blk(g, head_dim)].T

    @pl.loop(0, kv_heads * TILES)
    def _(item):
        g, tile = item // TILES, lax.rem(item, TILES)
        rows = blk(tile, tq)

        @pl.when(flag == 1)
        def _():
            load_q(item)

        @pl.loop(0, flag * TILES)
        def _(i):
            key_piece(item, kp_ref, 1, blk(i, tq), False)

        total = l_all[item]
        lse_ref[item] = m_all[item] * scale + jnp.log2(total)
        out_t = acc_all[item] / total
        for h in range(group):
            o_ref[rows, blk(g * group + h, head_dim)] = out_t[:, h * tq:h * tq + tq].T.astype(BF)

        for j in range(O_PIECES):
            @pl.when(item == (j + 1) * kv_heads * TILES // O_PIECES - 1)
            def _():
                oy_copy(j, far).wait_recv()
                od_copy(1 + O_PIECES + j, wo_out.at[f_x, o_span(1 - flag, j)], f_x, o_span(1 - flag, j)).start()

    od_copy(0, wo_ref, f_core, all_rows).wait_recv()
    for j in range(O_PIECES):
        od_copy(1 + j, wo_out.at[f_x, o_span(flag, j)], f_diag, o_span(flag, j)).wait_recv()
        od_copy(1 + O_PIECES + j, wo_out.at[f_x, o_span(1 - flag, j)], f_diag, o_span(1 - flag, j)).wait_recv()

    for k in range(1, n_line):
        zw_copy(k, lax.rem(z + n_line - k, n_line)).wait_recv()
        zw_copy(k, z).wait_send()
    for k, where, _ in gains:
        g_copy(k, where, f).wait_send()
    own_copy(f).wait_send()
    od_copy(0, wo_ref, f, all_rows).wait_send()
    for j in range(PIECES):
        x_copy(j).wait_send()
        y_copy(j, flag).wait_send()
        d_copy(j, flag, f_x).wait_send()
        d_copy(j, 1 - flag, f_x).wait_send()
    for j in range(O_PIECES):
        ox_copy(j, f).wait_send()
        oy_copy(j, flag).wait_send()
        od_copy(1 + j, wo_out.at[f_x, o_span(flag, j)], f_x, o_span(flag, j)).wait_send()
        od_copy(1 + O_PIECES + j, wo_out.at[f_x, o_span(1 - flag, j)], f_x, o_span(1 - flag, j)).wait_send()

    @pl.when(flag == 0)
    def _():
        for k in range(len(kv_pairs)):
            kv_copy(k).wait_send()

    for local in (local_o, put_n, put_w):
        local.wait()


def front(hidden, gain, w_qkv, w_out, cosines, sines, group, kv_width, n_line, cid):
    q_len, model_dim = hidden.shape
    feat, width = w_qkv.shape
    head_dim = cosines.shape[1]
    q_width = width - 2 * kv_width
    kv_heads = kv_width // head_dim
    o_rows, o_cols = w_out.shape
    n_fsdp = model_dim // feat
    tq = q_len // TILES
    wide = group * tq
    items = kv_heads * TILES
    sds = jax.ShapeDtypeStruct
    kv = sds((q_len, kv_width), BF)
    q_like = sds((q_len, q_width), BF)
    line = pltpu.VMEM((items, 1, wide), F32)
    own, pair, trio = DMA(()), DMA((2,)), DMA((n_fsdp - 1,))
    w_link, w_side, o_link, o_core, z_link = DMA((PIECES,)), DMA((2, PIECES)), DMA((O_PIECES,)), DMA((1 + 2 * O_PIECES,)), DMA((n_line - 1,))
    return pl.pallas_call(
        functools.partial(front_kernel, group, n_line),
        in_specs=[ANY] + [VMEM] * 5,
        out_specs=[VMEM] * 8 + [ANY] * 3,
        out_shape=[q_like, q_like, sds((items, 1, wide), F32), kv, kv, kv, kv, sds((1, model_dim), F32), sds((q_len, model_dim), BF), sds((n_fsdp, feat, width), BF), sds((n_line, n_fsdp, o_rows, o_cols), BF)],
        scratch_shapes=[
            pltpu.VMEM((n_fsdp, feat, width), BF),
            pltpu.VMEM((q_len, model_dim), BF),
            pltpu.VMEM((q_len, width), F32),
            pltpu.VMEM((2, tq, model_dim), BF),
            pltpu.VMEM((n_fsdp, 1, feat), F32),
            pltpu.VMEM((wide, head_dim), BF),
            pltpu.VMEM((kv_heads, 2, head_dim, q_len), BF),
            line,
            line,
            pltpu.VMEM((items, head_dim, wide), F32),
        ] + [pair, trio, trio, own, own, w_link, w_link, w_link, w_link, w_side, w_side, pair, pair, o_link, o_link, o_link, o_link, o_core, o_core, z_link, z_link, DMA((4,))],
        compiler_params=params(cid),
        name="front",
    )(hidden, gain, w_qkv, w_out, cosines, sines)


def back_kernel(n_line, group, o_ref, q_ref, lse_ref, cos_ref, sin_ref, kl_ref, vl_ref, kp_ref, vp_ref, _wo_in, ct_ref, d_ref, o_all, wo_all, w_ref, ctb_ref, do_ref, dkl_ref, dvl_ref, dkp_ref, dvp_ref, qs_ref, dos_ref, delta_ref, kt_ref, dqt_ref, load_sem, keep_sem, ct_sem, od_send, ou_send, o_recv, y_send, y_recv, x_send, x_recv, c_send, c_recv, cx_send, cx_recv, kv_send, kv_recv):
    last = n_line - 1
    z, flag, f = lax.axis_index("tp"), lax.axis_index("cp"), lax.axis_index("fsdp")
    far = 1 - flag
    f_core, f_x, f_diag = fsdp_peers(f)
    q_len, width = o_ref.shape
    head_dim = cos_ref.shape[1]
    half_dim = head_dim // 2
    kv_width = kl_ref.shape[1]
    kv_heads = kv_width // head_dim
    tq = q_len // TILES
    wide = group * tq
    score_scale = head_dim ** -0.5
    n_parts, o_rows, part = w_ref.shape
    o_half = o_rows // 2
    load = pltpu.make_async_copy(wo_all.at[z], w_ref, load_sem)
    load.start()
    keep = pltpu.make_async_copy(o_ref, o_all.at[z], keep_sem)
    keep.start()

    def ct_load(tile):
        slot = lax.rem(tile, 2)
        return pltpu.make_async_copy(ct_ref.at[blk(tile, tq)], ctb_ref.at[slot], ct_sem.at[slot])

    ct_load(0).start()
    ct_load(1).start()

    to_core, to_x, to_y = {"fsdp": f_core}, {"fsdp": f_x}, {"cp": far}
    meet([to_core, to_x, to_y] + others("tp", z, n_line))

    def tile_rows(j):
        return blk(j, tq)

    def o_down(t, j, src):
        return remote(src, o_all.at[t, tile_rows(j)], od_send.at[t, j], o_recv.at[t, j], {"tp": jnp.maximum(z - 1, 0)})

    def o_up(t, j, src):
        return remote(src, o_all.at[t, tile_rows(j)], ou_send.at[t, j], o_recv.at[t, j], {"tp": jnp.minimum(z + 1, last)})

    def wo_half(r, slot, side):
        return wo_all.at[lax.rem(z + r, n_line), slot, blk(side, o_half)]

    def y_copy(r, side):
        return remote(wo_half(r, f, side), wo_half(r, f, side), y_send.at[r - 1], y_recv.at[r - 1], to_y)

    def x_copy(r, side, slot):
        return remote(wo_half(r, slot, side), wo_half(r, slot, side), x_send.at[side, r - 1], x_recv.at[side, r - 1], to_x)

    def c_copy(r, side, slot):
        return remote(wo_half(r, slot, side), wo_half(r, slot, side), c_send.at[side, r - 1], c_recv.at[side, r - 1], to_core)

    def cx_copy(r, side, slot):
        return remote(wo_half(r, slot, side), wo_half(r, slot, side), cx_send.at[side, r - 1], cx_recv.at[side, r - 1], to_core)

    for j in range(TILES):
        @pl.when(z > 0)
        def _():
            o_down(z, j, o_ref.at[tile_rows(j)]).start()

        @pl.when(z < last)
        def _():
            o_up(z, j, o_ref.at[tile_rows(j)]).start()

    for r in range(1, n_line):
        y_copy(r, flag).start()
        x_copy(r, flag, f).start()
        c_copy(r, flag, f).start()

    def o_tick(k):
        r, j = k // TILES + 1, lax.rem(k, TILES)

        @pl.when(z + r <= last)
        def _():
            t = jnp.minimum(z + r, last)
            o_down(t, j, o_all.at[t, tile_rows(j)]).wait_recv()

            @pl.when(z > 0)
            def _():
                o_down(t, j, o_all.at[t, tile_rows(j)]).start()

        @pl.when(z - r >= 0)
        def _():
            t = jnp.maximum(z - r, 0)
            o_up(t, j, o_all.at[t, tile_rows(j)]).wait_recv()

            @pl.when(z < last)
            def _():
                o_up(t, j, o_all.at[t, tile_rows(j)]).start()

    def y_tick(r):
        y_copy(r, far).wait_recv()
        x_copy(r, far, f).start()
        c_copy(r, far, f).start()

    def x_tick(q):
        r, side = q % (n_line - 1) + 1, flag if q < n_line - 1 else far
        x_copy(r, side, f_x).wait_recv()
        cx_copy(r, side, f_x).start()

    zero(dkl_ref)
    zero(dvl_ref)

    @pl.when(flag == 1)
    def _():
        zero(dkp_ref)
        zero(dvp_ref)

    load.wait()

    def do_tile(tile):
        ct_load(tile).wait()
        slot = lax.rem(tile, 2)
        total = sum(dot(ctb_ref[slot, :, blk(k, part)], w_ref[k], NT) for k in range(n_parts))
        do_ref[tile_rows(tile), :] = total.astype(BF)

        @pl.when(tile + 2 < TILES)
        def _():
            ct_load(tile + 2).start()

    def bwd_item(item):
        g, tile = item // TILES, lax.rem(item, TILES)
        kv_cols = blk(g, head_dim)
        rows = blk(tile, tq)

        @pl.when(tile == 0)
        def _():
            kt_ref[0] = kl_ref[:, kv_cols].T
            kt_ref[1] = kp_ref[:, kv_cols].T

        for h in range(group):
            cols = blk(g * group + h, head_dim)
            stack = blk(h, tq)
            qs_ref[stack, :] = q_ref[rows, cols]
            d_h = do_ref[rows, cols]
            dos_ref[stack, :] = d_h
            prod = d_h.astype(F32) * o_ref[rows, cols].astype(F32)
            delta_ref[:, stack] = row_sum(prod.T)
        zero(dqt_ref)

        def piece(k_ref, v_ref, dk_ref, dv_ref, side, span, masked):
            scores = dot(k_ref[span, kv_cols], qs_ref[...], NT)
            if masked:
                scores = causal(scores, tq)
            probs = jnp.exp2(scores * (score_scale * LOG2E) - lse_ref[item])
            d_probs = dot(v_ref[span, kv_cols], dos_ref[...], NT)
            d_scores = (probs * (d_probs - delta_ref[...]) * score_scale).astype(BF)
            dv_ref[g, span, :] += dot(probs.astype(BF), dos_ref[...], NN)
            dk_ref[g, span, :] += dot(d_scores, qs_ref[...], NN)
            dqt_ref[...] += dot(kt_ref[side, :, span], d_scores, NN)

        piece(kl_ref, vl_ref, dkl_ref, dvl_ref, 0, blk(tile, tq), True)

        @pl.loop(0, tile)
        def _(i):
            piece(kl_ref, vl_ref, dkl_ref, dvl_ref, 0, blk(i, tq), False)

        @pl.loop(0, flag * (q_len // tq))
        def _(i):
            piece(kp_ref, vp_ref, dkp_ref, dvp_ref, 1, blk(i, tq), False)

        for h in range(group):
            dq_h = dqt_ref[:, h * tq:h * tq + tq].T
            d_ref[rows, blk(g * group + h, head_dim)] = rope(dq_h, cos_ref[rows, :], -sin_ref[rows, :], half_dim).astype(BF)

        @pl.when((tile == TILES - 1) & (flag == 1))
        def _():
            for copy in back(g):
                copy.start()

    def back(g):
        return [remote(ref.at[g], ref.at[g], kv_send.at[k, g], kv_recv.at[k, g], {"cp": 0}) for k, ref in enumerate((dkp_ref, dvp_ref))]

    def kv_done(g):
        @pl.when(flag == 0)
        def _():
            for copy in back(g):
                copy.wait_recv()
            dkl_ref[g] += dkp_ref[g]
            dvl_ref[g] += dvp_ref[g]

        dk = rope(dkl_ref[g], cos_ref[...], -sin_ref[...], half_dim)
        k_at = width // head_dim + g
        d_ref[:, blk(k_at, head_dim)] = dk.astype(BF)
        d_ref[:, blk(k_at + kv_heads, head_dim)] = dvl_ref[g].astype(BF)

        @pl.when(flag == 1)
        def _():
            for copy in back(g):
                copy.wait_send()

    items = TILES * (kv_heads + 1)
    o_ticks, x_ticks = TILES * last, 2 * last
    y_at = {4 + 3 * (r - 1): r for r in range(1, n_line)}
    x_at = {5: 0, 9: 1, 11: 2}

    @pl.loop(0, items)
    def _(item):
        @pl.when(item < TILES)
        def _():
            do_tile(item)

        @pl.when(item >= TILES)
        def _():
            bwd_item(item - TILES)

        @pl.when(lax.rem(item, 2) == 1)
        def _():
            o_tick(item // 2)

        for at, r in y_at.items():
            @pl.when(item == at)
            def _():
                y_tick(r)

        for at, q in x_at.items():
            @pl.when(item == at)
            def _():
                x_tick(q)

    done = items // 2
    tail = [("x", q) for q in range(len(x_at), x_ticks)] + [("kv", g) for g in range(kv_heads)]
    for k in range(done, o_ticks):
        o_tick(jnp.int32(k))
        if (k - done) % 2 == 1 and tail:
            kind, arg = tail.pop(0)
            x_tick(arg) if kind == "x" else kv_done(arg)
            later = [t for t in tail if t[0] == "kv"]
            if later:
                tail.remove(later[0])
                kv_done(later[0][1])
    for kind, arg in tail:
        x_tick(arg) if kind == "x" else kv_done(arg)

    for r in range(1, n_line):
        for side in (flag, far):
            c_copy(r, side, f_core).wait_recv()
            cx_copy(r, side, f_diag).wait_recv()
            x_copy(r, side, f).wait_send()
            c_copy(r, side, f).wait_send()
            cx_copy(r, side, f_x).wait_send()
        y_copy(r, flag).wait_send()

    @pl.loop(0, n_line)
    def _(t):
        @pl.when((t >= z) & (z > 0))
        def _():
            for j in range(TILES):
                o_down(t, j, o_all.at[t, tile_rows(j)]).wait_send()

        @pl.when((t <= z) & (z < last))
        def _():
            for j in range(TILES):
                o_up(t, j, o_all.at[t, tile_rows(j)]).wait_send()

    keep.wait()


def attn_back(attn_out, q_rot, lse, cosines, sines, k_loc, v_loc, k_prev, v_prev, wo_all, cotangent, n_line, group, cid):
    q_len, width = attn_out.shape
    head_dim = cosines.shape[1]
    kv_width = k_loc.shape[1]
    kv_heads = kv_width // head_dim
    _, n_fsdp, o_rows, o_cols = wo_all.shape
    tq = q_len // TILES
    wide = group * tq
    acc = pltpu.VMEM((kv_heads, q_len, head_dim), F32)
    stack = pltpu.VMEM((wide, head_dim), BF)
    own, pair, tiles, hop, side, kv = DMA(()), DMA((2,)), DMA((n_line, TILES)), DMA((n_line - 1,)), DMA((2, n_line - 1)), DMA((2, kv_heads))
    return pl.pallas_call(
        functools.partial(back_kernel, n_line, group),
        in_specs=[VMEM] * 9 + [ANY] * 2,
        out_specs=[VMEM, ANY, ANY],
        out_shape=[jax.ShapeDtypeStruct((q_len, width + 2 * kv_width), BF), jax.ShapeDtypeStruct((n_line, q_len, width), BF), jax.ShapeDtypeStruct(wo_all.shape, BF)],
        input_output_aliases={9: 2},
        scratch_shapes=[
            pltpu.VMEM((n_fsdp, o_rows, o_cols), BF),
            pltpu.VMEM((2, tq, cotangent.shape[1]), BF),
            pltpu.VMEM((q_len, width), BF),
            acc, acc, acc, acc,
            stack,
            stack,
            pltpu.VMEM((1, wide), F32),
            pltpu.VMEM((2, head_dim, q_len), BF),
            pltpu.VMEM((head_dim, wide), F32),
        ] + [own, own, pair, tiles, tiles, tiles, hop, hop, side, side, side, side, side, side, kv, kv],
        compiler_params=params(cid),
        name="attn_back",
    )(attn_out, q_rot, lse, cosines, sines, k_loc, v_loc, k_prev, v_prev, wo_all, cotangent)


class Line:
    def __init__(self, n_line, buf_ref, pbuf_ref, send_sem, recv_sem, fill, finish):
        self.last = n_line - 1
        self.z = lax.axis_index("tp")
        self.buf, self.pbuf, self.send_sem, self.recv_sem = buf_ref, pbuf_ref, send_sem, recv_sem
        self.chunks, self.rows = buf_ref.shape[1], buf_ref.shape[2]
        self.block = pbuf_ref.shape[1]
        self.per_block = self.block // self.rows
        self.fill, self.finish = fill, finish
        self.steps = self.chunks + self.last

    def dist(self, side):
        return self.z if side else self.last - self.z

    def toward(self, side, back=False):
        up = bool(side) != back
        return {"tp": jnp.clip(self.z + 1 if up else self.z - 1, 0, self.last)}

    def copy(self, side, chunk):
        spot = self.buf.at[side, chunk]
        return remote(spot, spot, self.send_sem.at[side, chunk], self.recv_sem.at[side, chunk], self.toward(side))

    def live(self, side, step):
        chunk = step - self.dist(side)
        return chunk, (chunk >= 0) & (chunk < self.chunks)

    def tick(self, step):
        for side in range(2):
            chunk, ok = self.live(side, step)

            @pl.when(ok & (lax.rem(chunk, self.per_block) == 0))
            def _():
                self.fill(self.pbuf.at[side], blk((side * self.chunks + chunk) // self.per_block, self.block))

        for side in range(2):
            chunk, ok = self.live(side, step)
            dist = self.dist(side)
            part = blk(lax.rem(jnp.maximum(chunk, 0), self.per_block), self.rows)

            @pl.when(ok & (dist == 0))
            def _():
                self.buf[side, chunk] = self.pbuf[side, part, :]

            @pl.when(ok & (dist > 0))
            def _():
                self.copy(side, chunk).wait_recv()
                self.buf[side, chunk] += self.pbuf[side, part, :]

            @pl.when(ok & (dist < self.last))
            def _():
                self.copy(side, chunk).start()

            @pl.when(ok & (dist == self.last))
            def _():
                self.finish(chunk, self.buf[side, chunk])

    def drain(self):
        for side in range(2):
            @pl.when(self.dist(side) < self.last)
            def _():
                @pl.loop(0, self.chunks)
                def _(chunk):
                    self.copy(side, chunk).wait_send()


def close_kernel(n_line, n_fsdp, d_ref, o_ref, gain_ref, hid_ref, ct_ref, n_ref, w_all, o_all, wo_all, out_ref, blk_ref, gg_ref, ts, yr, dl, xs, ks, xr, buf, gp, ga, gs, gb, gt, gc, ebuf, fb_in, fb_ct, fb_out, send_sem, recv_sem, w_sem, f_sem, ct_sem, fo_sem, lhs_sem, a_send, a_recv, ld_sem, st_sem, x_send, x_recv, e_sem, es_sem, y_send, y_recv, out_send, out_recv, o_sem, wl_sem, h_sem, r_sem, ga_send, ga_recv, gb_send, gb_recv, gc_send, gc_recv):
    last = n_line - 1
    z, flag, f = lax.axis_index("tp"), lax.axis_index("cp"), lax.axis_index("fsdp")
    far = 1 - flag
    f_core, f_x, f_diag = fsdp_peers(f)
    to_core, to_x, to_y = {"fsdp": f_core}, {"fsdp": f_x}, {"cp": far}
    _, feat, width = w_all.shape
    chunks, rows = buf.shape[1], buf.shape[2]
    half = chunks * rows
    g_rows = feat // GRAD_CHUNKS
    owner = (z == 0) | (z == last)
    own_base = jnp.where(z == last, chunks, 0)
    copy = pltpu.make_async_copy

    def own_span(chunk):
        return blk(own_base + chunk, rows)

    def f_loads(chunk):
        slot = lax.rem(chunk, 2)
        return copy(hid_ref.at[own_span(chunk)], fb_in.at[slot], f_sem.at[slot]), copy(ct_ref.at[own_span(chunk)], fb_ct.at[slot], ct_sem.at[slot])

    def f_store(chunk):
        slot = lax.rem(chunk, 2)
        return copy(fb_out.at[slot], out_ref.at[own_span(chunk)], fo_sem.at[slot])

    @pl.when(owner)
    def _():
        for chunk in range(2):
            for load in f_loads(chunk):
                load.start()

    zero(gp)
    meet([to_core, to_x, to_y] + others("tp", z, n_line) + [{"fsdp": f_diag}])

    def finish(chunk, total):
        slot = lax.rem(chunk, 2)
        for load in f_loads(chunk):
            load.wait()

        @pl.when(chunk > 1)
        def _():
            f_store(chunk - 2).wait()

        x_in = fb_in[slot].astype(F32)
        inv = lax.rsqrt(lane_mean(x_in * x_in) + NORM_EPS)
        x_hat = x_in * inv
        gp[...] += row_sum(total * x_hat)
        scaled = total * gain_ref[...]
        fb_out[slot] = (fb_ct[slot].astype(F32) + inv * (scaled - x_hat * lane_mean(scaled * x_hat))).astype(BF)
        f_store(chunk).start()

        @pl.when(chunk + 2 < chunks)
        def _():
            for load in f_loads(chunk + 2):
                load.start()

    kinds = range(2)

    def g_at(ref, j):
        return ref.at[blk(j, g_rows)]

    def x_copy(j):
        return remote(g_at(xs, j), g_at(xr, j), x_send.at[j], x_recv.at[j], to_x)

    def y_copy(j):
        return remote(g_at(ts, j), g_at(yr, j), y_send.at[j], y_recv.at[j], to_y)

    def e_store(j):
        return copy(ebuf.at[0], g_at(ts, j), es_sem)

    def meet_x(j):
        x_copy(j).wait_recv()
        loads = [copy(g_at(src, j), ebuf.at[k], e_sem.at[k]) for k, src in enumerate((ks, xr))]
        for load in loads:
            load.start()
        for load in loads:
            load.wait()
        ebuf[0] += ebuf[1]
        e_store(j).start()

    def send_y(j):
        e_store(j).wait()
        y_copy(j).start()

    def sum_phase(wbuf, pbuf, abuf, bbuf, lbuf, lhs):
        w_load = copy(w_all, wbuf, w_sem)
        w_load.start()

        def fill(dst, span):
            for k in range(n_fsdp):
                dst[:, blk(k, feat)] = dot(d_ref[span, :], wbuf[k], NT)

        line = Line(n_line, buf, pbuf, send_sem, recv_sem, fill, finish)
        slots = (f_diag, f_core, f_x, f)

        def lhs_loads(j):
            return [copy(src.at[:, blk(slot * GRAD_CHUNKS + j, g_rows)], lhs.at[m, k], lhs_sem.at[m, k]) for m, src in enumerate((n_ref, ct_ref)) for k, slot in enumerate(slots)]

        def a_copy(kind, j):
            return remote(abuf.at[kind], dl.at[kind, blk(j, g_rows)], a_send.at[kind], a_recv.at[kind, j], to_core)

        def b_stores(j):
            return [copy(bbuf.at[k], g_at(dst, j), st_sem.at[k]) for k, dst in enumerate((xs, ks))]

        def send_x(j):
            for kind in kinds:
                a_copy(kind, j).wait_send()
            for store in b_stores(j):
                store.wait()
            x_copy(j).start()

        def make(j):
            for load in lhs_loads(j):
                load.wait()
            for k in range(len(slots)):
                dst = (abuf, bbuf)[k // 2].at[k % 2]
                dst[:, :width] = dot(lhs[0, k], d_ref[...], TN)
                dst[:, width:] = dot(lhs[1, k], o_ref[...], TN)
            for kind in kinds:
                a_copy(kind, j).start()

            @pl.when(j + 1 < GRAD_CHUNKS)
            def _():
                for load in lhs_loads(j + 1):
                    load.start()

        def meet_core(j):
            loads = [copy(dl.at[kind, blk(j, g_rows)], lbuf.at[kind], ld_sem.at[kind]) for kind in kinds]
            for kind in kinds:
                a_copy(kind, j).wait_recv()
                loads[kind].start()
            for kind in kinds:
                loads[kind].wait()
                bbuf[kind] += lbuf[kind]
            for store in b_stores(j):
                store.start()

        for load in lhs_loads(0):
            load.start()
        w_load.wait()

        @pl.loop(0, line.steps)
        def _(step):
            line.tick(step)
            j, odd = step // 2, lax.rem(step, 2)

            @pl.when((odd == 0) & (j > 0) & (j <= GRAD_CHUNKS))
            def _():
                send_x(j - 1)

            @pl.when((odd == 0) & (j < GRAD_CHUNKS))
            def _():
                make(j)

            @pl.when((odd == 1) & (j < GRAD_CHUNKS))
            def _():
                meet_core(j)

            for late in range(2):
                k = (step - FIRST_X - late) * 2 // 5

                @pl.when((k >= 0) & (k < EARLY) & (step - late == FIRST_X + (5 * k + 1) // 2))
                def _():
                    send_y(k) if late else meet_x(k)

        line.drain()

    pl.run_scoped(
        sum_phase,
        pltpu.VMEM(w_all.shape, BF),
        pltpu.VMEM((2, min(128, half), buf.shape[3]), F32),
        pltpu.VMEM((2, g_rows, ts.shape[1]), F32),
        pltpu.VMEM((2, g_rows, ts.shape[1]), F32),
        pltpu.VMEM((2, g_rows, ts.shape[1]), F32),
        pltpu.VMEM((2, n_fsdp, d_ref.shape[0], g_rows), BF),
    )
    steps = chunks + last - 1

    def dist(side):
        return z if side else last - z

    def hop(side, chunk):
        span = blk(side * chunks + chunk, rows)
        up = z - 1 if side else z + 1
        return remote(out_ref.at[span], out_ref.at[span], out_send.at[side, chunk], out_recv.at[side, chunk], {"tp": jnp.clip(up, 0, last)})

    def ga_copy(end, k):
        return remote(gp, ga.at[end], ga_send.at[k], ga_recv.at[end], {"tp": k if end else 1 + k})

    def gb_copy():
        return remote(gs, gb, gb_send, gb_recv, to_y)

    def gc_copy(k, slot):
        to = lax.rem(f + k, n_fsdp)
        return remote(gt.at[to], gc.at[slot], gc_send.at[k - 1], gc_recv.at[k - 1], {"fsdp": to})

    ends = [(end, z == (last if end else 0)) for end in range(2)]

    def spread_phase(obuf, wbuf, hbuf, rbuf):
        o_load = copy(o_all, obuf, o_sem)
        o_load.start()
        q_len, n_cols = hbuf.shape[1], hbuf.shape[2]
        per_part = wo_all.shape[3] // n_cols
        items = per_part * n_fsdp

        def item_loads(item):
            slot = lax.rem(item, 2)
            return copy(wo_all.at[:, item // per_part, :, blk(lax.rem(item, per_part), n_cols)], wbuf.at[slot], wl_sem.at[slot]), copy(hid_ref.at[:, blk(item, n_cols)], hbuf.at[slot], h_sem.at[slot])

        def item_store(item):
            slot = lax.rem(item, 2)
            return copy(rbuf.at[slot], blk_ref.at[:, blk(item, n_cols)], r_sem.at[slot])

        for item in range(2):
            for load in item_loads(item):
                load.start()

        for end, here in ends:
            @pl.when(here)
            def _():
                ga[end] = gp[...]
                for k in range(last):
                    ga_copy(end, k).start()

                for chunk in range(chunks - 2, chunks):
                    f_store(chunk).wait()

                @pl.loop(0, chunks)
                def _(chunk):
                    hop(end, chunk).start()

        def project(item):
            slot = lax.rem(item, 2)
            for load in item_loads(item):
                load.wait()

            @pl.when(item > 1)
            def _():
                item_store(item - 2).wait()

            @pl.loop(0, TILES)
            def _(tile):
                span = blk(tile, q_len // TILES)
                total = sum(dot(obuf[t, span, :], wbuf[slot, t], NN) for t in range(n_line))
                rbuf[slot, span, :] = (hbuf[slot, span, :].astype(F32) + total).astype(BF)

            item_store(item).start()

            @pl.when(item + 2 < items)
            def _():
                for load in item_loads(item + 2):
                    load.start()

        for end, here in ends:
            @pl.when(jnp.logical_not(here))
            def _():
                ga_copy(end, 0).wait_recv()
        gs[...] = ga[0] + ga[1]
        o_load.wait()
        gb_copy().start()

        @pl.loop(0, steps)
        def _(step):
            for side in range(2):
                chunk = step - (last - 1 - dist(side))

                @pl.when((dist(side) < last) & (chunk >= 0) & (chunk < chunks))
                def _():
                    hop(side, chunk).wait_recv()

                    @pl.when(dist(side) > 0)
                    def _():
                        hop(side, chunk).start()

            @pl.when((lax.rem(step, 2) == 0) & (step // 2 < items))
            def _():
                project(step // 2)

            for k in range(EARLY, GRAD_CHUNKS):
                @pl.when(step == 1 + 5 * (k - EARLY))
                def _():
                    meet_x(k)

            for k in range(EARLY - 1, GRAD_CHUNKS):
                @pl.when(step == 2 + 5 * (k - EARLY) if k >= EARLY else step == 0)
                def _():
                    send_y(k)

        for item in range(items - 2, items):
            item_store(item).wait()

    pl.run_scoped(
        spread_phase,
        pltpu.VMEM(o_all.shape, BF),
        pltpu.VMEM((2, n_line, wo_all.shape[2], min(512, feat)), BF),
        pltpu.VMEM((2, d_ref.shape[0], min(512, feat)), BF),
        pltpu.VMEM((2, d_ref.shape[0], min(512, feat)), BF),
    )

    gb_copy().wait()
    for k in range(n_fsdp):
        gt[k] = gs[:, blk(k, feat)] + gb[:, blk(k, feat)]
    gc[f] = gt[f]
    for side in range(2):
        @pl.when(dist(side) > 0)
        def _():
            @pl.loop(0, chunks)
            def _(chunk):
                hop(side, chunk).wait_send()

    @pl.loop(0, GRAD_CHUNKS)
    def _(j):
        x_copy(j).wait_send()

    for k in range(1, n_fsdp):
        gc_copy(k, f).start()
    for k in range(1, n_fsdp):
        gc_copy(k, lax.rem(f + n_fsdp - k, n_fsdp)).wait_recv()
    gg_ref[...] = sum(gc[k] for k in range(n_fsdp))
    for k in range(1, n_fsdp):
        gc_copy(k, f).wait_send()
    for end, here in ends:
        @pl.when(here)
        def _():
            for k in range(last):
                ga_copy(end, k).wait_send()

    @pl.loop(0, GRAD_CHUNKS)
    def _(j):
        y_copy(j).wait()


def close(d_lin, attn_out, gain, hidden, cotangent, normed, w_full, o_all, wo_all, cid):
    q_len, model_dim = hidden.shape
    n_line, n_fsdp = wo_all.shape[:2]
    _, feat, width = w_full.shape
    g_width = width + attn_out.shape[1]
    half = q_len // 2
    rows = half // CHUNKS
    sds = jax.ShapeDtypeStruct
    row = pltpu.VMEM((1, model_dim), F32)
    slices = pltpu.VMEM((n_fsdp, 1, feat), F32)
    strip = pltpu.VMEM((2, rows, model_dim), BF)
    own, pair, line, grad, grads = DMA(()), DMA((2,)), DMA((2, CHUNKS)), DMA((GRAD_CHUNKS,)), DMA((2, GRAD_CHUNKS))
    z_trio, f_trio = DMA((n_line - 1,)), DMA((n_fsdp - 1,))
    act, g_part = sds((q_len, model_dim), BF), sds((feat, g_width), F32)
    return pl.pallas_call(
        functools.partial(close_kernel, n_line, n_fsdp),
        in_specs=[VMEM] * 3 + [ANY] * 6,
        out_specs=[ANY, ANY, VMEM] + [ANY] * 6,
        out_shape=[act, act, sds((1, feat), F32), g_part, g_part, sds((2, feat, g_width), F32), g_part, g_part, g_part],
        scratch_shapes=[
            pltpu.VMEM((2, CHUNKS, rows, model_dim), F32),
            row,
            pltpu.VMEM((2, 1, model_dim), F32),
            row,
            row,
            slices,
            slices,
            pltpu.VMEM((2, feat // GRAD_CHUNKS, g_width), F32),
            strip,
            strip,
            strip,
        ] + [line, line, own, pair, pair, pair, DMA((2, n_fsdp)), pair, grads, pair, pair, grad, grad, pair, own, grad, grad, line, line, own, pair, pair, pair, z_trio, pair, own, own, f_trio, f_trio],
        compiler_params=params(cid),
        name="close",
    )(d_lin, attn_out, gain, hidden, cotangent, normed, w_full, o_all, wo_all)


def solution(mesh):
    act_spec = P("fsdp", "cp", None)
    proj_spec = P("fsdp", "tp", None)
    wout_spec = P("tp", None, "fsdp")
    n_line = mesh.shape["tp"]

    def device_step(hidden, cotangent, positions, gain, w_query, w_key, w_value, w_out):
        hidden, cotangent = hidden[0], cotangent[0]
        assert hidden.shape[0] * mesh.shape["cp"] <= WINDOW_LEN
        feat, q_heads, head_dim = w_query.shape
        kv_heads = w_key.shape[1]
        group = q_heads // kv_heads
        q_width, kv_width = q_heads * head_dim, kv_heads * head_dim
        w_qkv = jnp.concatenate([w_query.reshape(feat, q_width), w_key.reshape(feat, kv_width), w_value.reshape(feat, kv_width)], axis=1)
        cosines, sines = rope_tables(positions, head_dim)
        attn_out, q_rot, lse, k_loc, v_loc, k_prev, v_prev, gain_full, normed, w_full, wo_all = front(hidden, gain.astype(F32)[None], w_qkv, w_out.reshape(q_width, feat), cosines, sines, group, kv_width, n_line, 0)
        d_lin, o_all, wo_all = attn_back(attn_out, q_rot, lse, cosines, sines, k_loc, v_loc, k_prev, v_prev, wo_all, cotangent, n_line, group, 1)
        grad_hidden, block_out, grad_gain, mine, theirs = close(d_lin, attn_out, gain_full, hidden, cotangent, normed, w_full, o_all, wo_all, 2)[:5]
        cuts = [q_width, q_width + kv_width, q_width + 2 * kv_width]
        g_query, g_key, g_value, g_out = [one + two for one, two in zip(jnp.split(mine, cuts, axis=1), jnp.split(theirs, cuts, axis=1))]
        return (
            block_out[None],
            grad_hidden[None],
            grad_gain[0],
            g_query.reshape(w_query.shape),
            g_key.reshape(w_key.shape),
            g_value.reshape(w_value.shape),
            g_out.T.reshape(w_out.shape),
        )

    specs = (act_spec, act_spec, P("fsdp"), proj_spec, proj_spec, proj_spec, wout_spec)
    return jax.shard_map(device_step, mesh=mesh, in_specs=specs[:2] + (P("cp"),) + specs[2:], out_specs=specs, check_vma=False)
```

time: 2380 us -> 664 us (0.28)
  waiting for transfers between devices: 1690 us -> 0 us
  Pallas kernels: 0 us -> 609 us
  matrix products: 423 us -> 0 us
  local copies, waits for them, and re-layouts: 122 us -> 31.9 us
  other arithmetic: 87.7 us -> 21.8 us
    psum x2 -> x0, waiting for transfers between devices: 1290 us -> none  [the longest x1 1100 us: device_step(): lax.psum(jnp.einsum('bshd,hdm->bsm', attn_out, wo_full, preferred_element...]
    pallas_call x0 -> x3, Pallas kernels: none -> 609 us  [the longest x1 344 us: close(): pl.pallas_call(functools.partial(close_kernel, n_line, n_fsdp), in_specs=...]
    dot_general x22 -> x0, matrix products: 404 us -> none  [the longest x2 77.6 us: one_tile(): jnp.einsum('kgqs,qkgd->skd', d_scores, q_blk, preferred_element_type=jnp....]
    reduce_scatter x6 -> x0, waiting for transfers between devices: 294 us -> none  [the longest x4 240 us: reduce_grad(): lax.psum_scatter(full_grad, 'fsdp', scatter_dimension=dim, tiled=True)]
    all_gather x6 -> x0, waiting for transfers between devices: 97.8 us -> none  [the longest x1 58.9 us: device_step(): wq_full = lax.all_gather(w_query, 'fsdp', axis=0, tiled=True)]
    dynamic_update_slice x4 -> x0, local copies, waits for them, and re-layouts: 85.4 us -> none  [attn_backward(): lax.scan(one_tile, (zero_acc, zero_acc), jnp.arange(num_rows * n_tiles))]
    reduce_sum x4 -> x0, other arithmetic: 45.5 us -> none  [the longest x2 30.2 us: one_tile(): row_total = jnp.sum(exp_scores, axis=-1, keepdims=True)]
    convert_element_type x3 -> x1, other arithmetic: 24.7 us -> 0.84 us  [rope_tables(): angles = positions.astype(F32)[:, None] * inv_freq[None, :]]
  transfers between devices with their start and end apart: 14 -> 0, of which waited for: 10 -> 0; matrix products, arithmetic and copies ran while one was open for 13% -> 0% of each run, Pallas kernels for 0% -> 0%
where the time goes in v1:
time: 664 us
  Pallas kernels  609 us (92%)
  local copies, waits for them, and re-layouts  31.9 us (5%)
  other arithmetic  21.8 us (3%)
    pallas_call x1, Pallas kernels, close(): pl.pallas_call(functools.partial(close_kernel, n_line, n_fsdp), in_specs=...  344 us
    pallas_call x1, Pallas kernels, attn_back(): pl.pallas_call(functools.partial(back_kernel, n_line, group), in_specs=[V...  151 us
    pallas_call x1, Pallas kernels, front(): pl.pallas_call(functools.partial(front_kernel, group, n_line), in_specs=[...  114 us
    unnamed x10, local copies, waits for them, and re-layouts  27.5 us

profile of v1, /device:TPU:0, one launch (start us, length us, event | category | flops | bytes accessed | tf_op | source)
XLA Modules:
  0.0 663.6 jit_solution(15824549682657007664)
XLA Ops:
  0.6 0.0 copy-start
  0.7 0.8 convert_element_type.11
  1.5 1.3 broadcast_in_dim.17
  2.8 1.4 copy_bitcast_fusion.1
  4.1 1.9 fusion
  6.0 1.3 pad_maximum_fusion.1
  7.3 0.0 copy-done
  7.3 0.6 copy.25
  8.0 1.8 pad_maximum_fusion.w_ref
  9.8 114.2 %front.1 = (bf16[1024,1024]{1,0:T(8,128)(2,1)}, bf16[1024,1024]{1,0:T(8,128)(2,1)}, f32[8,1,1024]{2,1,0:T(1,128)}, bf16[1024,256]{1,0:T(8,128)(2,1)}, bf16[1024,...) custom-call(bf16[1024,4096]{1,0:T(8,128)(2,1)} %bitcast.23, ...), custom_call_target="tpu_custom_call" | custom-call | tf_op jit(solution)/shard_map/front/pallas_call | solution.py:395
  123.9 151.3 %attn_back.1 = (bf16[1024,1536]{1,0:T(8,128)(2,1)}, bf16[4,1024,1024]{2,1,0:T(8,128)(2,1)}, bf16[4,4,1024,1024]{3,2,1,0:T(8,128)(2,1)}) custom-call(bf16[1024,1024]{1,0:T(8,128)(2,1)} %get-tuple-element.26.o_ref, bf16[1024,1024]{1,0:T(8,128)(2,1)} %get-tuple-element.27.q_ref, ...), custom_call_target="tpu_custom_call", output_to_operand_aliasing={{2}: (9, {})} | custom-call | tf_op jit(solution)/shard_map/attn_back/pallas_call | solution.py:685
  275.3 343.7 %close.1 = (bf16[1024,4096]{1,0:T(8,128)(2,1)}, bf16[1024,4096]{1,0:T(8,128)(2,1)}, f32[1,1024]{1,0:T(1,128)}, f32[1024,2560]{1,0:T(8,128)}, f32[1024,2560]{1,0:...) custom-call(bf16[1024,1536]{1,0:T(8,128)(2,1)} %get-tuple-element.34.d_, ...), custom_call_target="tpu_custom_call" | custom-call | tf_op jit(solution)/shard_map/close/pallas_call | solution.py:1118
  619.0 2.5 slice_add_fusion
  621.4 12.3 %add_bitcast_fusion = (f32[1024,1024]{0,1:T(8,128)}, f32[128,8,8,128]{3,1,2,0:T(8,128)}) fusion(f32[1024,2560]{1,0:T(8,128)} %get-tuple-element.44, f32[1024,2560]{1,0:T(8,128)} %get-tuple-element.43), kind=kLoop, calls=%fused_computation | loop fusion | flops 2097152 | bytes 25165824 | tf_op jit(solution)/shard_map/transpose | solution.py:1168
  633.7 5.3 copy.17
  639.0 1.5 reshape.53
  640.5 1.5 reshape.52
  642.0 5.2 copy.21
  647.2 7.9 %copy.30 = bf16[1,1024,4096]{2,1,0:T(8,128)(2,1)} copy(bf16[1,1024,4096]{2,1,0:T(8,128)(2,1)} %bitcast.29) | data formatting | bytes 16777216
  655.1 0.0 copy-start.1
  655.1 7.9 %copy.31 = bf16[1,1024,4096]{2,1,0:T(8,128)(2,1)} copy(bf16[1,1024,4096]{2,1,0:T(8,128)(2,1)} %bitcast.28) | data formatting | bytes 16777216
  663.0 0.0 copy-done.1
  663.0 0.6 copy.32
  (1 shorter events, 0.0 us)
Async XLA Ops:
  0.6 6.7 %copy-start = (bf16[1024,8,128]{2,1,0:T(8,128)(2,1)S(1)}, bf16[1024,8,128]{2,1,0:T(8,128)(2,1)}, u32[]{:S(2)}) copy-start(bf16[1024,8,128]{2,1,0:T(8,128)(2,1)} %param.12) | copy-start | bytes 6291460
  655.1 7.9 %copy-start.1 = (f32[1,1024]{1,0:T(1,128)S(1)}, f32[1,1024]{1,0:T(1,128)}, u32[]{:S(2)}) copy-start(f32[1,1024]{1,0:T(1,128)} %get-tuple-element.42) | copy-start | bytes 12292

commit v2 on v1

--- a/solution.py
+++ b/solution.py
@@ -14,12 +14,15 @@
 NEG_BIG = -1e30
 LOG2E = math.log2(math.e)
 TILES = 4
-CHUNKS = 16
+CHUNKS = 32
+PER_STEP = 2
 PIECES = 4
 O_PIECES = 2
+O_EARLY = 2
 GRAD_CHUNKS = 8
 FIRST_X = 5
-EARLY = 6
+EARLY = 5
+LATE = ((5, 1), (6, 10), (7, 20))
 VMEM_BYTES = 67043328
 
 MESH = pl.DeviceIdType.MESH
@@ -75,6 +78,12 @@
     return [{axis: lax.rem(index + k, count)} for k in range(1, count)]
 
 
+def nearest(z, last):
+    near = jnp.where(z > 0, last, 1)
+    second = jnp.where(z == 0, 2, jnp.where(z == last, last - 1, 1))
+    return near, second
+
+
 def rope(vals, cos, sin, half_dim):
     return vals * cos + pltpu.roll(vals, half_dim, 1) * sin
 
@@ -96,7 +105,7 @@
     return jnp.concatenate([cosines, cosines], axis=1), jnp.concatenate([-sines, sines], axis=1)
 
 
-def front_kernel(group, n_line, hid_ref, gain_ref, w_ref, wo_ref, cos_ref, sin_ref, o_ref, qr_ref, lse_ref, kl_ref, vl_ref, kp_ref, vp_ref, gfull_ref, n_out, w_out, wo_all, wbuf, nbuf, acc, hbuf, gbuf, qs, vt, m_all, l_all, acc_all, h_sem, g_send, g_recv, own_send, own_recv, x_send, x_recv, y_send, y_recv, d_send, d_recv, kv_send, kv_recv, ox_send, ox_recv, oy_send, oy_recv, od_send, od_recv, zw_send, zw_recv, out_sem):
+def front_kernel(group, n_line, hid_ref, gain_ref, w_ref, wo_ref, cos_ref, sin_ref, o_ref, qr_ref, lse_ref, kl_ref, vl_ref, kp_ref, vp_ref, gfull_ref, n_out, w_out, wo_all, o_all, wbuf, nbuf, acc, hbuf, gbuf, qs, vt, m_all, l_all, acc_all, h_sem, g_send, g_recv, own_send, own_recv, x_send, x_recv, y_send, y_recv, d_send, d_recv, kv_send, kv_recv, ox_send, ox_recv, oy_send, oy_recv, od_send, od_recv, zw_send, zw_recv, wx_send, wx_recv, ot_send, ot_recv, out_sem):
     q_len, feat = hid_ref.shape[0], w_ref.shape[0]
     head_dim = cos_ref.shape[1]
     half_dim = head_dim // 2
@@ -162,6 +171,21 @@
         mine = blk(flag, o_half)
         return remote(wo_ref.at[mine], wo_all.at[owner, f, mine], zw_send.at[k - 1], zw_recv.at[k - 1], {"tp": lax.rem(z + k, n_line)})
 
+    def wx_copy(k, r, slot):
+        spot = wo_all.at[lax.rem(z + r, n_line), slot, blk(flag, o_half)]
+        return remote(spot, spot, wx_send.at[k], wx_recv.at[k], to_x)
+
+    def wx_start(k, r):
+        zw_copy(n_line - r, lax.rem(z + r, n_line)).wait_recv()
+        wx_copy(k, r, f).start()
+
+    def ot_copy(up, j, owner):
+        src = o_ref.at[blk(j, tq)]
+        where = jnp.minimum(z + 1, last) if up else jnp.maximum(z - 1, 0)
+        return remote(src, o_all.at[owner, blk(j, tq)], ot_send.at[up, j], ot_recv.at[up, j], {"tp": where})
+
+    last = n_line - 1
+    steps_x = nearest(z, last)
     for k in range(1, n_line):
         zw_copy(k, z).start()
     gains = [(k, where, where["fsdp"]) for k, where in enumerate((to_core, to_x, to_diag))]
@@ -272,14 +296,14 @@
             kv_copy(k).start()
 
     def load_q(item):
-        g, tile = item // TILES, lax.rem(item, TILES)
+        g, tile = lax.rem(item, kv_heads), item // kv_heads
         rows = blk(tile, tq)
         for h in range(group):
-            qs[blk(h, tq), :] = qr_ref[rows, blk(g * group + h, head_dim)]
+            qs[:, blk(h, tq)] = qr_ref[rows, blk(g * group + h, head_dim)].T
 
     def key_piece(item, k_ref, side, start, masked):
-        g = item // TILES
-        scores = dot(k_ref[start, blk(g, head_dim)], qs[...], NT)
+        g = lax.rem(item, kv_heads)
+        scores = dot(k_ref[start, blk(g, head_dim)], qs[...], NN)
         if masked:
             scores = causal(scores, tq)
         m_old = m_all[item]
@@ -293,23 +317,30 @@
     for g in range(kv_heads):
         vt[g, 0] = vl_ref[:, blk(g, head_dim)].T
 
+    wx_start(0, steps_x[0])
+
     @pl.loop(0, kv_heads * TILES)
     def _(item):
-        tile = lax.rem(item, TILES)
+        tile = item // kv_heads
         load_q(item)
         m_all[item] = jnp.full_like(m_all[item], NEG_BIG)
         l_all[item] = jnp.zeros_like(l_all[item])
         acc_all[item] = jnp.zeros_like(acc_all[item])
         key_piece(item, kl_ref, 0, blk(tile, tq), True)
 
-        @pl.loop(0, tile)
+        @pl.loop(0, tile // 2)
         def _(i):
-            key_piece(item, kl_ref, 0, blk(i, tq), False)
+            key_piece(item, kl_ref, 0, blk(i, 2 * tq), False)
+
+        @pl.when(lax.rem(tile, 2) == 1)
+        def _():
+            key_piece(item, kl_ref, 0, blk(tile - 1, tq), False)
 
     for j in range(O_PIECES):
         ox_copy(j, f_x).wait_recv()
         oy_copy(j, flag).start()
         od_copy(1 + j, wo_out.at[f_x, o_span(flag, j)], f_x, o_span(flag, j)).start()
+    wx_start(1, steps_x[1])
 
     @pl.when(flag == 1)
     def _():
@@ -320,22 +351,31 @@
 
     @pl.loop(0, kv_heads * TILES)
     def _(item):
-        g, tile = item // TILES, lax.rem(item, TILES)
+        g, tile = lax.rem(item, kv_heads), item // kv_heads
         rows = blk(tile, tq)
 
         @pl.when(flag == 1)
         def _():
             load_q(item)
 
-        @pl.loop(0, flag * TILES)
+        @pl.loop(0, flag * TILES // 2)
         def _(i):
-            key_piece(item, kp_ref, 1, blk(i, tq), False)
+            key_piece(item, kp_ref, 1, blk(i, 2 * tq), False)
 
         total = l_all[item]
-        lse_ref[item] = m_all[item] * scale + jnp.log2(total)
+        lse_ref[g * TILES + tile] = m_all[item] * scale + jnp.log2(total)
         out_t = acc_all[item] / total
         for h in range(group):
             o_ref[rows, blk(g * group + h, head_dim)] = out_t[:, h * tq:h * tq + tq].T.astype(BF)
+
+        for j in range(O_EARLY):
+            @pl.when((item == (j + 1) * kv_heads) & (z > 0))
+            def _():
+                ot_copy(0, j, z).start()
+
+            @pl.when((item == (j + 1) * kv_heads) & (z < last))
+            def _():
+                ot_copy(1, j, z).start()
 
         for j in range(O_PIECES):
             @pl.when(item == (j + 1) * kv_heads * TILES // O_PIECES - 1)
@@ -348,9 +388,20 @@
         od_copy(1 + j, wo_out.at[f_x, o_span(flag, j)], f_diag, o_span(flag, j)).wait_recv()
         od_copy(1 + O_PIECES + j, wo_out.at[f_x, o_span(1 - flag, j)], f_diag, o_span(1 - flag, j)).wait_recv()
 
+    third = n_line * last // 2 - sum(steps_x)
+    zw_copy(n_line - third, lax.rem(z + third, n_line)).wait_recv()
     for k in range(1, n_line):
-        zw_copy(k, lax.rem(z + n_line - k, n_line)).wait_recv()
         zw_copy(k, z).wait_send()
+    for k, r in enumerate(steps_x):
+        wx_copy(k, r, f_x).wait_recv()
+        wx_copy(k, r, f).wait_send()
+    for j in range(O_EARLY):
+        for up in range(2):
+            @pl.when(z < last if up else z > 0)
+            def _():
+                ot_copy(up, j, z).wait_send()
+                ot_copy(1 - up, j, z + 1 if up else z - 1).wait_recv()
+
     for k, where, _ in gains:
         g_copy(k, where, f).wait_send()
     own_copy(f).wait_send()
@@ -391,30 +442,31 @@
     q_like = sds((q_len, q_width), BF)
     line = pltpu.VMEM((items, 1, wide), F32)
     own, pair, trio = DMA(()), DMA((2,)), DMA((n_fsdp - 1,))
+    early = DMA((2, O_EARLY))
     w_link, w_side, o_link, o_core, z_link = DMA((PIECES,)), DMA((2, PIECES)), DMA((O_PIECES,)), DMA((1 + 2 * O_PIECES,)), DMA((n_line - 1,))
     return pl.pallas_call(
         functools.partial(front_kernel, group, n_line),
         in_specs=[ANY] + [VMEM] * 5,
-        out_specs=[VMEM] * 8 + [ANY] * 3,
-        out_shape=[q_like, q_like, sds((items, 1, wide), F32), kv, kv, kv, kv, sds((1, model_dim), F32), sds((q_len, model_dim), BF), sds((n_fsdp, feat, width), BF), sds((n_line, n_fsdp, o_rows, o_cols), BF)],
+        out_specs=[VMEM] * 8 + [ANY] * 4,
+        out_shape=[q_like, q_like, sds((items, 1, wide), F32), kv, kv, kv, kv, sds((1, model_dim), F32), sds((q_len, model_dim), BF), sds((n_fsdp, feat, width), BF), sds((n_line, n_fsdp, o_rows, o_cols), BF), sds((n_line, q_len, q_width), BF)],
         scratch_shapes=[
             pltpu.VMEM((n_fsdp, feat, width), BF),
             pltpu.VMEM((q_len, model_dim), BF),
             pltpu.VMEM((q_len, width), F32),
             pltpu.VMEM((2, tq, model_dim), BF),
             pltpu.VMEM((n_fsdp, 1, feat), F32),
-            pltpu.VMEM((wide, head_dim), BF),
+            pltpu.VMEM((head_dim, wide), BF),
             pltpu.VMEM((kv_heads, 2, head_dim, q_len), BF),
             line,
             line,
             pltpu.VMEM((items, head_dim, wide), F32),
-        ] + [pair, trio, trio, own, own, w_link, w_link, w_link, w_link, w_side, w_side, pair, pair, o_link, o_link, o_link, o_link, o_core, o_core, z_link, z_link, DMA((4,))],
+        ] + [pair, trio, trio, own, own, w_link, w_link, w_link, w_link, w_side, w_side, pair, pair, o_link, o_link, o_link, o_link, o_core, o_core, z_link, z_link, pair, pair, early, early, DMA((4,))],
         compiler_params=params(cid),
         name="front",
     )(hidden, gain, w_qkv, w_out, cosines, sines)
 
 
-def back_kernel(n_line, group, o_ref, q_ref, lse_ref, cos_ref, sin_ref, kl_ref, vl_ref, kp_ref, vp_ref, _wo_in, ct_ref, d_ref, o_all, wo_all, w_ref, ctb_ref, do_ref, dkl_ref, dvl_ref, dkp_ref, dvp_ref, qs_ref, dos_ref, delta_ref, kt_ref, dqt_ref, load_sem, keep_sem, ct_sem, od_send, ou_send, o_recv, y_send, y_recv, x_send, x_recv, c_send, c_recv, cx_send, cx_recv, kv_send, kv_recv):
+def back_kernel(n_line, group, o_ref, q_ref, lse_ref, cos_ref, sin_ref, kl_ref, vl_ref, kp_ref, vp_ref, _wo_in, _o_in, ct_ref, d_ref, o_all, wo_all, w_ref, ctb_ref, do_ref, dkl_ref, dvl_ref, dkp_ref, dvp_ref, qs_ref, dos_ref, delta_ref, kt_ref, dqt_ref, load_sem, keep_sem, ct_sem, od_send, ou_send, o_recv, y_send, y_recv, x_send, x_recv, c_send, c_recv, cx_send, cx_recv, kv_send, kv_recv):
     last = n_line - 1
     z, flag, f = lax.axis_index("tp"), lax.axis_index("cp"), lax.axis_index("fsdp")
     far = 1 - flag
@@ -468,7 +520,7 @@
     def cx_copy(r, side, slot):
         return remote(wo_half(r, slot, side), wo_half(r, slot, side), cx_send.at[side, r - 1], cx_recv.at[side, r - 1], to_core)
 
-    for j in range(TILES):
+    for j in range(O_EARLY, TILES):
         @pl.when(z > 0)
         def _():
             o_down(z, j, o_ref.at[tile_rows(j)]).start()
@@ -477,9 +529,19 @@
         def _():
             o_up(z, j, o_ref.at[tile_rows(j)]).start()
 
+    for j in range(O_EARLY):
+        @pl.when((z > 0) & (z < last))
+        def _():
+            o_down(z + 1, j, o_all.at[z + 1, tile_rows(j)]).start()
+            o_up(z - 1, j, o_all.at[z - 1, tile_rows(j)]).start()
+
+    steps_x = nearest(z, last)
+    third = n_line * last // 2 - sum(steps_x)
+    x_copy(third, flag, f).start()
+    for r in steps_x:
+        cx_copy(r, flag, f_x).start()
     for r in range(1, n_line):
         y_copy(r, flag).start()
-        x_copy(r, flag, f).start()
         c_copy(r, flag, f).start()
 
     def o_tick(k):
@@ -509,7 +571,7 @@
         c_copy(r, far, f).start()
 
     def x_tick(q):
-        r, side = q % (n_line - 1) + 1, flag if q < n_line - 1 else far
+        r, side = (q, far) if q else (third, flag)
         x_copy(r, side, f_x).wait_recv()
         cx_copy(r, side, f_x).start()
 
@@ -559,23 +621,27 @@
                 scores = causal(scores, tq)
             probs = jnp.exp2(scores * (score_scale * LOG2E) - lse_ref[item])
             d_probs = dot(v_ref[span, kv_cols], dos_ref[...], NT)
-            d_scores = (probs * (d_probs - delta_ref[...]) * score_scale).astype(BF)
+            d_scores = (probs * (d_probs - delta_ref[...])).astype(BF)
             dv_ref[g, span, :] += dot(probs.astype(BF), dos_ref[...], NN)
             dk_ref[g, span, :] += dot(d_scores, qs_ref[...], NN)
             dqt_ref[...] += dot(kt_ref[side, :, span], d_scores, NN)
 
         piece(kl_ref, vl_ref, dkl_ref, dvl_ref, 0, blk(tile, tq), True)
 
-        @pl.loop(0, tile)
+        @pl.loop(0, tile // 2)
         def _(i):
-            piece(kl_ref, vl_ref, dkl_ref, dvl_ref, 0, blk(i, tq), False)
-
-        @pl.loop(0, flag * (q_len // tq))
+            piece(kl_ref, vl_ref, dkl_ref, dvl_ref, 0, blk(i, 2 * tq), False)
+
+        @pl.when(lax.rem(tile, 2) == 1)
+        def _():
+            piece(kl_ref, vl_ref, dkl_ref, dvl_ref, 0, blk(tile - 1, tq), False)
+
+        @pl.loop(0, flag * TILES // 2)
         def _(i):
-            piece(kp_ref, vp_ref, dkp_ref, dvp_ref, 1, blk(i, tq), False)
+            piece(kp_ref, vp_ref, dkp_ref, dvp_ref, 1, blk(i, 2 * tq), False)
 
         for h in range(group):
-            dq_h = dqt_ref[:, h * tq:h * tq + tq].T
+            dq_h = dqt_ref[:, blk(h, tq)].T * score_scale
             d_ref[rows, blk(g * group + h, head_dim)] = rope(dq_h, cos_ref[rows, :], -sin_ref[rows, :], half_dim).astype(BF)
 
         @pl.when((tile == TILES - 1) & (flag == 1))
@@ -594,7 +660,7 @@
             dkl_ref[g] += dkp_ref[g]
             dvl_ref[g] += dvp_ref[g]
 
-        dk = rope(dkl_ref[g], cos_ref[...], -sin_ref[...], half_dim)
+        dk = rope(dkl_ref[g] * score_scale, cos_ref[...], -sin_ref[...], half_dim)
         k_at = width // head_dim + g
         d_ref[:, blk(k_at, head_dim)] = dk.astype(BF)
         d_ref[:, blk(k_at + kv_heads, head_dim)] = dvl_ref[g].astype(BF)
@@ -605,9 +671,8 @@
                 copy.wait_send()
 
     items = TILES * (kv_heads + 1)
-    o_ticks, x_ticks = TILES * last, 2 * last
-    y_at = {4 + 3 * (r - 1): r for r in range(1, n_line)}
-    x_at = {5: 0, 9: 1, 11: 2}
+    o_ticks = TILES * last
+    x_at = {5: 0, 8: 1, 11: 2}
 
     @pl.loop(0, items)
     def _(item):
@@ -619,12 +684,12 @@
         def _():
             bwd_item(item - TILES)
 
-        @pl.when(lax.rem(item, 2) == 1)
-        def _():
-            o_tick(item // 2)
-
-        for at, r in y_at.items():
-            @pl.when(item == at)
+        @pl.when((lax.rem(item, 2) == 1) & (item > 1))
+        def _():
+            o_tick(item // 2 - 1 + O_EARLY)
+
+        for r in range(1, n_line):
+            @pl.when(item == 3 * r + 1)
             def _():
                 y_tick(r)
 
@@ -633,8 +698,8 @@
             def _():
                 x_tick(q)
 
-    done = items // 2
-    tail = [("x", q) for q in range(len(x_at), x_ticks)] + [("kv", g) for g in range(kv_heads)]
+    done = items // 2 - 1 + O_EARLY
+    tail = [("x", q) for q in range(len(x_at), n_line)] + [("kv", g) for g in range(kv_heads)]
     for k in range(done, o_ticks):
         o_tick(jnp.int32(k))
         if (k - done) % 2 == 1 and tail:
@@ -651,27 +716,30 @@
         for side in (flag, far):
             c_copy(r, side, f_core).wait_recv()
             cx_copy(r, side, f_diag).wait_recv()
-            x_copy(r, side, f).wait_send()
             c_copy(r, side, f).wait_send()
             cx_copy(r, side, f_x).wait_send()
+        x_copy(r, far, f).wait_send()
         y_copy(r, flag).wait_send()
+    x_copy(third, flag, f).wait_send()
 
     @pl.loop(0, n_line)
     def _(t):
         @pl.when((t >= z) & (z > 0))
         def _():
-            for j in range(TILES):
+            @pl.loop(jnp.where(t == z, O_EARLY, 0), TILES)
+            def _(j):
                 o_down(t, j, o_all.at[t, tile_rows(j)]).wait_send()
 
         @pl.when((t <= z) & (z < last))
         def _():
-            for j in range(TILES):
+            @pl.loop(jnp.where(t == z, O_EARLY, 0), TILES)
+            def _(j):
                 o_up(t, j, o_all.at[t, tile_rows(j)]).wait_send()
 
     keep.wait()
 
 
-def attn_back(attn_out, q_rot, lse, cosines, sines, k_loc, v_loc, k_prev, v_prev, wo_all, cotangent, n_line, group, cid):
+def attn_back(attn_out, q_rot, lse, cosines, sines, k_loc, v_loc, k_prev, v_prev, wo_all, o_all, cotangent, n_line, group, cid):
     q_len, width = attn_out.shape
     head_dim = cosines.shape[1]
     kv_width = k_loc.shape[1]
@@ -684,10 +752,10 @@
     own, pair, tiles, hop, side, kv = DMA(()), DMA((2,)), DMA((n_line, TILES)), DMA((n_line - 1,)), DMA((2, n_line - 1)), DMA((2, kv_heads))
     return pl.pallas_call(
         functools.partial(back_kernel, n_line, group),
-        in_specs=[VMEM] * 9 + [ANY] * 2,
+        in_specs=[VMEM] * 9 + [ANY] * 3,
         out_specs=[VMEM, ANY, ANY],
         out_shape=[jax.ShapeDtypeStruct((q_len, width + 2 * kv_width), BF), jax.ShapeDtypeStruct((n_line, q_len, width), BF), jax.ShapeDtypeStruct(wo_all.shape, BF)],
-        input_output_aliases={9: 2},
+        input_output_aliases={9: 2, 10: 1},
         scratch_shapes=[
             pltpu.VMEM((n_fsdp, o_rows, o_cols), BF),
             pltpu.VMEM((2, tq, cotangent.shape[1]), BF),
@@ -701,7 +769,7 @@
         ] + [own, own, pair, tiles, tiles, tiles, hop, hop, side, side, side, side, side, side, kv, kv],
         compiler_params=params(cid),
         name="attn_back",
-    )(attn_out, q_rot, lse, cosines, sines, k_loc, v_loc, k_prev, v_prev, wo_all, cotangent)
+    )(attn_out, q_rot, lse, cosines, sines, k_loc, v_loc, k_prev, v_prev, wo_all, o_all, cotangent)
 
 
 class Line:
@@ -853,6 +921,38 @@
         e_store(j).wait()
         y_copy(j).start()
 
+    steps = chunks + last - 1
+
+    def dist(side):
+        return z if side else last - z
+
+    def hop(side, chunk):
+        span = blk(side * chunks + chunk, rows)
+        up = z - 1 if side else z + 1
+        return remote(out_ref.at[span], out_ref.at[span], out_send.at[side, chunk], out_recv.at[side, chunk], {"tp": jnp.clip(up, 0, last)})
+
+    ends = [(end, z == (last if end else 0)) for end in range(2)]
+
+    def owner_send(first, stop):
+        for end, here in ends:
+            @pl.when(here)
+            def _():
+                @pl.loop(first, stop)
+                def _(c):
+                    hop(end, c).start()
+
+    def pass_on(step):
+        for side in range(2):
+            chunk = step - (last - 1 - dist(side))
+
+            @pl.when((dist(side) < last) & (chunk >= 0) & (chunk < chunks))
+            def _():
+                hop(side, chunk).wait_recv()
+
+                @pl.when(dist(side) > 0)
+                def _():
+                    hop(side, chunk).start()
+
     def sum_phase(wbuf, pbuf, abuf, bbuf, lbuf, lhs):
         w_load = copy(w_all, wbuf, w_sem)
         w_load.start()
@@ -911,29 +1011,47 @@
         w_load.wait()
 
         @pl.loop(0, line.steps)
-        def _(step):
-            line.tick(step)
+        def _(fine):
+            line.tick(fine)
+            step = fine // PER_STEP
+            whole = lax.rem(fine, PER_STEP) == 0
             j, odd = step // 2, lax.rem(step, 2)
 
-            @pl.when((odd == 0) & (j > 0) & (j <= GRAD_CHUNKS))
+            @pl.when(whole & (odd == 0) & (j > 0) & (j <= GRAD_CHUNKS))
             def _():
                 send_x(j - 1)
 
-            @pl.when((odd == 0) & (j < GRAD_CHUNKS))
+            @pl.when(whole & (odd == 0) & (j < GRAD_CHUNKS))
             def _():
                 make(j)
 
-            @pl.when((odd == 1) & (j < GRAD_CHUNKS))
+            @pl.when(whole & (odd == 1) & (j < GRAD_CHUNKS))
             def _():
                 meet_core(j)
 
             for late in range(2):
                 k = (step - FIRST_X - late) * 2 // 5
 
-                @pl.when((k >= 0) & (k < EARLY) & (step - late == FIRST_X + (5 * k + 1) // 2))
+                @pl.when(whole & (k >= 0) & (k < EARLY) & (step - late == FIRST_X + (5 * k + 1) // 2))
                 def _():
                     send_y(k) if late else meet_x(k)
 
+            @pl.when(fine >= chunks)
+            def _():
+                ready = fine - last - 1
+                owner_send(jnp.where(fine == chunks, 0, ready - 1), ready)
+
+            @pl.when(fine > chunks)
+            def _():
+                for k in range(PER_STEP):
+                    pass_on((fine - chunks - 1) * PER_STEP + k)
+
+        @pl.when(owner)
+        def _():
+            for chunk in range(chunks - 2, chunks):
+                f_store(chunk).wait()
+
+        owner_send(chunks - 2, chunks)
         line.drain()
 
     pl.run_scoped(
@@ -945,16 +1063,6 @@
         pltpu.VMEM((2, g_rows, ts.shape[1]), F32),
         pltpu.VMEM((2, n_fsdp, d_ref.shape[0], g_rows), BF),
     )
-    steps = chunks + last - 1
-
-    def dist(side):
-        return z if side else last - z
-
-    def hop(side, chunk):
-        span = blk(side * chunks + chunk, rows)
-        up = z - 1 if side else z + 1
-        return remote(out_ref.at[span], out_ref.at[span], out_send.at[side, chunk], out_recv.at[side, chunk], {"tp": jnp.clip(up, 0, last)})
-
     def ga_copy(end, k):
         return remote(gp, ga.at[end], ga_send.at[k], ga_recv.at[end], {"tp": k if end else 1 + k})
 
@@ -964,8 +1072,6 @@
     def gc_copy(k, slot):
         to = lax.rem(f + k, n_fsdp)
         return remote(gt.at[to], gc.at[slot], gc_send.at[k - 1], gc_recv.at[k - 1], {"fsdp": to})
-
-    ends = [(end, z == (last if end else 0)) for end in range(2)]
 
     def spread_phase(obuf, wbuf, hbuf, rbuf):
         o_load = copy(o_all, obuf, o_sem)
@@ -993,12 +1099,6 @@
                 for k in range(last):
                     ga_copy(end, k).start()
 
-                for chunk in range(chunks - 2, chunks):
-                    f_store(chunk).wait()
-
-                @pl.loop(0, chunks)
-                def _(chunk):
-                    hop(end, chunk).start()
 
         def project(item):
             slot = lax.rem(item, 2)
@@ -1030,30 +1130,23 @@
         o_load.wait()
         gb_copy().start()
 
-        @pl.loop(0, steps)
+        early = (last - 1) * PER_STEP
+
+        @pl.loop(0, steps - early)
         def _(step):
-            for side in range(2):
-                chunk = step - (last - 1 - dist(side))
-
-                @pl.when((dist(side) < last) & (chunk >= 0) & (chunk < chunks))
-                def _():
-                    hop(side, chunk).wait_recv()
-
-                    @pl.when(dist(side) > 0)
-                    def _():
-                        hop(side, chunk).start()
-
-            @pl.when((lax.rem(step, 2) == 0) & (step // 2 < items))
-            def _():
-                project(step // 2)
-
-            for k in range(EARLY, GRAD_CHUNKS):
-                @pl.when(step == 1 + 5 * (k - EARLY))
+            pass_on(step + early)
+
+            @pl.when((lax.rem(step, 3) == 0) & (step // 3 < items))
+            def _():
+                project(step // 3)
+
+            for k, at in LATE:
+                @pl.when(step == at)
                 def _():
                     meet_x(k)
 
-            for k in range(EARLY - 1, GRAD_CHUNKS):
-                @pl.when(step == 2 + 5 * (k - EARLY) if k >= EARLY else step == 0)
+            for k, at in LATE:
+                @pl.when(step == at + 1)
                 def _():
                     send_y(k)
 
@@ -1138,6 +1231,44 @@
     )(d_lin, attn_out, gain, hidden, cotangent, normed, w_full, o_all, wo_all)
 
 
+def tail_kernel(head_dim, blk_ref, hid_ref, mine_ref, theirs_ref, blk_out, hid_out, q_out, k_out, v_out, o_out):
+    blk_out[...] = blk_ref[...]
+    hid_out[...] = hid_ref[...]
+    at = 0
+    for ref in (q_out, k_out, v_out):
+        for h in range(ref.shape[1]):
+            cols = blk(at, head_dim)
+            ref[:, h, :] = mine_ref[:, cols] + theirs_ref[:, cols]
+            at += 1
+    rest = slice(at * head_dim, None)
+    o_out[...] = (mine_ref[:, rest] + theirs_ref[:, rest]).T
+
+
+def tail(block_out, grad_hidden, mine, theirs, q_heads, kv_heads, head_dim):
+    q_len, model_dim = block_out.shape
+    feat = mine.shape[0]
+    sds = jax.ShapeDtypeStruct
+    act = pl.BlockSpec((q_len // GRAD_CHUNKS, model_dim), lambda i: (i, 0))
+    part = pl.BlockSpec((feat // GRAD_CHUNKS, mine.shape[1]), lambda i: (i, 0))
+
+    def heads(n):
+        return pl.BlockSpec((feat // GRAD_CHUNKS, n, head_dim), lambda i: (i, 0, 0))
+
+    def like(n):
+        return sds((feat, n, head_dim), F32)
+
+    o_rows = q_heads * head_dim
+    return pl.pallas_call(
+        functools.partial(tail_kernel, head_dim),
+        grid=(GRAD_CHUNKS,),
+        in_specs=[act, act, part, part],
+        out_specs=[act, act, heads(q_heads), heads(kv_heads), heads(kv_heads), pl.BlockSpec((o_rows, feat // GRAD_CHUNKS), lambda i: (0, i))],
+        out_shape=[sds(block_out.shape, BF), sds(block_out.shape, BF), like(q_heads), like(kv_heads), like(kv_heads), sds((o_rows, feat), F32)],
+        compiler_params=pltpu.CompilerParams(vmem_limit_bytes=VMEM_BYTES),
+        name="tail",
+    )(block_out, grad_hidden, mine, theirs)
+
+
 def solution(mesh):
     act_spec = P("fsdp", "cp", None)
     proj_spec = P("fsdp", "tp", None)
@@ -1153,20 +1284,11 @@
         q_width, kv_width = q_heads * head_dim, kv_heads * head_dim
         w_qkv = jnp.concatenate([w_query.reshape(feat, q_width), w_key.reshape(feat, kv_width), w_value.reshape(feat, kv_width)], axis=1)
         cosines, sines = rope_tables(positions, head_dim)
-        attn_out, q_rot, lse, k_loc, v_loc, k_prev, v_prev, gain_full, normed, w_full, wo_all = front(hidden, gain.astype(F32)[None], w_qkv, w_out.reshape(q_width, feat), cosines, sines, group, kv_width, n_line, 0)
-        d_lin, o_all, wo_all = attn_back(attn_out, q_rot, lse, cosines, sines, k_loc, v_loc, k_prev, v_prev, wo_all, cotangent, n_line, group, 1)
+        attn_out, q_rot, lse, k_loc, v_loc, k_prev, v_prev, gain_full, normed, w_full, wo_all, o_all = front(hidden, gain.astype(F32)[None], w_qkv, w_out.reshape(q_width, feat), cosines, sines, group, kv_width, n_line, 0)
+        d_lin, o_all, wo_all = attn_back(attn_out, q_rot, lse, cosines, sines, k_loc, v_loc, k_prev, v_prev, wo_all, o_all, cotangent, n_line, group, 1)
         grad_hidden, block_out, grad_gain, mine, theirs = close(d_lin, attn_out, gain_full, hidden, cotangent, normed, w_full, o_all, wo_all, 2)[:5]
-        cuts = [q_width, q_width + kv_width, q_width + 2 * kv_width]
-        g_query, g_key, g_value, g_out = [one + two for one, two in zip(jnp.split(mine, cuts, axis=1), jnp.split(theirs, cuts, axis=1))]
-        return (
-            block_out[None],
-            grad_hidden[None],
-            grad_gain[0],
-            g_query.reshape(w_query.shape),
-            g_key.reshape(w_key.shape),
-            g_value.reshape(w_value.shape),
-            g_out.T.reshape(w_out.shape),
-        )
+        block_out, grad_hidden, g_query, g_key, g_value, g_out = tail(block_out, grad_hidden, mine, theirs, q_heads, kv_heads, head_dim)
+        return block_out[None], grad_hidden[None], grad_gain[0], g_query, g_key, g_value, g_out.reshape(w_out.shape)
 
     specs = (act_spec, act_spec, P("fsdp"), proj_spec, proj_spec, proj_spec, wout_spec)
     return jax.shard_map(device_step, mesh=mesh, in_specs=specs[:2] + (P("cp"),) + specs[2:], out_specs=specs, check_vma=False)

time: 664 us -> 742 us (1.12)
  Pallas kernels: 609 us -> 730 us
  local copies, waits for them, and re-layouts: 31.9 us -> 3.26 us
  other arithmetic: 21.8 us -> 7.12 us
    pallas_call x1, Pallas kernels: 344 us -> 454 us  [close(): pl.pallas_call(functools.partial(close_kernel, n_line, n_fsdp), in_specs=...]
    unnamed x10 -> x4, local copies, waits for them, and re-layouts: 27.5 us -> 1.9 us
    pallas_call x1, Pallas kernels: 151 us -> 129 us  [attn_back(): pl.pallas_call(functools.partial(back_kernel, n_line, group), in_specs=[V...]
    pallas_call x0 -> x1, Pallas kernels: none -> 21.1 us  [tail(): pl.pallas_call(functools.partial(tail_kernel, head_dim), grid=(GRAD_CHUNK...]
    pallas_call x1, Pallas kernels: 114 us -> 126 us  [front(): pl.pallas_call(functools.partial(front_kernel, group, n_line), in_specs=[...]
    transpose x1 -> x0, other arithmetic: 12.3 us -> none  [device_step(): g_out.T.reshape(w_out.shape)]
where the time goes in v2:
time: 742 us; the launch traced here: 741 us
  Pallas kernels  730 us (98%)
    pallas_call x1, Pallas kernels, close(): pl.pallas_call(functools.partial(close_kernel, n_line, n_fsdp), in_specs=...  454 us
    pallas_call x1, Pallas kernels, attn_back(): pl.pallas_call(functools.partial(back_kernel, n_line, group), in_specs=[V...  129 us
    pallas_call x1, Pallas kernels, front(): pl.pallas_call(functools.partial(front_kernel, group, n_line), in_specs=[...  126 us
    pallas_call x1, Pallas kernels, tail(): pl.pallas_call(functools.partial(tail_kernel, head_dim), grid=(GRAD_CHUNK...  21.1 us

profile of v2, /device:TPU:0, one launch (start us, length us, event | category | flops | bytes accessed | tf_op | source)
XLA Modules:
  0.0 741.4 jit_solution(1589510020362385605)
XLA Ops:
  0.6 0.0 copy-start
  0.7 0.8 convert_element_type.11
  1.5 1.3 broadcast_in_dim.17
  2.8 1.4 copy_bitcast_fusion.1
  4.1 1.9 fusion
  6.0 1.3 pad_maximum_fusion.1
  7.3 0.0 copy-done
  7.3 0.6 copy.23
  8.0 1.8 pad_maximum_fusion.w_ref
  9.8 126.5 %front.1 = (bf16[1024,1024]{1,0:T(8,128)(2,1)}, bf16[1024,1024]{1,0:T(8,128)(2,1)}, f32[8,1,1024]{2,1,0:T(1,128)}, bf16[1024,256]{1,0:T(8,128)(2,1)}, bf16[1024,...) custom-call(bf16[1024,4096]{1,0:T(8,128)(2,1)} %bitcast.20, ...), custom_call_target="tpu_custom_call" | custom-call | tf_op jit(solution)/shard_map/front/pallas_call | solution.py:447
  136.3 128.6 %attn_back.1 = (bf16[1024,1536]{1,0:T(8,128)(2,1)}, bf16[4,1024,1024]{2,1,0:T(8,128)(2,1)}, bf16[4,4,1024,1024]{3,2,1,0:T(8,128)(2,1)}) custom-call(bf16[1024,1024]{1,0:T(8,128)(2,1)} %get-tuple-element.33.o_ref, bf16[1024,1024]{1,0:T(8,128)(2,1)} %get-tuple-element.34.q_ref, ...), custom_call_target="tpu_custom_call", output_to_operand_aliasing={{2}: (9, {}), {1}: (10, {})} | custom-call | tf_op jit(solution)/shard_map/attn_back/pallas_call | solution.py:753
  264.9 454.0 %close.1 = (bf16[1024,4096]{1,0:T(8,128)(2,1)}, bf16[1024,4096]{1,0:T(8,128)(2,1)}, f32[1,1024]{1,0:T(1,128)}, f32[1024,2560]{1,0:T(8,128)}, f32[1024,2560]{1,0:...) custom-call(bf16[1024,1536]{1,0:T(8,128)(2,1)} %get-tuple-element.42.d_, ...), custom_call_target="tpu_custom_call" | custom-call | tf_op jit(solution)/shard_map/close/pallas_call | solution.py:1211
  719.0 21.1 %tail.1 = (bf16[1024,4096]{1,0:T(8,128)(2,1)}, bf16[1024,4096]{1,0:T(8,128)(2,1)}, f32[1024,8,128]{2,1,0:T(8,128)}, f32[1024,2,128]{2,1,0:T(2,128)}, f32[1024,2,128]{2,1,0:T(2,128)}, /*index=5*/f32[1024,1024]{1,0:T(8,128)}) custom-call(bf16[1024,4096]{1,0:T(8,128)(2,1)} %get-tuple-element.48.blk_ref, bf16[1024,4096]{1,0:T(8,128)(2,1)} %get-tuple-element.49.hid_ref, ...), custom_call_target="tpu_custom_call" | custom-call | tf_op jit(solution)/shard_map/tail/pallas_call | solution.py:1261
  740.1 1.3 copy.27
  (1 shorter events, 0.0 us)
Async XLA Ops:
  0.6 6.7 copy-start

commit v3 on v2

--- a/solution.py
+++ b/solution.py
@@ -14,16 +14,17 @@
 NEG_BIG = -1e30
 LOG2E = math.log2(math.e)
 TILES = 4
-CHUNKS = 32
-PER_STEP = 2
+CHUNKS = 16
+PER_STEP = 1
 PIECES = 4
 O_PIECES = 2
 O_EARLY = 2
 GRAD_CHUNKS = 8
 FIRST_X = 5
-EARLY = 5
-LATE = ((5, 1), (6, 10), (7, 20))
+EARLY = 6
+LATE = ((6, 2), (7, 7))
 VMEM_BYTES = 67043328
+SIDES = range(2)
 
 MESH = pl.DeviceIdType.MESH
 ANY = pl.BlockSpec(memory_space=pl.ANY)
@@ -40,6 +41,10 @@
     return lax.dot_general(a, b, dims, preferred_element_type=F32)
 
 
+def parity(k):
+    return lax.rem(k, 2)
+
+
 def blk(k, n):
     return pl.ds(k * n if isinstance(k, int) else pl.multiple_of(k * n, n), n)
 
@@ -68,7 +73,7 @@
 
 
 def fsdp_peers(f):
-    core = lax.rem(f, 2)
+    core = parity(f)
     other = f + 1 - 2 * core
     far = lax.rem(f + 2, 4)
     return other, far, lax.rem(other + 2, 4)
@@ -122,12 +127,13 @@
     o_piece = o_half // O_PIECES
     flag, f, z = lax.axis_index("cp"), lax.axis_index("fsdp"), lax.axis_index("tp")
     wo_out = wo_all.at[z]
+    last = n_line - 1
     far = 1 - flag
     f_core, f_x, f_diag = fsdp_peers(f)
     to_core, to_x, to_diag, to_y = {"fsdp": f_core}, {"fsdp": f_x}, {"fsdp": f_diag}, {"cp": far}
 
     def h_load(tile):
-        slot = lax.rem(tile, 2)
+        slot = parity(tile)
         return pltpu.make_async_copy(hid_ref.at[blk(tile, tq)], hbuf.at[slot], h_sem.at[slot])
 
     h_load(0).start()
@@ -167,27 +173,39 @@
     def od_copy(k, src, slot, where):
         return remote(src, wo_out.at[slot, where], od_send.at[k], od_recv.at[k], to_core)
 
-    def zw_copy(k, owner):
-        mine = blk(flag, o_half)
-        return remote(wo_ref.at[mine], wo_all.at[owner, f, mine], zw_send.at[k - 1], zw_recv.at[k - 1], {"tp": lax.rem(z + k, n_line)})
+    def zw_copy(up, t):
+        spot = wo_all.at[t, f, blk(flag, o_half)]
+        where = jnp.minimum(z + 1, last) if up else jnp.maximum(z - 1, 0)
+        src = spot if t is not z else wo_ref.at[blk(flag, o_half)]
+        return remote(src, spot, zw_send.at[up, t], zw_recv.at[t], {"tp": where})
+
+    def zw_tick(r):
+        for up, t, here in ((0, z + r, z + r <= last), (1, z - r, z >= r)):
+            at = jnp.clip(t, 0, last)
+
+            @pl.when(here)
+            def _():
+                zw_copy(up, at).wait_recv()
+
+            @pl.when(here & (z < last if up else z > 0))
+            def _():
+                zw_copy(up, at).start()
 
     def wx_copy(k, r, slot):
         spot = wo_all.at[lax.rem(z + r, n_line), slot, blk(flag, o_half)]
         return remote(spot, spot, wx_send.at[k], wx_recv.at[k], to_x)
-
-    def wx_start(k, r):
-        zw_copy(n_line - r, lax.rem(z + r, n_line)).wait_recv()
-        wx_copy(k, r, f).start()
 
     def ot_copy(up, j, owner):
         src = o_ref.at[blk(j, tq)]
         where = jnp.minimum(z + 1, last) if up else jnp.maximum(z - 1, 0)
         return remote(src, o_all.at[owner, blk(j, tq)], ot_send.at[up, j], ot_recv.at[up, j], {"tp": where})
 
-    last = n_line - 1
     steps_x = nearest(z, last)
-    for k in range(1, n_line):
-        zw_copy(k, z).start()
+    for up in SIDES:
+        @pl.when(z < last if up else z > 0)
+        def _():
+            zw_copy(up, z).start()
+
     gains = [(k, where, where["fsdp"]) for k, where in enumerate((to_core, to_x, to_diag))]
     for k, where, _ in gains:
         g_copy(k, where, f).start()
@@ -248,6 +266,8 @@
     project(f_core, 0, feat)
     x_tick(1)
     y_tick(0)
+    zw_tick(1)
+    wx_copy(0, steps_x[0], f).start()
     x_tick(2)
     y_tick(1)
     x_tick(3)
@@ -260,9 +280,11 @@
     y_tick(3)
     for j in range(PIECES):
         d_copy(j, 1 - flag, f_diag).wait_recv()
-    second_half = pl.multiple_of((far) * half, half)
+    second_half = pl.multiple_of(far * half, half)
     project(f_x, second_half, half)
     project(f_diag, second_half, half)
+    zw_tick(2)
+    wx_copy(1, steps_x[1], f).start()
     put_w = pltpu.make_async_copy(wbuf, w_out, out_sem.at[3])
     put_w.start()
 
@@ -317,8 +339,6 @@
     for g in range(kv_heads):
         vt[g, 0] = vl_ref[:, blk(g, head_dim)].T
 
-    wx_start(0, steps_x[0])
-
     @pl.loop(0, kv_heads * TILES)
     def _(item):
         tile = item // kv_heads
@@ -332,7 +352,7 @@
         def _(i):
             key_piece(item, kl_ref, 0, blk(i, 2 * tq), False)
 
-        @pl.when(lax.rem(tile, 2) == 1)
+        @pl.when(parity(tile) == 1)
         def _():
             key_piece(item, kl_ref, 0, blk(tile - 1, tq), False)
 
@@ -340,7 +360,6 @@
         ox_copy(j, f_x).wait_recv()
         oy_copy(j, flag).start()
         od_copy(1 + j, wo_out.at[f_x, o_span(flag, j)], f_x, o_span(flag, j)).start()
-    wx_start(1, steps_x[1])
 
     @pl.when(flag == 1)
     def _():
@@ -388,15 +407,21 @@
         od_copy(1 + j, wo_out.at[f_x, o_span(flag, j)], f_diag, o_span(flag, j)).wait_recv()
         od_copy(1 + O_PIECES + j, wo_out.at[f_x, o_span(1 - flag, j)], f_diag, o_span(1 - flag, j)).wait_recv()
 
-    third = n_line * last // 2 - sum(steps_x)
-    zw_copy(n_line - third, lax.rem(z + third, n_line)).wait_recv()
-    for k in range(1, n_line):
-        zw_copy(k, z).wait_send()
+    for r in range(3, n_line):
+        zw_tick(r)
+
+    @pl.loop(0, n_line)
+    def _(t):
+        for up in SIDES:
+            @pl.when((t <= z) & (z < last) if up else (t >= z) & (z > 0))
+            def _():
+                zw_copy(up, t).wait_send()
+
     for k, r in enumerate(steps_x):
         wx_copy(k, r, f_x).wait_recv()
         wx_copy(k, r, f).wait_send()
     for j in range(O_EARLY):
-        for up in range(2):
+        for up in SIDES:
             @pl.when(z < last if up else z > 0)
             def _():
                 ot_copy(up, j, z).wait_send()
@@ -443,7 +468,7 @@
     line = pltpu.VMEM((items, 1, wide), F32)
     own, pair, trio = DMA(()), DMA((2,)), DMA((n_fsdp - 1,))
     early = DMA((2, O_EARLY))
-    w_link, w_side, o_link, o_core, z_link = DMA((PIECES,)), DMA((2, PIECES)), DMA((O_PIECES,)), DMA((1 + 2 * O_PIECES,)), DMA((n_line - 1,))
+    w_link, w_side, o_link, o_core = DMA((PIECES,)), DMA((2, PIECES)), DMA((O_PIECES,)), DMA((1 + 2 * O_PIECES,))
     return pl.pallas_call(
         functools.partial(front_kernel, group, n_line),
         in_specs=[ANY] + [VMEM] * 5,
@@ -460,7 +485,7 @@
             line,
             line,
             pltpu.VMEM((items, head_dim, wide), F32),
-        ] + [pair, trio, trio, own, own, w_link, w_link, w_link, w_link, w_side, w_side, pair, pair, o_link, o_link, o_link, o_link, o_core, o_core, z_link, z_link, pair, pair, early, early, DMA((4,))],
+        ] + [pair, trio, trio, own, own, w_link, w_link, w_link, w_link, w_side, w_side, pair, pair, o_link, o_link, o_link, o_link, o_core, o_core, DMA((2, n_line)), DMA((n_line,)), pair, pair, early, early, DMA((4,))],
         compiler_params=params(cid),
         name="front",
     )(hidden, gain, w_qkv, w_out, cosines, sines)
@@ -487,7 +512,7 @@
     keep.start()
 
     def ct_load(tile):
-        slot = lax.rem(tile, 2)
+        slot = parity(tile)
         return pltpu.make_async_copy(ct_ref.at[blk(tile, tq)], ctb_ref.at[slot], ct_sem.at[slot])
 
     ct_load(0).start()
@@ -587,7 +612,7 @@
 
     def do_tile(tile):
         ct_load(tile).wait()
-        slot = lax.rem(tile, 2)
+        slot = parity(tile)
         total = sum(dot(ctb_ref[slot, :, blk(k, part)], w_ref[k], NT) for k in range(n_parts))
         do_ref[tile_rows(tile), :] = total.astype(BF)
 
@@ -632,7 +657,7 @@
         def _(i):
             piece(kl_ref, vl_ref, dkl_ref, dvl_ref, 0, blk(i, 2 * tq), False)
 
-        @pl.when(lax.rem(tile, 2) == 1)
+        @pl.when(parity(tile) == 1)
         def _():
             piece(kl_ref, vl_ref, dkl_ref, dvl_ref, 0, blk(tile - 1, tq), False)
 
@@ -684,7 +709,7 @@
         def _():
             bwd_item(item - TILES)
 
-        @pl.when((lax.rem(item, 2) == 1) & (item > 1))
+        @pl.when((parity(item) == 1) & (item > 1))
         def _():
             o_tick(item // 2 - 1 + O_EARLY)
 
@@ -798,15 +823,16 @@
         chunk = step - self.dist(side)
         return chunk, (chunk >= 0) & (chunk < self.chunks)
 
+    def prepare(self, step):
+        for side in SIDES:
+            chunk, ok = self.live(side, step)
+
+            @pl.when(ok & (lax.rem(chunk, self.per_block) == 0))
+            def _():
+                self.fill(self.pbuf.at[side], blk((side * self.chunks + chunk) // self.per_block, self.block))
+
     def tick(self, step):
-        for side in range(2):
-            chunk, ok = self.live(side, step)
-
-            @pl.when(ok & (lax.rem(chunk, self.per_block) == 0))
-            def _():
-                self.fill(self.pbuf.at[side], blk((side * self.chunks + chunk) // self.per_block, self.block))
-
-        for side in range(2):
+        for side in SIDES:
             chunk, ok = self.live(side, step)
             dist = self.dist(side)
             part = blk(lax.rem(jnp.maximum(chunk, 0), self.per_block), self.rows)
@@ -828,8 +854,10 @@
             def _():
                 self.finish(chunk, self.buf[side, chunk])
 
+        self.prepare(step + 1)
+
     def drain(self):
-        for side in range(2):
+        for side in SIDES:
             @pl.when(self.dist(side) < self.last)
             def _():
                 @pl.loop(0, self.chunks)
@@ -855,16 +883,16 @@
         return blk(own_base + chunk, rows)
 
     def f_loads(chunk):
-        slot = lax.rem(chunk, 2)
+        slot = parity(chunk)
         return copy(hid_ref.at[own_span(chunk)], fb_in.at[slot], f_sem.at[slot]), copy(ct_ref.at[own_span(chunk)], fb_ct.at[slot], ct_sem.at[slot])
 
     def f_store(chunk):
-        slot = lax.rem(chunk, 2)
+        slot = parity(chunk)
         return copy(fb_out.at[slot], out_ref.at[own_span(chunk)], fo_sem.at[slot])
 
     @pl.when(owner)
     def _():
-        for chunk in range(2):
+        for chunk in SIDES:
             for load in f_loads(chunk):
                 load.start()
 
@@ -872,7 +900,7 @@
     meet([to_core, to_x, to_y] + others("tp", z, n_line) + [{"fsdp": f_diag}])
 
     def finish(chunk, total):
-        slot = lax.rem(chunk, 2)
+        slot = parity(chunk)
         for load in f_loads(chunk):
             load.wait()
 
@@ -931,7 +959,7 @@
         up = z - 1 if side else z + 1
         return remote(out_ref.at[span], out_ref.at[span], out_send.at[side, chunk], out_recv.at[side, chunk], {"tp": jnp.clip(up, 0, last)})
 
-    ends = [(end, z == (last if end else 0)) for end in range(2)]
+    ends = [(end, z == (last if end else 0)) for end in SIDES]
 
     def owner_send(first, stop):
         for end, here in ends:
@@ -942,7 +970,7 @@
                     hop(end, c).start()
 
     def pass_on(step):
-        for side in range(2):
+        for side in SIDES:
             chunk = step - (last - 1 - dist(side))
 
             @pl.when((dist(side) < last) & (chunk >= 0) & (chunk < chunks))
@@ -1009,13 +1037,14 @@
         for load in lhs_loads(0):
             load.start()
         w_load.wait()
+        line.prepare(0)
 
         @pl.loop(0, line.steps)
         def _(fine):
             line.tick(fine)
             step = fine // PER_STEP
             whole = lax.rem(fine, PER_STEP) == 0
-            j, odd = step // 2, lax.rem(step, 2)
+            j, odd = step // 2, parity(step)
 
             @pl.when(whole & (odd == 0) & (j > 0) & (j <= GRAD_CHUNKS))
             def _():
@@ -1029,7 +1058,7 @@
             def _():
                 meet_core(j)
 
-            for late in range(2):
+            for late in SIDES:
                 k = (step - FIRST_X - late) * 2 // 5
 
                 @pl.when(whole & (k >= 0) & (k < EARLY) & (step - late == FIRST_X + (5 * k + 1) // 2))
@@ -1081,14 +1110,14 @@
         items = per_part * n_fsdp
 
         def item_loads(item):
-            slot = lax.rem(item, 2)
+            slot = parity(item)
             return copy(wo_all.at[:, item // per_part, :, blk(lax.rem(item, per_part), n_cols)], wbuf.at[slot], wl_sem.at[slot]), copy(hid_ref.at[:, blk(item, n_cols)], hbuf.at[slot], h_sem.at[slot])
 
         def item_store(item):
-            slot = lax.rem(item, 2)
+            slot = parity(item)
             return copy(rbuf.at[slot], blk_ref.at[:, blk(item, n_cols)], r_sem.at[slot])
 
-        for item in range(2):
+        for item in SIDES:
             for load in item_loads(item):
                 load.start()
 
@@ -1101,7 +1130,7 @@
 
 
         def project(item):
-            slot = lax.rem(item, 2)
+            slot = parity(item)
             for load in item_loads(item):
                 load.wait()
 
@@ -1136,16 +1165,16 @@
         def _(step):
             pass_on(step + early)
 
-            @pl.when((lax.rem(step, 3) == 0) & (step // 3 < items))
-            def _():
-                project(step // 3)
+            @pl.when((parity(step) == 0) & (step // 2 < items))
+            def _():
+                project(step // 2)
 
             for k, at in LATE:
                 @pl.when(step == at)
                 def _():
                     meet_x(k)
 
-            for k, at in LATE:
+            for k, at in ((EARLY - 1, -1),) + LATE:
                 @pl.when(step == at + 1)
                 def _():
                     send_y(k)
@@ -1165,7 +1194,7 @@
     for k in range(n_fsdp):
         gt[k] = gs[:, blk(k, feat)] + gb[:, blk(k, feat)]
     gc[f] = gt[f]
-    for side in range(2):
+    for side in SIDES:
         @pl.when(dist(side) > 0)
         def _():
             @pl.loop(0, chunks)

time: 742 us -> 670 us (0.903)
  Pallas kernels: 730 us -> 658 us
    pallas_call x1, Pallas kernels: 454 us -> 390 us  [close(): pl.pallas_call(functools.partial(close_kernel, n_line, n_fsdp), in_specs=...]
    pallas_call x1, Pallas kernels: 126 us -> 115 us  [front(): pl.pallas_call(functools.partial(front_kernel, group, n_line), in_specs=[...]
where the time goes in v3:
time: 670 us; the launch traced here: 669 us
  Pallas kernels  658 us (98%)
  other arithmetic  7.12 us (1%)
    pallas_call x1, Pallas kernels, close(): pl.pallas_call(functools.partial(close_kernel, n_line, n_fsdp), in_specs=...  390 us
    pallas_call x1, Pallas kernels, attn_back(): pl.pallas_call(functools.partial(back_kernel, n_line, group), in_specs=[V...  132 us
    pallas_call x1, Pallas kernels, front(): pl.pallas_call(functools.partial(front_kernel, group, n_line), in_specs=[...  115 us
    pallas_call x1, Pallas kernels, tail(): pl.pallas_call(functools.partial(tail_kernel, head_dim), grid=(GRAD_CHUNK...  21.1 us

profile of v3, /device:TPU:0, one launch (start us, length us, event | category | flops | bytes accessed | tf_op | source)
XLA Modules:
  0.0 668.8 jit_solution(3530981798831465538)
XLA Ops:
  0.6 0.0 copy-start
  0.7 0.8 convert_element_type.11
  1.5 1.3 broadcast_in_dim.17
  2.8 1.4 copy_bitcast_fusion.1
  4.1 1.9 fusion
  6.0 1.3 pad_maximum_fusion.1
  7.3 0.0 copy-done
  7.3 0.6 copy.23
  8.0 1.8 pad_maximum_fusion.w_ref
  9.8 114.6 %front.1 = (bf16[1024,1024]{1,0:T(8,128)(2,1)}, bf16[1024,1024]{1,0:T(8,128)(2,1)}, f32[8,1,1024]{2,1,0:T(1,128)}, bf16[1024,256]{1,0:T(8,128)(2,1)}, bf16[1024,...) custom-call(bf16[1024,4096]{1,0:T(8,128)(2,1)} %bitcast.20, ...), custom_call_target="tpu_custom_call" | custom-call | tf_op jit(solution)/shard_map/front/pallas_call | solution.py:472
  124.4 131.6 %attn_back.1 = (bf16[1024,1536]{1,0:T(8,128)(2,1)}, bf16[4,1024,1024]{2,1,0:T(8,128)(2,1)}, bf16[4,4,1024,1024]{3,2,1,0:T(8,128)(2,1)}) custom-call(bf16[1024,1024]{1,0:T(8,128)(2,1)} %get-tuple-element.33.o_ref, bf16[1024,1024]{1,0:T(8,128)(2,1)} %get-tuple-element.34.q_ref, ...), custom_call_target="tpu_custom_call", output_to_operand_aliasing={{2}: (9, {}), {1}: (10, {})} | custom-call | tf_op jit(solution)/shard_map/attn_back/pallas_call | solution.py:778
  256.1 390.4 %close.1 = (bf16[1024,4096]{1,0:T(8,128)(2,1)}, bf16[1024,4096]{1,0:T(8,128)(2,1)}, f32[1,1024]{1,0:T(1,128)}, f32[1024,2560]{1,0:T(8,128)}, f32[1024,2560]{1,0:...) custom-call(bf16[1024,1536]{1,0:T(8,128)(2,1)} %get-tuple-element.42.d_, ...), custom_call_target="tpu_custom_call" | custom-call | tf_op jit(solution)/shard_map/close/pallas_call | solution.py:1240
  646.4 21.1 %tail.1 = (bf16[1024,4096]{1,0:T(8,128)(2,1)}, bf16[1024,4096]{1,0:T(8,128)(2,1)}, f32[1024,8,128]{2,1,0:T(8,128)}, f32[1024,2,128]{2,1,0:T(2,128)}, f32[1024,2,128]{2,1,0:T(2,128)}, /*index=5*/f32[1024,1024]{1,0:T(8,128)}) custom-call(bf16[1024,4096]{1,0:T(8,128)(2,1)} %get-tuple-element.48.blk_ref, bf16[1024,4096]{1,0:T(8,128)(2,1)} %get-tuple-element.49.hid_ref, ...), custom_call_target="tpu_custom_call" | custom-call | tf_op jit(solution)/shard_map/tail/pallas_call | solution.py:1290
  667.6 1.3 copy.27
  (1 shorter events, 0.0 us)
Async XLA Ops:
  0.6 6.7 %copy-start = (bf16[1024,8,128]{2,1,0:T(8,128)(2,1)S(1)}, bf16[1024,8,128]{2,1,0:T(8,128)(2,1)}, u32[]{:S(2)}) copy-start(bf16[1024,8,128]{2,1,0:T(8,128)(2,1)} %param.12) | copy-start | bytes 6291460

commit v4 on v3

--- a/solution.py
+++ b/solution.py
@@ -16,6 +16,7 @@
 TILES = 4
 CHUNKS = 16
 PER_STEP = 1
+LEAD = 2
 PIECES = 4
 O_PIECES = 2
 O_EARLY = 2
@@ -200,22 +201,20 @@
         where = jnp.minimum(z + 1, last) if up else jnp.maximum(z - 1, 0)
         return remote(src, o_all.at[owner, blk(j, tq)], ot_send.at[up, j], ot_recv.at[up, j], {"tp": where})
 
+    gains = [(k, where, where["fsdp"]) for k, where in enumerate((to_core, to_x, to_diag))]
+    for k, where, _ in gains:
+        g_copy(k, where, f).start()
+    sends = [x_copy(j) for j in range(PIECES)] + [ox_copy(j, f) for j in range(O_PIECES)]
+    for j in range(LEAD):
+        sends[j].start()
+    own_copy(f).start()
+    all_rows = pl.ds(0, o_rows)
     steps_x = nearest(z, last)
     for up in SIDES:
         @pl.when(z < last if up else z > 0)
         def _():
             zw_copy(up, z).start()
 
-    gains = [(k, where, where["fsdp"]) for k, where in enumerate((to_core, to_x, to_diag))]
-    for k, where, _ in gains:
-        g_copy(k, where, f).start()
-    for j in range(PIECES):
-        x_copy(j).start()
-    own_copy(f).start()
-    for j in range(O_PIECES):
-        ox_copy(j, f).start()
-    all_rows = pl.ds(0, o_rows)
-    od_copy(0, wo_ref, f, all_rows).start()
     local_w = pltpu.make_async_copy(w_ref, wbuf.at[f], out_sem.at[0])
     local_w.start()
     local_o = pltpu.make_async_copy(wo_ref, wo_out.at[f], out_sem.at[1])
@@ -254,6 +253,7 @@
         x_in(j).wait_recv()
         y_copy(j, flag).start()
         d_copy(j, flag, f_x).start()
+        sends[j + LEAD].start()
 
     def y_tick(j):
         y_copy(j, far).wait_recv()
@@ -263,11 +263,11 @@
     project(f, 0, feat, first=True)
     x_tick(0)
     own_copy(f_core).wait_recv()
+    od_copy(0, wo_ref, f, all_rows).start()
     project(f_core, 0, feat)
     x_tick(1)
     y_tick(0)
     zw_tick(1)
-    wx_copy(0, steps_x[0], f).start()
     x_tick(2)
     y_tick(1)
     x_tick(3)
@@ -284,7 +284,7 @@
     project(f_x, second_half, half)
     project(f_diag, second_half, half)
     zw_tick(2)
-    wx_copy(1, steps_x[1], f).start()
+    wx_copy(0, steps_x[0], f).start()
     put_w = pltpu.make_async_copy(wbuf, w_out, out_sem.at[3])
     put_w.start()
 
@@ -360,6 +360,8 @@
         ox_copy(j, f_x).wait_recv()
         oy_copy(j, flag).start()
         od_copy(1 + j, wo_out.at[f_x, o_span(flag, j)], f_x, o_span(flag, j)).start()
+
+    wx_copy(1, steps_x[1], f).start()
 
     @pl.when(flag == 1)
     def _():
@@ -554,23 +556,26 @@
         def _():
             o_up(z, j, o_ref.at[tile_rows(j)]).start()
 
-    for j in range(O_EARLY):
+    def o_early(j):
         @pl.when((z > 0) & (z < last))
         def _():
             o_down(z + 1, j, o_all.at[z + 1, tile_rows(j)]).start()
             o_up(z - 1, j, o_all.at[z - 1, tile_rows(j)]).start()
 
+    o_early(0)
     steps_x = nearest(z, last)
     third = n_line * last // 2 - sum(steps_x)
     x_copy(third, flag, f).start()
-    for r in steps_x:
-        cx_copy(r, flag, f_x).start()
-    for r in range(1, n_line):
+    for r in range(1, n_line - 1):
         y_copy(r, flag).start()
-        c_copy(r, flag, f).start()
 
     def o_tick(k):
         r, j = k // TILES + 1, lax.rem(k, TILES)
+
+        @pl.when(k == O_EARLY)
+        def _():
+            for early in range(1, O_EARLY):
+                o_early(early)
 
         @pl.when(z + r <= last)
         def _():
@@ -593,7 +598,12 @@
     def y_tick(r):
         y_copy(r, far).wait_recv()
         x_copy(r, far, f).start()
-        c_copy(r, far, f).start()
+        for side in (flag, far):
+            c_copy(r, side, f).start()
+        if r == 1:
+            y_copy(n_line - 1, flag).start()
+        if r < n_line - 1:
+            cx_copy(steps_x[r - 1], flag, f_x).start()
 
     def x_tick(q):
         r, side = (q, far) if q else (third, flag)
@@ -1067,8 +1077,7 @@
 
             @pl.when(fine >= chunks)
             def _():
-                ready = fine - last - 1
-                owner_send(jnp.where(fine == chunks, 0, ready - 1), ready)
+                owner_send((fine - chunks) * LEAD, (fine - chunks + 1) * LEAD)
 
             @pl.when(fine > chunks)
             def _():
@@ -1080,7 +1089,6 @@
             for chunk in range(chunks - 2, chunks):
                 f_store(chunk).wait()
 
-        owner_send(chunks - 2, chunks)
         line.drain()
 
     pl.run_scoped(
@@ -1163,6 +1171,8 @@
 
         @pl.loop(0, steps - early)
         def _(step):
+            sent = step + last * LEAD
+            owner_send(sent, jnp.minimum(sent + 1, chunks))
             pass_on(step + early)
 
             @pl.when((parity(step) == 0) & (step // 2 < items))

time: 670 us -> 618 us (0.922)
  Pallas kernels: 658 us -> 606 us
    pallas_call x1, Pallas kernels: 390 us -> 339 us  [close(): pl.pallas_call(functools.partial(close_kernel, n_line, n_fsdp), in_specs=...]
where the time goes in v4:
time: 618 us; the launch traced here: 617 us
  Pallas kernels  606 us (98%)
  other arithmetic  7.12 us (1%)
    pallas_call x1, Pallas kernels, close(): pl.pallas_call(functools.partial(close_kernel, n_line, n_fsdp), in_specs=...  339 us
    pallas_call x1, Pallas kernels, attn_back(): pl.pallas_call(functools.partial(back_kernel, n_line, group), in_specs=[V...  132 us
    pallas_call x1, Pallas kernels, front(): pl.pallas_call(functools.partial(front_kernel, group, n_line), in_specs=[...  115 us
    pallas_call x1, Pallas kernels, tail(): pl.pallas_call(functools.partial(tail_kernel, head_dim), grid=(GRAD_CHUNK...  21.1 us

profile of v4, /device:TPU:0, one launch (start us, length us, event | category | flops | bytes accessed | tf_op | source)
XLA Modules:
  0.0 617.4 jit_solution(12632823657319857185)
XLA Ops:
  0.6 0.0 copy-start
  0.7 0.8 convert_element_type.11
  1.5 1.3 broadcast_in_dim.17
  2.8 1.4 copy_bitcast_fusion.1
  4.1 1.9 fusion
  6.0 1.3 pad_maximum_fusion.1
  7.3 0.0 copy-done
  7.3 0.6 copy.23
  8.0 1.8 pad_maximum_fusion.w_ref
  9.8 114.6 %front.1 = (bf16[1024,1024]{1,0:T(8,128)(2,1)}, bf16[1024,1024]{1,0:T(8,128)(2,1)}, f32[8,1,1024]{2,1,0:T(1,128)}, bf16[1024,256]{1,0:T(8,128)(2,1)}, bf16[1024,...) custom-call(bf16[1024,4096]{1,0:T(8,128)(2,1)} %bitcast.20, ...), custom_call_target="tpu_custom_call" | custom-call | tf_op jit(solution)/shard_map/front/pallas_call | solution.py:474
  124.4 131.7 %attn_back.1 = (bf16[1024,1536]{1,0:T(8,128)(2,1)}, bf16[4,1024,1024]{2,1,0:T(8,128)(2,1)}, bf16[4,4,1024,1024]{3,2,1,0:T(8,128)(2,1)}) custom-call(bf16[1024,1024]{1,0:T(8,128)(2,1)} %get-tuple-element.33.o_ref, bf16[1024,1024]{1,0:T(8,128)(2,1)} %get-tuple-element.34.q_ref, ...), custom_call_target="tpu_custom_call", output_to_operand_aliasing={{2}: (9, {}), {1}: (10, {})} | custom-call | tf_op jit(solution)/shard_map/attn_back/pallas_call | solution.py:788
  256.1 338.9 %close.1 = (bf16[1024,4096]{1,0:T(8,128)(2,1)}, bf16[1024,4096]{1,0:T(8,128)(2,1)}, f32[1,1024]{1,0:T(1,128)}, f32[1024,2560]{1,0:T(8,128)}, f32[1024,2560]{1,0:...) custom-call(bf16[1024,1536]{1,0:T(8,128)(2,1)} %get-tuple-element.42.d_, ...), custom_call_target="tpu_custom_call" | custom-call | tf_op jit(solution)/shard_map/close/pallas_call | solution.py:1250
  595.0 21.1 %tail.1 = (bf16[1024,4096]{1,0:T(8,128)(2,1)}, bf16[1024,4096]{1,0:T(8,128)(2,1)}, f32[1024,8,128]{2,1,0:T(8,128)}, f32[1024,2,128]{2,1,0:T(2,128)}, f32[1024,2,128]{2,1,0:T(2,128)}, /*index=5*/f32[1024,1024]{1,0:T(8,128)}) custom-call(bf16[1024,4096]{1,0:T(8,128)(2,1)} %get-tuple-element.48.blk_ref, bf16[1024,4096]{1,0:T(8,128)(2,1)} %get-tuple-element.49.hid_ref, ...), custom_call_target="tpu_custom_call" | custom-call | tf_op jit(solution)/shard_map/tail/pallas_call | solution.py:1300
  616.1 1.3 copy.27
  (1 shorter events, 0.0 us)
Async XLA Ops:
  0.6 6.7 %copy-start = (bf16[1024,8,128]{2,1,0:T(8,128)(2,1)S(1)}, bf16[1024,8,128]{2,1,0:T(8,128)(2,1)}, u32[]{:S(2)}) copy-start(bf16[1024,8,128]{2,1,0:T(8,128)(2,1)} %param.12) | copy-start | bytes 6291460

commit v5 on v4

--- a/solution.py
+++ b/solution.py
@@ -17,9 +17,8 @@
 CHUNKS = 16
 PER_STEP = 1
 LEAD = 2
-PIECES = 4
+PIECES = 8
 O_PIECES = 2
-O_EARLY = 2
 GRAD_CHUNKS = 8
 FIRST_X = 5
 EARLY = 6
@@ -111,15 +110,16 @@
     return jnp.concatenate([cosines, cosines], axis=1), jnp.concatenate([-sines, sines], axis=1)
 
 
-def front_kernel(group, n_line, hid_ref, gain_ref, w_ref, wo_ref, cos_ref, sin_ref, o_ref, qr_ref, lse_ref, kl_ref, vl_ref, kp_ref, vp_ref, gfull_ref, n_out, w_out, wo_all, o_all, wbuf, nbuf, acc, hbuf, gbuf, qs, vt, m_all, l_all, acc_all, h_sem, g_send, g_recv, own_send, own_recv, x_send, x_recv, y_send, y_recv, d_send, d_recv, kv_send, kv_recv, ox_send, ox_recv, oy_send, oy_recv, od_send, od_recv, zw_send, zw_recv, wx_send, wx_recv, ot_send, ot_recv, out_sem):
+def core_kernel(group, n_line, hid_ref, gain_ref, w_ref, wo_ref, cos_ref, sin_ref, ct_ref, d_ref, o_ref, gfull_ref, n_out, w_out, wo_all, o_all, wbuf, nbuf, acc, hbuf, gbuf, qs, vt, m_all, l_all, acc_all, q_ref, lse_ref, kl_ref, vl_ref, kp_ref, vp_ref, do_ref, dkl_ref, dvl_ref, dkp_ref, dvp_ref, qs_ref, dos_ref, delta_ref, kt_ref, dqt_ref, h_sem, g_send, g_recv, own_send, own_recv, x_send, x_recv, y_send, y_recv, d_send, d_recv, kv_send, kv_recv, ox_send, ox_recv, oy_send, oy_recv, od_send, od_recv, zw_send, zw_recv, out_sem, ct_sem, on_send, ou_send, o_recv, wy_send, wy_recv, wx_send, wx_recv, wc_send, wc_recv, cx_send, cx_recv, dk_send, dk_recv):
     q_len, feat = hid_ref.shape[0], w_ref.shape[0]
     head_dim = cos_ref.shape[1]
     half_dim = head_dim // 2
     kv_width = kl_ref.shape[1]
     kv_heads = kv_width // head_dim
-    q_width = qr_ref.shape[1]
+    q_width = q_ref.shape[1]
     tq = q_len // TILES
     wide = group * tq
+    score_scale = head_dim ** -0.5
     scale = head_dim ** -0.5 * LOG2E
     half = feat // 2
     piece = half // PIECES
@@ -192,14 +192,75 @@
             def _():
                 zw_copy(up, at).start()
 
-    def wx_copy(k, r, slot):
-        spot = wo_all.at[lax.rem(z + r, n_line), slot, blk(flag, o_half)]
-        return remote(spot, spot, wx_send.at[k], wx_recv.at[k], to_x)
-
-    def ot_copy(up, j, owner):
-        src = o_ref.at[blk(j, tq)]
-        where = jnp.minimum(z + 1, last) if up else jnp.maximum(z - 1, 0)
-        return remote(src, o_all.at[owner, blk(j, tq)], ot_send.at[up, j], ot_recv.at[up, j], {"tp": where})
+    def tile_rows(j):
+        return blk(j, tq)
+
+    def o_down(t, j, src):
+        return remote(src, o_all.at[t, tile_rows(j)], on_send.at[t, j], o_recv.at[t, j], {"tp": jnp.maximum(z - 1, 0)})
+
+    def o_up(t, j, src):
+        return remote(src, o_all.at[t, tile_rows(j)], ou_send.at[t, j], o_recv.at[t, j], {"tp": jnp.minimum(z + 1, last)})
+
+    def wo_half(r, slot, side):
+        return wo_all.at[lax.rem(z + r, n_line), slot, blk(side, o_half)]
+
+    def wy_copy(r, side):
+        return remote(wo_half(r, f, side), wo_half(r, f, side), wy_send.at[r - 1], wy_recv.at[r - 1], to_y)
+
+    def wx_copy(r, side, slot):
+        return remote(wo_half(r, slot, side), wo_half(r, slot, side), wx_send.at[side, r - 1], wx_recv.at[side, r - 1], to_x)
+
+    def wc_copy(r, side, slot):
+        return remote(wo_half(r, slot, side), wo_half(r, slot, side), wc_send.at[side, r - 1], wc_recv.at[side, r - 1], to_core)
+
+    def cx_copy(r, side, slot):
+        return remote(wo_half(r, slot, side), wo_half(r, slot, side), cx_send.at[side, r - 1], cx_recv.at[side, r - 1], to_core)
+
+    def o_tick(k):
+        r, j = k // TILES + 1, lax.rem(k, TILES)
+
+        @pl.when(z + r <= last)
+        def _():
+            t = jnp.minimum(z + r, last)
+            o_down(t, j, o_all.at[t, tile_rows(j)]).wait_recv()
+
+            @pl.when(z > 0)
+            def _():
+                o_down(t, j, o_all.at[t, tile_rows(j)]).start()
+
+        @pl.when(z - r >= 0)
+        def _():
+            t = jnp.maximum(z - r, 0)
+            o_up(t, j, o_all.at[t, tile_rows(j)]).wait_recv()
+
+            @pl.when(z < last)
+            def _():
+                o_up(t, j, o_all.at[t, tile_rows(j)]).start()
+
+    def wy_tick(r):
+        wy_copy(r, far).wait_recv()
+        wx_copy(r, far, f).start()
+        for side in (flag, far):
+            wc_copy(r, side, f).start()
+        if r == 1:
+            wy_copy(last, flag).start()
+
+    near, second = nearest(z, last)
+    own_order = (near, second, n_line * last // 2 - near - second)
+
+    def wx_tick(q):
+        r, side = (own_order[q], flag) if q < last else (q - last + 1, far)
+        wx_copy(r, side, f_x).wait_recv()
+        cx_copy(r, side, f_x).start()
+
+    def o_send(j):
+        @pl.when(z > 0)
+        def _():
+            o_down(z, j, o_ref.at[tile_rows(j)]).start()
+
+        @pl.when(z < last)
+        def _():
+            o_up(z, j, o_ref.at[tile_rows(j)]).start()
 
     gains = [(k, where, where["fsdp"]) for k, where in enumerate((to_core, to_x, to_diag))]
     for k, where, _ in gains:
@@ -209,7 +270,6 @@
         sends[j].start()
     own_copy(f).start()
     all_rows = pl.ds(0, o_rows)
-    steps_x = nearest(z, last)
     for up in SIDES:
         @pl.when(z < last if up else z > 0)
         def _():
@@ -237,7 +297,7 @@
 
         if tile + 2 < TILES:
             h_load(tile + 2).start()
-    put_n = pltpu.make_async_copy(nbuf, n_out, out_sem.at[2])
+    put_n = pltpu.make_async_copy(nbuf.at[pl.ds(0, q_len)], n_out, out_sem.at[2])
     put_n.start()
 
     def project(slot, start, rows, first=False):
@@ -262,29 +322,29 @@
     local_w.wait()
     project(f, 0, feat, first=True)
     x_tick(0)
+    x_tick(1)
     own_copy(f_core).wait_recv()
     od_copy(0, wo_ref, f, all_rows).start()
     project(f_core, 0, feat)
-    x_tick(1)
-    y_tick(0)
-    zw_tick(1)
-    x_tick(2)
-    y_tick(1)
-    x_tick(3)
+    for j in range(2, PIECES):
+        x_tick(j)
+        y_tick(j - 2)
+        if j == PIECES // 2:
+            zw_tick(1)
     for j in range(PIECES):
         d_copy(j, flag, f_diag).wait_recv()
     first_half = pl.multiple_of(flag * half, half)
     project(f_x, first_half, half)
-    y_tick(2)
+    y_tick(PIECES - 2)
     project(f_diag, first_half, half)
-    y_tick(3)
+    y_tick(PIECES - 1)
     for j in range(PIECES):
-        d_copy(j, 1 - flag, f_diag).wait_recv()
+        d_copy(j, far, f_diag).wait_recv()
     second_half = pl.multiple_of(far * half, half)
     project(f_x, second_half, half)
     project(f_diag, second_half, half)
     zw_tick(2)
-    wx_copy(0, steps_x[0], f).start()
+    wx_copy(near, flag, f).start()
     put_w = pltpu.make_async_copy(wbuf, w_out, out_sem.at[3])
     put_w.start()
 
@@ -299,8 +359,16 @@
 
     kv_pairs = ((kl_ref, kp_ref), (vl_ref, vp_ref))
 
-    def kv_copy(k):
-        return remote(kv_pairs[k][0], kv_pairs[k][1], kv_send.at[k], kv_recv.at[k], {"cp": 1})
+    def kv_copies(g):
+        return [remote(src.at[:, blk(g, head_dim)], dst.at[:, blk(g, head_dim)], kv_send.at[k, g], kv_recv.at[k, g], {"cp": 1}) for k, (src, dst) in enumerate(kv_pairs)]
+
+    @pl.when(flag == 0)
+    def _():
+        zero(kp_ref)
+        zero(vp_ref)
+        for g in range(kv_heads):
+            for copy in kv_copies(g):
+                copy.start()
 
     @pl.loop(0, TILES)
     def _(tile):
@@ -308,23 +376,16 @@
         cos, sin = cos_ref[here, :], sin_ref[here, :]
         for h in range(group * kv_heads):
             cols = blk(h, head_dim)
-            qr_ref[here, cols] = rope(acc[here, cols], cos, sin, half_dim).astype(BF)
-
-    @pl.when(flag == 0)
-    def _():
-        zero(kp_ref)
-        zero(vp_ref)
-        for k in range(len(kv_pairs)):
-            kv_copy(k).start()
+            q_ref[here, cols] = rope(acc[here, cols], cos, sin, half_dim).astype(BF)
 
     def load_q(item):
-        g, tile = lax.rem(item, kv_heads), item // kv_heads
+        g, tile = item // TILES, lax.rem(item, TILES)
         rows = blk(tile, tq)
         for h in range(group):
-            qs[:, blk(h, tq)] = qr_ref[rows, blk(g * group + h, head_dim)].T
+            qs[:, blk(h, tq)] = q_ref[rows, blk(g * group + h, head_dim)].T
 
     def key_piece(item, k_ref, side, start, masked):
-        g = lax.rem(item, kv_heads)
+        g = item // TILES
         scores = dot(k_ref[start, blk(g, head_dim)], qs[...], NN)
         if masked:
             scores = causal(scores, tq)
@@ -341,7 +402,7 @@
 
     @pl.loop(0, kv_heads * TILES)
     def _(item):
-        tile = item // kv_heads
+        tile = lax.rem(item, TILES)
         load_q(item)
         m_all[item] = jnp.full_like(m_all[item], NEG_BIG)
         l_all[item] = jnp.zeros_like(l_all[item])
@@ -361,19 +422,19 @@
         oy_copy(j, flag).start()
         od_copy(1 + j, wo_out.at[f_x, o_span(flag, j)], f_x, o_span(flag, j)).start()
 
-    wx_copy(1, steps_x[1], f).start()
-
-    @pl.when(flag == 1)
-    def _():
-        for k in range(len(kv_pairs)):
-            kv_copy(k).wait_recv()
-        for g in range(kv_heads):
-            vt[g, 1] = vp_ref[:, blk(g, head_dim)].T
+    wx_copy(second, flag, f).start()
+    zw_tick(last)
 
     @pl.loop(0, kv_heads * TILES)
     def _(item):
-        g, tile = lax.rem(item, kv_heads), item // kv_heads
+        g, tile = item // TILES, lax.rem(item, TILES)
         rows = blk(tile, tq)
+
+        @pl.when((flag == 1) & (tile == 0))
+        def _():
+            for copy in kv_copies(g):
+                copy.wait_recv()
+            vt[g, 1] = vp_ref[:, blk(g, head_dim)].T
 
         @pl.when(flag == 1)
         def _():
@@ -384,19 +445,16 @@
             key_piece(item, kp_ref, 1, blk(i, 2 * tq), False)
 
         total = l_all[item]
-        lse_ref[g * TILES + tile] = m_all[item] * scale + jnp.log2(total)
+        lse_ref[item] = m_all[item] * scale + jnp.log2(total)
         out_t = acc_all[item] / total
         for h in range(group):
             o_ref[rows, blk(g * group + h, head_dim)] = out_t[:, h * tq:h * tq + tq].T.astype(BF)
 
-        for j in range(O_EARLY):
-            @pl.when((item == (j + 1) * kv_heads) & (z > 0))
-            def _():
-                ot_copy(0, j, z).start()
-
-            @pl.when((item == (j + 1) * kv_heads) & (z < last))
-            def _():
-                ot_copy(1, j, z).start()
+        ready = item - TILES * (kv_heads - 1) - 1
+
+        @pl.when(ready >= 0)
+        def _():
+            o_send(ready)
 
         for j in range(O_PIECES):
             @pl.when(item == (j + 1) * kv_heads * TILES // O_PIECES - 1)
@@ -404,13 +462,170 @@
                 oy_copy(j, far).wait_recv()
                 od_copy(1 + O_PIECES + j, wo_out.at[f_x, o_span(1 - flag, j)], f_x, o_span(1 - flag, j)).start()
 
+    o_send(TILES - 1)
+    wx_copy(own_order[last - 1], flag, f).start()
+    for r in range(1, last):
+        wy_copy(r, flag).start()
     od_copy(0, wo_ref, f_core, all_rows).wait_recv()
     for j in range(O_PIECES):
         od_copy(1 + j, wo_out.at[f_x, o_span(flag, j)], f_diag, o_span(flag, j)).wait_recv()
         od_copy(1 + O_PIECES + j, wo_out.at[f_x, o_span(1 - flag, j)], f_diag, o_span(1 - flag, j)).wait_recv()
 
-    for r in range(3, n_line):
-        zw_tick(r)
+    put_n.wait()
+    local_o.wait()
+    n_parts, _, part = wo_out.shape
+    loads = [pltpu.make_async_copy(wo_out.at[k], nbuf.at[pl.ds(0, o_rows), blk(k, part)], out_sem.at[4 + k]) for k in range(n_parts)]
+    for load in loads:
+        load.start()
+    keep = pltpu.make_async_copy(o_ref, o_all.at[z], out_sem.at[2])
+    keep.start()
+
+    def ct_load(tile):
+        slot = parity(tile)
+        return pltpu.make_async_copy(ct_ref.at[blk(tile, tq)], hbuf.at[slot], ct_sem.at[slot])
+
+    ct_load(0).start()
+    ct_load(1).start()
+    zero(dkl_ref)
+    zero(dvl_ref)
+
+    @pl.when(flag == 1)
+    def _():
+        zero(dkp_ref)
+        zero(dvp_ref)
+
+    wx_tick(0)
+    o_tick(jnp.int32(0))
+    for load in loads:
+        load.wait()
+
+    def do_tile(tile):
+        ct_load(tile).wait()
+        do_ref[tile_rows(tile), :] = dot(hbuf[parity(tile)], nbuf[pl.ds(0, o_rows), :], NT).astype(BF)
+
+        @pl.when(tile + 2 < TILES)
+        def _():
+            ct_load(tile + 2).start()
+
+    def bwd_item(item):
+        g, tile = item // TILES, lax.rem(item, TILES)
+        kv_cols = blk(g, head_dim)
+        rows = blk(tile, tq)
+
+        @pl.when(tile == 0)
+        def _():
+            kt_ref[0] = kl_ref[:, kv_cols].T
+            kt_ref[1] = kp_ref[:, kv_cols].T
+
+        for h in range(group):
+            cols = blk(g * group + h, head_dim)
+            stack = blk(h, tq)
+            qs_ref[stack, :] = q_ref[rows, cols]
+            d_h = do_ref[rows, cols]
+            dos_ref[stack, :] = d_h
+            prod = d_h.astype(F32) * o_ref[rows, cols].astype(F32)
+            delta_ref[:, stack] = row_sum(prod.T)
+        zero(dqt_ref)
+
+        def piece(k_ref, v_ref, dk_ref, dv_ref, side, span, masked):
+            scores = dot(k_ref[span, kv_cols], qs_ref[...], NT)
+            if masked:
+                scores = causal(scores, tq)
+            probs = jnp.exp2(scores * (score_scale * LOG2E) - lse_ref[item])
+            d_probs = dot(v_ref[span, kv_cols], dos_ref[...], NT)
+            d_scores = (probs * (d_probs - delta_ref[...])).astype(BF)
+            dv_ref[g, span, :] += dot(probs.astype(BF), dos_ref[...], NN)
+            dk_ref[g, span, :] += dot(d_scores, qs_ref[...], NN)
+            dqt_ref[...] += dot(kt_ref[side, :, span], d_scores, NN)
+
+        piece(kl_ref, vl_ref, dkl_ref, dvl_ref, 0, blk(tile, tq), True)
+
+        @pl.loop(0, tile // 2)
+        def _(i):
+            piece(kl_ref, vl_ref, dkl_ref, dvl_ref, 0, blk(i, 2 * tq), False)
+
+        @pl.when(parity(tile) == 1)
+        def _():
+            piece(kl_ref, vl_ref, dkl_ref, dvl_ref, 0, blk(tile - 1, tq), False)
+
+        @pl.loop(0, flag * TILES // 2)
+        def _(i):
+            piece(kp_ref, vp_ref, dkp_ref, dvp_ref, 1, blk(i, 2 * tq), False)
+
+        for h in range(group):
+            dq_h = dqt_ref[:, blk(h, tq)].T * score_scale
+            d_ref[rows, blk(g * group + h, head_dim)] = rope(dq_h, cos_ref[rows, :], -sin_ref[rows, :], half_dim).astype(BF)
+
+        @pl.when((tile == TILES - 1) & (flag == 1))
+        def _():
+            for copy in back(g):
+                copy.start()
+
+    def back(g):
+        return [remote(ref.at[g], ref.at[g], dk_send.at[k, g], dk_recv.at[k, g], {"cp": 0}) for k, ref in enumerate((dkp_ref, dvp_ref))]
+
+    def kv_done(g):
+        @pl.when(flag == 0)
+        def _():
+            for copy in back(g):
+                copy.wait_recv()
+            dkl_ref[g] += dkp_ref[g]
+            dvl_ref[g] += dvp_ref[g]
+
+        dk = rope(dkl_ref[g] * score_scale, cos_ref[...], -sin_ref[...], half_dim)
+        k_at = q_width // head_dim + g
+        d_ref[:, blk(k_at, head_dim)] = dk.astype(BF)
+        d_ref[:, blk(k_at + kv_heads, head_dim)] = dvl_ref[g].astype(BF)
+
+        @pl.when(flag == 1)
+        def _():
+            for copy in back(g):
+                copy.wait_send()
+
+    items = TILES * (kv_heads + 1)
+    plan = {1: [(o_tick, 1), (wx_tick, 1)], 4: [(o_tick, 2)], 5: [(wy_tick, 1)], 6: [(o_tick, 3), (wx_tick, 2)], 8: [(o_tick, 4), (wy_tick, 2)], 9: [(o_tick, 5), (wx_tick, 3)], 11: [(o_tick, 6)]}
+
+    def run(tick, arg):
+        tick(jnp.int32(arg) if tick is o_tick else arg)
+
+    @pl.loop(0, items)
+    def _(item):
+        @pl.when(item < TILES)
+        def _():
+            do_tile(item)
+
+        @pl.when(item >= TILES)
+        def _():
+            bwd_item(item - TILES)
+
+        for at, jobs in plan.items():
+            @pl.when(item == at)
+            def _():
+                for tick, arg in jobs:
+                    run(tick, arg)
+
+    for tick, arg in [(wy_tick, 3), (o_tick, 7), (wx_tick, 4), (o_tick, 8), (kv_done, 0), (o_tick, 9), (wx_tick, 5), (o_tick, 10), (kv_done, 1), (o_tick, 11)]:
+        run(tick, arg)
+
+    for r in range(1, n_line):
+        for side in (flag, far):
+            wc_copy(r, side, f_core).wait_recv()
+            cx_copy(r, side, f_diag).wait_recv()
+            wc_copy(r, side, f).wait_send()
+            cx_copy(r, side, f_x).wait_send()
+            wx_copy(r, side, f).wait_send()
+        wy_copy(r, flag).wait_send()
+
+    @pl.loop(0, n_line)
+    def _(t):
+        for j in range(TILES):
+            @pl.when((t >= z) & (z > 0))
+            def _():
+                o_down(t, j, o_all.at[t, tile_rows(j)]).wait_send()
+
+            @pl.when((t <= z) & (z < last))
+            def _():
+                o_up(t, j, o_all.at[t, tile_rows(j)]).wait_send()
 
     @pl.loop(0, n_line)
     def _(t):
@@ -418,16 +633,6 @@
             @pl.when((t <= z) & (z < last) if up else (t >= z) & (z > 0))
             def _():
                 zw_copy(up, t).wait_send()
-
-    for k, r in enumerate(steps_x):
-        wx_copy(k, r, f_x).wait_recv()
-        wx_copy(k, r, f).wait_send()
-    for j in range(O_EARLY):
-        for up in SIDES:
-            @pl.when(z < last if up else z > 0)
-            def _():
-                ot_copy(up, j, z).wait_send()
-                ot_copy(1 - up, j, z + 1 if up else z - 1).wait_recv()
 
     for k, where, _ in gains:
         g_copy(k, where, f).wait_send()
@@ -446,14 +651,15 @@
 
     @pl.when(flag == 0)
     def _():
-        for k in range(len(kv_pairs)):
-            kv_copy(k).wait_send()
-
-    for local in (local_o, put_n, put_w):
+        for g in range(kv_heads):
+            for copy in kv_copies(g):
+                copy.wait_send()
+
+    for local in (keep, put_w):
         local.wait()
 
 
-def front(hidden, gain, w_qkv, w_out, cosines, sines, group, kv_width, n_line, cid):
+def core(hidden, gain, w_qkv, w_out, cosines, sines, cotangent, group, kv_width, n_line, cid):
     q_len, model_dim = hidden.shape
     feat, width = w_qkv.shape
     head_dim = cosines.shape[1]
@@ -465,20 +671,22 @@
     wide = group * tq
     items = kv_heads * TILES
     sds = jax.ShapeDtypeStruct
-    kv = sds((q_len, kv_width), BF)
-    q_like = sds((q_len, q_width), BF)
     line = pltpu.VMEM((items, 1, wide), F32)
+    kv = pltpu.VMEM((q_len, kv_width), BF)
+    heads = pltpu.VMEM((q_len, q_width), BF)
+    sums = pltpu.VMEM((kv_heads, q_len, head_dim), F32)
+    stack = pltpu.VMEM((wide, head_dim), BF)
     own, pair, trio = DMA(()), DMA((2,)), DMA((n_fsdp - 1,))
-    early = DMA((2, O_EARLY))
     w_link, w_side, o_link, o_core = DMA((PIECES,)), DMA((2, PIECES)), DMA((O_PIECES,)), DMA((1 + 2 * O_PIECES,))
+    tiles, hop, side, dkv = DMA((n_line, TILES)), DMA((n_line - 1,)), DMA((2, n_line - 1)), DMA((2, kv_heads))
     return pl.pallas_call(
-        functools.partial(front_kernel, group, n_line),
-        in_specs=[ANY] + [VMEM] * 5,
-        out_specs=[VMEM] * 8 + [ANY] * 4,
-        out_shape=[q_like, q_like, sds((items, 1, wide), F32), kv, kv, kv, kv, sds((1, model_dim), F32), sds((q_len, model_dim), BF), sds((n_fsdp, feat, width), BF), sds((n_line, n_fsdp, o_rows, o_cols), BF), sds((n_line, q_len, q_width), BF)],
+        functools.partial(core_kernel, group, n_line),
+        in_specs=[ANY] + [VMEM] * 5 + [ANY],
+        out_specs=[VMEM] * 3 + [ANY] * 4,
+        out_shape=[sds((q_len, width), BF), sds((q_len, q_width), BF), sds((1, model_dim), F32), sds((q_len, model_dim), BF), sds((n_fsdp, feat, width), BF), sds((n_line, n_fsdp, o_rows, o_cols), BF), sds((n_line, q_len, q_width), BF)],
         scratch_shapes=[
             pltpu.VMEM((n_fsdp, feat, width), BF),
-            pltpu.VMEM((q_len, model_dim), BF),
+            pltpu.VMEM((max(q_len, o_rows), model_dim), BF),
             pltpu.VMEM((q_len, width), F32),
             pltpu.VMEM((2, tq, model_dim), BF),
             pltpu.VMEM((n_fsdp, 1, feat), F32),
@@ -487,324 +695,20 @@
             line,
             line,
             pltpu.VMEM((items, head_dim, wide), F32),
-        ] + [pair, trio, trio, own, own, w_link, w_link, w_link, w_link, w_side, w_side, pair, pair, o_link, o_link, o_link, o_link, o_core, o_core, DMA((2, n_line)), DMA((n_line,)), pair, pair, early, early, DMA((4,))],
-        compiler_params=params(cid),
-        name="front",
-    )(hidden, gain, w_qkv, w_out, cosines, sines)
-
-
-def back_kernel(n_line, group, o_ref, q_ref, lse_ref, cos_ref, sin_ref, kl_ref, vl_ref, kp_ref, vp_ref, _wo_in, _o_in, ct_ref, d_ref, o_all, wo_all, w_ref, ctb_ref, do_ref, dkl_ref, dvl_ref, dkp_ref, dvp_ref, qs_ref, dos_ref, delta_ref, kt_ref, dqt_ref, load_sem, keep_sem, ct_sem, od_send, ou_send, o_recv, y_send, y_recv, x_send, x_recv, c_send, c_recv, cx_send, cx_recv, kv_send, kv_recv):
-    last = n_line - 1
-    z, flag, f = lax.axis_index("tp"), lax.axis_index("cp"), lax.axis_index("fsdp")
-    far = 1 - flag
-    f_core, f_x, f_diag = fsdp_peers(f)
-    q_len, width = o_ref.shape
-    head_dim = cos_ref.shape[1]
-    half_dim = head_dim // 2
-    kv_width = kl_ref.shape[1]
-    kv_heads = kv_width // head_dim
-    tq = q_len // TILES
-    wide = group * tq
-    score_scale = head_dim ** -0.5
-    n_parts, o_rows, part = w_ref.shape
-    o_half = o_rows // 2
-    load = pltpu.make_async_copy(wo_all.at[z], w_ref, load_sem)
-    load.start()
-    keep = pltpu.make_async_copy(o_ref, o_all.at[z], keep_sem)
-    keep.start()
-
-    def ct_load(tile):
-        slot = parity(tile)
-        return pltpu.make_async_copy(ct_ref.at[blk(tile, tq)], ctb_ref.at[slot], ct_sem.at[slot])
-
-    ct_load(0).start()
-    ct_load(1).start()
-
-    to_core, to_x, to_y = {"fsdp": f_core}, {"fsdp": f_x}, {"cp": far}
-    meet([to_core, to_x, to_y] + others("tp", z, n_line))
-
-    def tile_rows(j):
-        return blk(j, tq)
-
-    def o_down(t, j, src):
-        return remote(src, o_all.at[t, tile_rows(j)], od_send.at[t, j], o_recv.at[t, j], {"tp": jnp.maximum(z - 1, 0)})
-
-    def o_up(t, j, src):
-        return remote(src, o_all.at[t, tile_rows(j)], ou_send.at[t, j], o_recv.at[t, j], {"tp": jnp.minimum(z + 1, last)})
-
-    def wo_half(r, slot, side):
-        return wo_all.at[lax.rem(z + r, n_line), slot, blk(side, o_half)]
-
-    def y_copy(r, side):
-        return remote(wo_half(r, f, side), wo_half(r, f, side), y_send.at[r - 1], y_recv.at[r - 1], to_y)
-
-    def x_copy(r, side, slot):
-        return remote(wo_half(r, slot, side), wo_half(r, slot, side), x_send.at[side, r - 1], x_recv.at[side, r - 1], to_x)
-
-    def c_copy(r, side, slot):
-        return remote(wo_half(r, slot, side), wo_half(r, slot, side), c_send.at[side, r - 1], c_recv.at[side, r - 1], to_core)
-
-    def cx_copy(r, side, slot):
-        return remote(wo_half(r, slot, side), wo_half(r, slot, side), cx_send.at[side, r - 1], cx_recv.at[side, r - 1], to_core)
-
-    for j in range(O_EARLY, TILES):
-        @pl.when(z > 0)
-        def _():
-            o_down(z, j, o_ref.at[tile_rows(j)]).start()
-
-        @pl.when(z < last)
-        def _():
-            o_up(z, j, o_ref.at[tile_rows(j)]).start()
-
-    def o_early(j):
-        @pl.when((z > 0) & (z < last))
-        def _():
-            o_down(z + 1, j, o_all.at[z + 1, tile_rows(j)]).start()
-            o_up(z - 1, j, o_all.at[z - 1, tile_rows(j)]).start()
-
-    o_early(0)
-    steps_x = nearest(z, last)
-    third = n_line * last // 2 - sum(steps_x)
-    x_copy(third, flag, f).start()
-    for r in range(1, n_line - 1):
-        y_copy(r, flag).start()
-
-    def o_tick(k):
-        r, j = k // TILES + 1, lax.rem(k, TILES)
-
-        @pl.when(k == O_EARLY)
-        def _():
-            for early in range(1, O_EARLY):
-                o_early(early)
-
-        @pl.when(z + r <= last)
-        def _():
-            t = jnp.minimum(z + r, last)
-            o_down(t, j, o_all.at[t, tile_rows(j)]).wait_recv()
-
-            @pl.when(z > 0)
-            def _():
-                o_down(t, j, o_all.at[t, tile_rows(j)]).start()
-
-        @pl.when(z - r >= 0)
-        def _():
-            t = jnp.maximum(z - r, 0)
-            o_up(t, j, o_all.at[t, tile_rows(j)]).wait_recv()
-
-            @pl.when(z < last)
-            def _():
-                o_up(t, j, o_all.at[t, tile_rows(j)]).start()
-
-    def y_tick(r):
-        y_copy(r, far).wait_recv()
-        x_copy(r, far, f).start()
-        for side in (flag, far):
-            c_copy(r, side, f).start()
-        if r == 1:
-            y_copy(n_line - 1, flag).start()
-        if r < n_line - 1:
-            cx_copy(steps_x[r - 1], flag, f_x).start()
-
-    def x_tick(q):
-        r, side = (q, far) if q else (third, flag)
-        x_copy(r, side, f_x).wait_recv()
-        cx_copy(r, side, f_x).start()
-
-    zero(dkl_ref)
-    zero(dvl_ref)
-
-    @pl.when(flag == 1)
-    def _():
-        zero(dkp_ref)
-        zero(dvp_ref)
-
-    load.wait()
-
-    def do_tile(tile):
-        ct_load(tile).wait()
-        slot = parity(tile)
-        total = sum(dot(ctb_ref[slot, :, blk(k, part)], w_ref[k], NT) for k in range(n_parts))
-        do_ref[tile_rows(tile), :] = total.astype(BF)
-
-        @pl.when(tile + 2 < TILES)
-        def _():
-            ct_load(tile + 2).start()
-
-    def bwd_item(item):
-        g, tile = item // TILES, lax.rem(item, TILES)
-        kv_cols = blk(g, head_dim)
-        rows = blk(tile, tq)
-
-        @pl.when(tile == 0)
-        def _():
-            kt_ref[0] = kl_ref[:, kv_cols].T
-            kt_ref[1] = kp_ref[:, kv_cols].T
-
-        for h in range(group):
-            cols = blk(g * group + h, head_dim)
-            stack = blk(h, tq)
-            qs_ref[stack, :] = q_ref[rows, cols]
-            d_h = do_ref[rows, cols]
-            dos_ref[stack, :] = d_h
-            prod = d_h.astype(F32) * o_ref[rows, cols].astype(F32)
-            delta_ref[:, stack] = row_sum(prod.T)
-        zero(dqt_ref)
-
-        def piece(k_ref, v_ref, dk_ref, dv_ref, side, span, masked):
-            scores = dot(k_ref[span, kv_cols], qs_ref[...], NT)
-            if masked:
-                scores = causal(scores, tq)
-            probs = jnp.exp2(scores * (score_scale * LOG2E) - lse_ref[item])
-            d_probs = dot(v_ref[span, kv_cols], dos_ref[...], NT)
-            d_scores = (probs * (d_probs - delta_ref[...])).astype(BF)
-            dv_ref[g, span, :] += dot(probs.astype(BF), dos_ref[...], NN)
-            dk_ref[g, span, :] += dot(d_scores, qs_ref[...], NN)
-            dqt_ref[...] += dot(kt_ref[side, :, span], d_scores, NN)
-
-        piece(kl_ref, vl_ref, dkl_ref, dvl_ref, 0, blk(tile, tq), True)
-
-        @pl.loop(0, tile // 2)
-        def _(i):
-            piece(kl_ref, vl_ref, dkl_ref, dvl_ref, 0, blk(i, 2 * tq), False)
-
-        @pl.when(parity(tile) == 1)
-        def _():
-            piece(kl_ref, vl_ref, dkl_ref, dvl_ref, 0, blk(tile - 1, tq), False)
-
-        @pl.loop(0, flag * TILES // 2)
-        def _(i):
-            piece(kp_ref, vp_ref, dkp_ref, dvp_ref, 1, blk(i, 2 * tq), False)
-
-        for h in range(group):
-            dq_h = dqt_ref[:, blk(h, tq)].T * score_scale
-            d_ref[rows, blk(g * group + h, head_dim)] = rope(dq_h, cos_ref[rows, :], -sin_ref[rows, :], half_dim).astype(BF)
-
-        @pl.when((tile == TILES - 1) & (flag == 1))
-        def _():
-            for copy in back(g):
-                copy.start()
-
-    def back(g):
-        return [remote(ref.at[g], ref.at[g], kv_send.at[k, g], kv_recv.at[k, g], {"cp": 0}) for k, ref in enumerate((dkp_ref, dvp_ref))]
-
-    def kv_done(g):
-        @pl.when(flag == 0)
-        def _():
-            for copy in back(g):
-                copy.wait_recv()
-            dkl_ref[g] += dkp_ref[g]
-            dvl_ref[g] += dvp_ref[g]
-
-        dk = rope(dkl_ref[g] * score_scale, cos_ref[...], -sin_ref[...], half_dim)
-        k_at = width // head_dim + g
-        d_ref[:, blk(k_at, head_dim)] = dk.astype(BF)
-        d_ref[:, blk(k_at + kv_heads, head_dim)] = dvl_ref[g].astype(BF)
-
-        @pl.when(flag == 1)
-        def _():
-            for copy in back(g):
-                copy.wait_send()
-
-    items = TILES * (kv_heads + 1)
-    o_ticks = TILES * last
-    x_at = {5: 0, 8: 1, 11: 2}
-
-    @pl.loop(0, items)
-    def _(item):
-        @pl.when(item < TILES)
-        def _():
-            do_tile(item)
-
-        @pl.when(item >= TILES)
-        def _():
-            bwd_item(item - TILES)
-
-        @pl.when((parity(item) == 1) & (item > 1))
-        def _():
-            o_tick(item // 2 - 1 + O_EARLY)
-
-        for r in range(1, n_line):
-            @pl.when(item == 3 * r + 1)
-            def _():
-                y_tick(r)
-
-        for at, q in x_at.items():
-            @pl.when(item == at)
-            def _():
-                x_tick(q)
-
-    done = items // 2 - 1 + O_EARLY
-    tail = [("x", q) for q in range(len(x_at), n_line)] + [("kv", g) for g in range(kv_heads)]
-    for k in range(done, o_ticks):
-        o_tick(jnp.int32(k))
-        if (k - done) % 2 == 1 and tail:
-            kind, arg = tail.pop(0)
-            x_tick(arg) if kind == "x" else kv_done(arg)
-            later = [t for t in tail if t[0] == "kv"]
-            if later:
-                tail.remove(later[0])
-                kv_done(later[0][1])
-    for kind, arg in tail:
-        x_tick(arg) if kind == "x" else kv_done(arg)
-
-    for r in range(1, n_line):
-        for side in (flag, far):
-            c_copy(r, side, f_core).wait_recv()
-            cx_copy(r, side, f_diag).wait_recv()
-            c_copy(r, side, f).wait_send()
-            cx_copy(r, side, f_x).wait_send()
-        x_copy(r, far, f).wait_send()
-        y_copy(r, flag).wait_send()
-    x_copy(third, flag, f).wait_send()
-
-    @pl.loop(0, n_line)
-    def _(t):
-        @pl.when((t >= z) & (z > 0))
-        def _():
-            @pl.loop(jnp.where(t == z, O_EARLY, 0), TILES)
-            def _(j):
-                o_down(t, j, o_all.at[t, tile_rows(j)]).wait_send()
-
-        @pl.when((t <= z) & (z < last))
-        def _():
-            @pl.loop(jnp.where(t == z, O_EARLY, 0), TILES)
-            def _(j):
-                o_up(t, j, o_all.at[t, tile_rows(j)]).wait_send()
-
-    keep.wait()
-
-
-def attn_back(attn_out, q_rot, lse, cosines, sines, k_loc, v_loc, k_prev, v_prev, wo_all, o_all, cotangent, n_line, group, cid):
-    q_len, width = attn_out.shape
-    head_dim = cosines.shape[1]
-    kv_width = k_loc.shape[1]
-    kv_heads = kv_width // head_dim
-    _, n_fsdp, o_rows, o_cols = wo_all.shape
-    tq = q_len // TILES
-    wide = group * tq
-    acc = pltpu.VMEM((kv_heads, q_len, head_dim), F32)
-    stack = pltpu.VMEM((wide, head_dim), BF)
-    own, pair, tiles, hop, side, kv = DMA(()), DMA((2,)), DMA((n_line, TILES)), DMA((n_line - 1,)), DMA((2, n_line - 1)), DMA((2, kv_heads))
-    return pl.pallas_call(
-        functools.partial(back_kernel, n_line, group),
-        in_specs=[VMEM] * 9 + [ANY] * 3,
-        out_specs=[VMEM, ANY, ANY],
-        out_shape=[jax.ShapeDtypeStruct((q_len, width + 2 * kv_width), BF), jax.ShapeDtypeStruct((n_line, q_len, width), BF), jax.ShapeDtypeStruct(wo_all.shape, BF)],
-        input_output_aliases={9: 2, 10: 1},
-        scratch_shapes=[
-            pltpu.VMEM((n_fsdp, o_rows, o_cols), BF),
-            pltpu.VMEM((2, tq, cotangent.shape[1]), BF),
-            pltpu.VMEM((q_len, width), BF),
-            acc, acc, acc, acc,
+            heads,
+            line,
+            kv, kv, kv, kv,
+            heads,
+            sums, sums, sums, sums,
             stack,
             stack,
             pltpu.VMEM((1, wide), F32),
             pltpu.VMEM((2, head_dim, q_len), BF),
             pltpu.VMEM((head_dim, wide), F32),
-        ] + [own, own, pair, tiles, tiles, tiles, hop, hop, side, side, side, side, side, side, kv, kv],
+        ] + [pair, trio, trio, own, own, w_link, w_link, w_link, w_link, w_side, w_side, dkv, dkv, o_link, o_link, o_link, o_link, o_core, o_core, DMA((2, n_line)), DMA((n_line,)), DMA((4 + n_fsdp,)), pair, tiles, tiles, tiles, hop, hop, side, side, side, side, side, side, dkv, dkv],
         compiler_params=params(cid),
-        name="attn_back",
-    )(attn_out, q_rot, lse, cosines, sines, k_loc, v_loc, k_prev, v_prev, wo_all, o_all, cotangent)
+        name="core",
+    )(hidden, gain, w_qkv, w_out, cosines, sines, cotangent)
 
 
 class Line:
@@ -1323,9 +1227,8 @@
         q_width, kv_width = q_heads * head_dim, kv_heads * head_dim
         w_qkv = jnp.concatenate([w_query.reshape(feat, q_width), w_key.reshape(feat, kv_width), w_value.reshape(feat, kv_width)], axis=1)
         cosines, sines = rope_tables(positions, head_dim)
-        attn_out, q_rot, lse, k_loc, v_loc, k_prev, v_prev, gain_full, normed, w_full, wo_all, o_all = front(hidden, gain.astype(F32)[None], w_qkv, w_out.reshape(q_width, feat), cosines, sines, group, kv_width, n_line, 0)
-        d_lin, o_all, wo_all = attn_back(attn_out, q_rot, lse, cosines, sines, k_loc, v_loc, k_prev, v_prev, wo_all, o_all, cotangent, n_line, group, 1)
-        grad_hidden, block_out, grad_gain, mine, theirs = close(d_lin, attn_out, gain_full, hidden, cotangent, normed, w_full, o_all, wo_all, 2)[:5]
+        d_lin, attn_out, gain_full, normed, w_full, wo_all, o_all = core(hidden, gain.astype(F32)[None], w_qkv, w_out.reshape(q_width, feat), cosines, sines, cotangent, group, kv_width, n_line, 0)
+        grad_hidden, block_out, grad_gain, mine, theirs = close(d_lin, attn_out, gain_full, hidden, cotangent, normed, w_full, o_all, wo_all, 1)[:5]
         block_out, grad_hidden, g_query, g_key, g_value, g_out = tail(block_out, grad_hidden, mine, theirs, q_heads, kv_heads, head_dim)
         return block_out[None], grad_hidden[None], grad_gain[0], g_query, g_key, g_value, g_out.reshape(w_out.shape)
 

time: 618 us -> 614 us (level)
    pallas_call x2 -> x1, Pallas kernels: 246 us -> 232 us  [core(): pl.pallas_call(functools.partial(core_kernel, group, n_line), in_specs=[A...]
    pallas_call x1, Pallas kernels: 339 us -> 348 us  [close(): pl.pallas_call(functools.partial(close_kernel, n_line, n_fsdp), in_specs=...]
where the time goes in v5:
time: 614 us; the launch traced here: 612 us
  Pallas kernels  601 us (98%)
  other arithmetic  7.12 us (1%)
    pallas_call x1, Pallas kernels, close(): pl.pallas_call(functools.partial(close_kernel, n_line, n_fsdp), in_specs=...  348 us
    pallas_call x1, Pallas kernels, core(): pl.pallas_call(functools.partial(core_kernel, group, n_line), in_specs=[A...  232 us
    pallas_call x1, Pallas kernels, tail(): pl.pallas_call(functools.partial(tail_kernel, head_dim), grid=(GRAD_CHUNK...  21.1 us

profile of v5, /device:TPU:0, one launch (start us, length us, event | category | flops | bytes accessed | tf_op | source)
XLA Modules:
  0.0 612.5 jit_solution(13211868360823839828)
XLA Ops:
  0.6 0.0 copy-start
  0.7 0.8 convert_element_type.11
  1.5 1.3 broadcast_in_dim.17
  2.8 1.4 copy_bitcast_fusion.1
  4.1 1.9 fusion
  6.0 1.3 pad_maximum_fusion.1
  7.3 0.0 copy-done
  7.3 0.6 copy.21
  8.0 1.8 pad_maximum_fusion.w_ref
  9.8 232.3 %core.1 = (bf16[1024,1536]{1,0:T(8,128)(2,1)}, bf16[1024,1024]{1,0:T(8,128)(2,1)}, f32[1,4096]{1,0:T(1,128)}, bf16[1024,4096]{1,0:T(8,128)(2,1)}, bf16[4,1024,15...) custom-call(bf16[1024,4096]{1,0:T(8,128)(2,1)} %bitcast.18, ...), custom_call_target="tpu_custom_call" | custom-call | tf_op jit(solution)/shard_map/core/pallas_call | solution.py:682
  242.1 348.0 %close.1 = (bf16[1024,4096]{1,0:T(8,128)(2,1)}, bf16[1024,4096]{1,0:T(8,128)(2,1)}, f32[1,1024]{1,0:T(1,128)}, f32[1024,2560]{1,0:T(8,128)}, f32[1024,2560]{1,0:...) custom-call(bf16[1024,1536]{1,0:T(8,128)(2,1)} %get-tuple-element.25.d_, ...), custom_call_target="tpu_custom_call" | custom-call | tf_op jit(solution)/shard_map/close/pallas_call | solution.py:1154
  590.1 21.1 %tail.1 = (bf16[1024,4096]{1,0:T(8,128)(2,1)}, bf16[1024,4096]{1,0:T(8,128)(2,1)}, f32[1024,8,128]{2,1,0:T(8,128)}, f32[1024,2,128]{2,1,0:T(2,128)}, f32[1024,2,128]{2,1,0:T(2,128)}, /*index=5*/f32[1024,1024]{1,0:T(8,128)}) custom-call(bf16[1024,4096]{1,0:T(8,128)(2,1)} %get-tuple-element.32.blk_ref, bf16[1024,4096]{1,0:T(8,128)(2,1)} %get-tuple-element.33.hid_ref, ...), custom_call_target="tpu_custom_call" | custom-call | tf_op jit(solution)/shard_map/tail/pallas_call | solution.py:1204
  611.2 1.3 copy.23
  (1 shorter events, 0.0 us)
Async XLA Ops:
  0.6 6.7 %copy-start = (bf16[1024,8,128]{2,1,0:T(8,128)(2,1)S(1)}, bf16[1024,8,128]{2,1,0:T(8,128)(2,1)}, u32[]{:S(2)}) copy-start(bf16[1024,8,128]{2,1,0:T(8,128)(2,1)} %param.12) | copy-start | bytes 6291460

commit v6 on v5

--- a/solution.py
+++ b/solution.py
@@ -110,7 +110,7 @@
     return jnp.concatenate([cosines, cosines], axis=1), jnp.concatenate([-sines, sines], axis=1)
 
 
-def core_kernel(group, n_line, hid_ref, gain_ref, w_ref, wo_ref, cos_ref, sin_ref, ct_ref, d_ref, o_ref, gfull_ref, n_out, w_out, wo_all, o_all, wbuf, nbuf, acc, hbuf, gbuf, qs, vt, m_all, l_all, acc_all, q_ref, lse_ref, kl_ref, vl_ref, kp_ref, vp_ref, do_ref, dkl_ref, dvl_ref, dkp_ref, dvp_ref, qs_ref, dos_ref, delta_ref, kt_ref, dqt_ref, h_sem, g_send, g_recv, own_send, own_recv, x_send, x_recv, y_send, y_recv, d_send, d_recv, kv_send, kv_recv, ox_send, ox_recv, oy_send, oy_recv, od_send, od_recv, zw_send, zw_recv, out_sem, ct_sem, on_send, ou_send, o_recv, wy_send, wy_recv, wx_send, wx_recv, wc_send, wc_recv, cx_send, cx_recv, dk_send, dk_recv):
+def core_kernel(group, n_line, hid_ref, gain_ref, w_ref, wo_ref, cos_ref, sin_ref, ct_ref, d_ref, o_ref, gfull_ref, n_out, w_out, wo_all, o_all, wbuf, nbuf, acc, hbuf, gbuf, qs, vt, m_all, l_all, acc_all, q_ref, lse_ref, kl_ref, vl_ref, kp_ref, vp_ref, do_ref, dkl_ref, dvl_ref, dkp_ref, dvp_ref, qs_ref, dos_ref, delta_ref, kt_ref, dqt_ref, h_sem, g_send, g_recv, own_send, own_recv, x_send, x_recv, y_send, y_recv, d_send, d_recv, kv_send, kv_recv, ox_send, ox_recv, oy_send, oy_recv, od_send, od_recv, zw_send, zw_recv, out_sem, ct_sem, o_sems, o_recv, wy_send, wy_recv, wx_send, wx_recv, wc_send, wc_recv, cx_send, cx_recv, dk_send, dk_recv):
     q_len, feat = hid_ref.shape[0], w_ref.shape[0]
     head_dim = cos_ref.shape[1]
     half_dim = head_dim // 2
@@ -195,11 +195,16 @@
     def tile_rows(j):
         return blk(j, tq)
 
-    def o_down(t, j, src):
-        return remote(src, o_all.at[t, tile_rows(j)], on_send.at[t, j], o_recv.at[t, j], {"tp": jnp.maximum(z - 1, 0)})
-
-    def o_up(t, j, src):
-        return remote(src, o_all.at[t, tile_rows(j)], ou_send.at[t, j], o_recv.at[t, j], {"tp": jnp.minimum(z + 1, last)})
+    o_parts = kv_heads * TILES
+
+    def o_piece_at(ref, j):
+        return ref.at[tile_rows(lax.rem(j, TILES)), blk(j // TILES, group * head_dim)]
+
+    def o_copy(up, t, j, own=False):
+        spot = o_piece_at(o_all.at[t], j)
+        src = o_piece_at(o_ref, j) if own else spot
+        where = jnp.minimum(z + 1, last) if up else jnp.maximum(z - 1, 0)
+        return remote(src, spot, o_sems.at[up, t, j], o_recv.at[t, j], {"tp": where})
 
     def wo_half(r, slot, side):
         return wo_all.at[lax.rem(z + r, n_line), slot, blk(side, o_half)]
@@ -217,25 +222,17 @@
         return remote(wo_half(r, slot, side), wo_half(r, slot, side), cx_send.at[side, r - 1], cx_recv.at[side, r - 1], to_core)
 
     def o_tick(k):
-        r, j = k // TILES + 1, lax.rem(k, TILES)
-
-        @pl.when(z + r <= last)
-        def _():
-            t = jnp.minimum(z + r, last)
-            o_down(t, j, o_all.at[t, tile_rows(j)]).wait_recv()
-
-            @pl.when(z > 0)
-            def _():
-                o_down(t, j, o_all.at[t, tile_rows(j)]).start()
-
-        @pl.when(z - r >= 0)
-        def _():
-            t = jnp.maximum(z - r, 0)
-            o_up(t, j, o_all.at[t, tile_rows(j)]).wait_recv()
-
-            @pl.when(z < last)
-            def _():
-                o_up(t, j, o_all.at[t, tile_rows(j)]).start()
+        r, j = k // o_parts + 1, lax.rem(k, o_parts)
+        for up, t, here in ((0, z + r, z + r <= last), (1, z - r, z >= r)):
+            at = jnp.clip(t, 0, last)
+
+            @pl.when(here)
+            def _():
+                o_copy(up, at, j).wait_recv()
+
+            @pl.when(here & (z < last if up else z > 0))
+            def _():
+                o_copy(up, at, j).start()
 
     def wy_tick(r):
         wy_copy(r, far).wait_recv()
@@ -254,13 +251,10 @@
         cx_copy(r, side, f_x).start()
 
     def o_send(j):
-        @pl.when(z > 0)
-        def _():
-            o_down(z, j, o_ref.at[tile_rows(j)]).start()
-
-        @pl.when(z < last)
-        def _():
-            o_up(z, j, o_ref.at[tile_rows(j)]).start()
+        for up in SIDES:
+            @pl.when(z < last if up else z > 0)
+            def _():
+                o_copy(up, z, j, True).start()
 
     gains = [(k, where, where["fsdp"]) for k, where in enumerate((to_core, to_x, to_diag))]
     for k, where, _ in gains:
@@ -450,11 +444,9 @@
         for h in range(group):
             o_ref[rows, blk(g * group + h, head_dim)] = out_t[:, h * tq:h * tq + tq].T.astype(BF)
 
-        ready = item - TILES * (kv_heads - 1) - 1
-
-        @pl.when(ready >= 0)
-        def _():
-            o_send(ready)
+        @pl.when(item > 0)
+        def _():
+            o_send(item - 1)
 
         for j in range(O_PIECES):
             @pl.when(item == (j + 1) * kv_heads * TILES // O_PIECES - 1)
@@ -462,7 +454,7 @@
                 oy_copy(j, far).wait_recv()
                 od_copy(1 + O_PIECES + j, wo_out.at[f_x, o_span(1 - flag, j)], f_x, o_span(1 - flag, j)).start()
 
-    o_send(TILES - 1)
+    o_send(o_parts - 1)
     wx_copy(own_order[last - 1], flag, f).start()
     for r in range(1, last):
         wy_copy(r, flag).start()
@@ -495,7 +487,8 @@
         zero(dvp_ref)
 
     wx_tick(0)
-    o_tick(jnp.int32(0))
+    for k in SIDES:
+        o_tick(jnp.int32(k))
     for load in loads:
         load.wait()
 
@@ -583,10 +576,7 @@
                 copy.wait_send()
 
     items = TILES * (kv_heads + 1)
-    plan = {1: [(o_tick, 1), (wx_tick, 1)], 4: [(o_tick, 2)], 5: [(wy_tick, 1)], 6: [(o_tick, 3), (wx_tick, 2)], 8: [(o_tick, 4), (wy_tick, 2)], 9: [(o_tick, 5), (wx_tick, 3)], 11: [(o_tick, 6)]}
-
-    def run(tick, arg):
-        tick(jnp.int32(arg) if tick is o_tick else arg)
+    plan = {1: [(wx_tick, 1)], 5: [(wy_tick, 1)], 6: [(wx_tick, 2)], 8: [(wy_tick, 2)], 9: [(wx_tick, 3)]}
 
     @pl.loop(0, items)
     def _(item):
@@ -598,14 +588,22 @@
         def _():
             bwd_item(item - TILES)
 
+        @pl.when(item != 1)
+        def _():
+            o_tick(jnp.where(item > 1, item + 1, 2))
+
         for at, jobs in plan.items():
             @pl.when(item == at)
             def _():
                 for tick, arg in jobs:
-                    run(tick, arg)
-
-    for tick, arg in [(wy_tick, 3), (o_tick, 7), (wx_tick, 4), (o_tick, 8), (kv_done, 0), (o_tick, 9), (wx_tick, 5), (o_tick, 10), (kv_done, 1), (o_tick, 11)]:
-        run(tick, arg)
+                    tick(arg)
+
+    rest = {1: (wy_tick, 3), 2: (wx_tick, 4), 5: (kv_done, 0), 6: (wx_tick, 5), 9: (kv_done, 1)}
+    for k in range(items + 1, o_parts * last):
+        o_tick(jnp.int32(k))
+        if k - items in rest:
+            tick, arg = rest[k - items]
+            tick(arg)
 
     for r in range(1, n_line):
         for side in (flag, far):
@@ -618,14 +616,11 @@
 
     @pl.loop(0, n_line)
     def _(t):
-        for j in range(TILES):
-            @pl.when((t >= z) & (z > 0))
-            def _():
-                o_down(t, j, o_all.at[t, tile_rows(j)]).wait_send()
-
-            @pl.when((t <= z) & (z < last))
-            def _():
-                o_up(t, j, o_all.at[t, tile_rows(j)]).wait_send()
+        for up in SIDES:
+            @pl.when((t <= z) & (z < last) if up else (t >= z) & (z > 0))
+            def _():
+                for j in range(o_parts):
+                    o_copy(up, t, j).wait_send()
 
     @pl.loop(0, n_line)
     def _(t):
@@ -678,7 +673,7 @@
     stack = pltpu.VMEM((wide, head_dim), BF)
     own, pair, trio = DMA(()), DMA((2,)), DMA((n_fsdp - 1,))
     w_link, w_side, o_link, o_core = DMA((PIECES,)), DMA((2, PIECES)), DMA((O_PIECES,)), DMA((1 + 2 * O_PIECES,))
-    tiles, hop, side, dkv = DMA((n_line, TILES)), DMA((n_line - 1,)), DMA((2, n_line - 1)), DMA((2, kv_heads))
+    hop, side, dkv = DMA((n_line - 1,)), DMA((2, n_line - 1)), DMA((2, kv_heads))
     return pl.pallas_call(
         functools.partial(core_kernel, group, n_line),
         in_specs=[ANY] + [VMEM] * 5 + [ANY],
@@ -705,7 +700,7 @@
             pltpu.VMEM((1, wide), F32),
             pltpu.VMEM((2, head_dim, q_len), BF),
             pltpu.VMEM((head_dim, wide), F32),
-        ] + [pair, trio, trio, own, own, w_link, w_link, w_link, w_link, w_side, w_side, dkv, dkv, o_link, o_link, o_link, o_link, o_core, o_core, DMA((2, n_line)), DMA((n_line,)), DMA((4 + n_fsdp,)), pair, tiles, tiles, tiles, hop, hop, side, side, side, side, side, side, dkv, dkv],
+        ] + [pair, trio, trio, own, own, w_link, w_link, w_link, w_link, w_side, w_side, dkv, dkv, o_link, o_link, o_link, o_link, o_core, o_core, DMA((2, n_line)), DMA((n_line,)), DMA((4 + n_fsdp,)), pair, DMA((2, n_line, items)), DMA((n_line, items)), hop, hop, side, side, side, side, side, side, dkv, dkv],
         compiler_params=params(cid),
         name="core",
     )(hidden, gain, w_qkv, w_out, cosines, sines, cotangent)
@@ -960,10 +955,6 @@
             whole = lax.rem(fine, PER_STEP) == 0
             j, odd = step // 2, parity(step)
 
-            @pl.when(whole & (odd == 0) & (j > 0) & (j <= GRAD_CHUNKS))
-            def _():
-                send_x(j - 1)
-
             @pl.when(whole & (odd == 0) & (j < GRAD_CHUNKS))
             def _():
                 make(j)
@@ -971,13 +962,14 @@
             @pl.when(whole & (odd == 1) & (j < GRAD_CHUNKS))
             def _():
                 meet_core(j)
-
-            for late in SIDES:
-                k = (step - FIRST_X - late) * 2 // 5
-
-                @pl.when(whole & (k >= 0) & (k < EARLY) & (step - late == FIRST_X + (5 * k + 1) // 2))
-                def _():
-                    send_y(k) if late else meet_x(k)
+                send_x(j)
+
+            k = ((step - FIRST_X) * 2 + 1) // 5
+
+            @pl.when(whole & (k >= 0) & (k < EARLY) & (step == FIRST_X + 5 * k // 2))
+            def _():
+                meet_x(k)
+                send_y(k)
 
             @pl.when(fine >= chunks)
             def _():
@@ -1087,10 +1079,6 @@
                 @pl.when(step == at)
                 def _():
                     meet_x(k)
-
-            for k, at in ((EARLY - 1, -1),) + LATE:
-                @pl.when(step == at + 1)
-                def _():
                     send_y(k)
 
         for item in range(items - 2, items):

time: 614 us -> 610 us (level)
  no operation moved by 1% of the time
where the time goes in v6:
time: 610 us; the launch traced here: 609 us
  Pallas kernels  598 us (98%)
  other arithmetic  7.12 us (1%)
    pallas_call x1, Pallas kernels, close(): pl.pallas_call(functools.partial(close_kernel, n_line, n_fsdp), in_specs=...  346 us
    pallas_call x1, Pallas kernels, core(): pl.pallas_call(functools.partial(core_kernel, group, n_line), in_specs=[A...  230 us
    pallas_call x1, Pallas kernels, tail(): pl.pallas_call(functools.partial(tail_kernel, head_dim), grid=(GRAD_CHUNK...  21.1 us

profile of v6, /device:TPU:0, one launch (start us, length us, event | category | flops | bytes accessed | tf_op | source)
XLA Modules:
  0.0 608.8 jit_solution(13470075917793686409)
XLA Ops:
  0.6 0.0 copy-start
  0.7 0.8 convert_element_type.11
  1.5 1.3 broadcast_in_dim.17
  2.8 1.4 copy_bitcast_fusion.1
  4.1 1.9 fusion
  6.0 1.3 pad_maximum_fusion.1
  7.3 0.0 copy-done
  7.3 0.6 copy.21
  8.0 1.8 pad_maximum_fusion.w_ref
  9.8 230.3 %core.1 = (bf16[1024,1536]{1,0:T(8,128)(2,1)}, bf16[1024,1024]{1,0:T(8,128)(2,1)}, f32[1,4096]{1,0:T(1,128)}, bf16[1024,4096]{1,0:T(8,128)(2,1)}, bf16[4,1024,15...) custom-call(bf16[1024,4096]{1,0:T(8,128)(2,1)} %bitcast.18, ...), custom_call_target="tpu_custom_call" | custom-call | tf_op jit(solution)/shard_map/core/pallas_call | solution.py:677
  240.0 346.3 %close.1 = (bf16[1024,4096]{1,0:T(8,128)(2,1)}, bf16[1024,4096]{1,0:T(8,128)(2,1)}, f32[1,1024]{1,0:T(1,128)}, f32[1024,2560]{1,0:T(8,128)}, f32[1024,2560]{1,0:...) custom-call(bf16[1024,1536]{1,0:T(8,128)(2,1)} %get-tuple-element.25.d_, ...), custom_call_target="tpu_custom_call" | custom-call | tf_op jit(solution)/shard_map/close/pallas_call | solution.py:1142
  586.4 21.1 %tail.1 = (bf16[1024,4096]{1,0:T(8,128)(2,1)}, bf16[1024,4096]{1,0:T(8,128)(2,1)}, f32[1024,8,128]{2,1,0:T(8,128)}, f32[1024,2,128]{2,1,0:T(2,128)}, f32[1024,2,128]{2,1,0:T(2,128)}, /*index=5*/f32[1024,1024]{1,0:T(8,128)}) custom-call(bf16[1024,4096]{1,0:T(8,128)(2,1)} %get-tuple-element.32.blk_ref, bf16[1024,4096]{1,0:T(8,128)(2,1)} %get-tuple-element.33.hid_ref, ...), custom_call_target="tpu_custom_call" | custom-call | tf_op jit(solution)/shard_map/tail/pallas_call | solution.py:1192
  607.5 1.3 copy.23
  (1 shorter events, 0.0 us)
Async XLA Ops:
  0.6 6.7 %copy-start = (bf16[1024,8,128]{2,1,0:T(8,128)(2,1)S(1)}, bf16[1024,8,128]{2,1,0:T(8,128)(2,1)}, u32[]{:S(2)}) copy-start(bf16[1024,8,128]{2,1,0:T(8,128)(2,1)} %param.12) | copy-start | bytes 6291460

commit v7 on v6

--- a/solution.py
+++ b/solution.py
@@ -17,6 +17,7 @@
 CHUNKS = 16
 PER_STEP = 1
 LEAD = 2
+QUARTERS = 3
 PIECES = 8
 O_PIECES = 2
 GRAD_CHUNKS = 8
@@ -277,7 +278,7 @@
     for k, where, slot in gains:
         g_copy(k, where, slot).wait_recv()
     for k in range(gbuf.shape[0]):
-        gfull_ref[:, blk(k, feat)] = gbuf[k]
+        gfull_ref[:, blk(k, feat)] = gbuf[k].astype(F32)
 
     for tile in range(TILES):
         h_load(tile).wait()
@@ -684,7 +685,7 @@
             pltpu.VMEM((max(q_len, o_rows), model_dim), BF),
             pltpu.VMEM((q_len, width), F32),
             pltpu.VMEM((2, tq, model_dim), BF),
-            pltpu.VMEM((n_fsdp, 1, feat), F32),
+            pltpu.VMEM((n_fsdp, 1, feat), BF),
             pltpu.VMEM((head_dim, wide), BF),
             pltpu.VMEM((kv_heads, 2, head_dim, q_len), BF),
             line,
@@ -1033,34 +1034,37 @@
                     ga_copy(end, k).start()
 
 
-        def project(item):
+        def project(quarter):
+            item, tile = quarter // TILES, lax.rem(quarter, TILES)
             slot = parity(item)
-            for load in item_loads(item):
-                load.wait()
-
-            @pl.when(item > 1)
+
+            @pl.when(tile == 0)
+            def _():
+                for load in item_loads(item):
+                    load.wait()
+
+            @pl.when((tile == 0) & (item > 1))
             def _():
                 item_store(item - 2).wait()
 
-            @pl.loop(0, TILES)
-            def _(tile):
-                span = blk(tile, q_len // TILES)
-                total = sum(dot(obuf[t, span, :], wbuf[slot, t], NN) for t in range(n_line))
-                rbuf[slot, span, :] = (hbuf[slot, span, :].astype(F32) + total).astype(BF)
-
-            item_store(item).start()
-
-            @pl.when(item + 2 < items)
-            def _():
-                for load in item_loads(item + 2):
-                    load.start()
+            span = blk(tile, q_len // TILES)
+            total = sum(dot(obuf[t, span, :], wbuf[slot, t], NN) for t in range(n_line))
+            rbuf[slot, span, :] = (hbuf[slot, span, :].astype(F32) + total).astype(BF)
+
+            @pl.when(tile == TILES - 1)
+            def _():
+                item_store(item).start()
+
+                @pl.when(item + 2 < items)
+                def _():
+                    for load in item_loads(item + 2):
+                        load.start()
 
         for end, here in ends:
             @pl.when(jnp.logical_not(here))
             def _():
                 ga_copy(end, 0).wait_recv()
         gs[...] = ga[0] + ga[1]
-        o_load.wait()
         gb_copy().start()
 
         early = (last - 1) * PER_STEP
@@ -1071,9 +1075,17 @@
             owner_send(sent, jnp.minimum(sent + 1, chunks))
             pass_on(step + early)
 
-            @pl.when((parity(step) == 0) & (step // 2 < items))
-            def _():
-                project(step // 2)
+            @pl.when(step == 1)
+            def _():
+                o_load.wait()
+
+            @pl.when(step > 0)
+            def _():
+                first = (step - 1) * QUARTERS
+
+                @pl.loop(first, jnp.minimum(first + QUARTERS, items * TILES))
+                def _(quarter):
+                    project(quarter)
 
             for k, at in LATE:
                 @pl.when(step == at)
@@ -1215,7 +1227,7 @@
         q_width, kv_width = q_heads * head_dim, kv_heads * head_dim
         w_qkv = jnp.concatenate([w_query.reshape(feat, q_width), w_key.reshape(feat, kv_width), w_value.reshape(feat, kv_width)], axis=1)
         cosines, sines = rope_tables(positions, head_dim)
-        d_lin, attn_out, gain_full, normed, w_full, wo_all, o_all = core(hidden, gain.astype(F32)[None], w_qkv, w_out.reshape(q_width, feat), cosines, sines, cotangent, group, kv_width, n_line, 0)
+        d_lin, attn_out, gain_full, normed, w_full, wo_all, o_all = core(hidden, gain[None], w_qkv, w_out.reshape(q_width, feat), cosines, sines, cotangent, group, kv_width, n_line, 0)
         grad_hidden, block_out, grad_gain, mine, theirs = close(d_lin, attn_out, gain_full, hidden, cotangent, normed, w_full, o_all, wo_all, 1)[:5]
         block_out, grad_hidden, g_query, g_key, g_value, g_out = tail(block_out, grad_hidden, mine, theirs, q_heads, kv_heads, head_dim)
         return block_out[None], grad_hidden[None], grad_gain[0], g_query, g_key, g_value, g_out.reshape(w_out.shape)

time: 610 us -> 603 us (0.989)
  Pallas kernels: 598 us -> 591 us
    pallas_call x1, Pallas kernels: 346 us -> 340 us  [close(): pl.pallas_call(functools.partial(close_kernel, n_line, n_fsdp), in_specs=...]
where the time goes in v7:
time: 603 us; the launch traced here: 602 us
  Pallas kernels  591 us (98%)
    pallas_call x1, Pallas kernels, close(): pl.pallas_call(functools.partial(close_kernel, n_line, n_fsdp), in_specs=...  340 us
    pallas_call x1, Pallas kernels, core(): pl.pallas_call(functools.partial(core_kernel, group, n_line), in_specs=[A...  230 us
    pallas_call x1, Pallas kernels, tail(): pl.pallas_call(functools.partial(tail_kernel, head_dim), grid=(GRAD_CHUNK...  21.1 us

profile of v7, /device:TPU:0, one launch (start us, length us, event | category | flops | bytes accessed | tf_op | source)
XLA Modules:
  0.0 602.4 jit_solution(9471205382479794741)
XLA Ops:
  0.6 0.0 copy-start
  0.7 0.8 convert_element_type.10
  1.5 1.3 broadcast_in_dim.11.gain_ref
  2.8 1.4 copy_bitcast_fusion.1
  4.1 1.9 fusion
  6.0 1.3 pad_maximum_fusion.1
  7.3 0.0 copy-done
  7.3 0.6 copy.21
  8.0 1.8 pad_maximum_fusion.w_ref
  9.8 230.3 %core.1 = (bf16[1024,1536]{1,0:T(8,128)(2,1)}, bf16[1024,1024]{1,0:T(8,128)(2,1)}, f32[1,4096]{1,0:T(1,128)}, bf16[1024,4096]{1,0:T(8,128)(2,1)}, bf16[4,1024,15...) custom-call(bf16[1024,4096]{1,0:T(8,128)(2,1)} %bitcast.17, ...), custom_call_target="tpu_custom_call" | custom-call | tf_op jit(solution)/shard_map/core/pallas_call | solution.py:678
  240.0 339.9 %close.1 = (bf16[1024,4096]{1,0:T(8,128)(2,1)}, bf16[1024,4096]{1,0:T(8,128)(2,1)}, f32[1,1024]{1,0:T(1,128)}, f32[1024,2560]{1,0:T(8,128)}, f32[1024,2560]{1,0:...) custom-call(bf16[1024,1536]{1,0:T(8,128)(2,1)} %get-tuple-element.25.d_, ...), custom_call_target="tpu_custom_call" | custom-call | tf_op jit(solution)/shard_map/close/pallas_call | solution.py:1154
  579.9 21.1 %tail.1 = (bf16[1024,4096]{1,0:T(8,128)(2,1)}, bf16[1024,4096]{1,0:T(8,128)(2,1)}, f32[1024,8,128]{2,1,0:T(8,128)}, f32[1024,2,128]{2,1,0:T(2,128)}, f32[1024,2,128]{2,1,0:T(2,128)}, /*index=5*/f32[1024,1024]{1,0:T(8,128)}) custom-call(bf16[1024,4096]{1,0:T(8,128)(2,1)} %get-tuple-element.32.blk_ref, bf16[1024,4096]{1,0:T(8,128)(2,1)} %get-tuple-element.33.hid_ref, ...), custom_call_target="tpu_custom_call" | custom-call | tf_op jit(solution)/shard_map/tail/pallas_call | solution.py:1204
  601.1 1.3 copy.23
  (1 shorter events, 0.0 us)
Async XLA Ops:
  0.6 6.7 %copy-start = (bf16[1024,8,128]{2,1,0:T(8,128)(2,1)S(1)}, bf16[1024,8,128]{2,1,0:T(8,128)(2,1)}, u32[]{:S(2)}) copy-start(bf16[1024,8,128]{2,1,0:T(8,128)(2,1)} %param.12) | copy-start | bytes 6291460

commit v8 on v7

--- a/solution.py
+++ b/solution.py
@@ -15,15 +15,14 @@
 LOG2E = math.log2(math.e)
 TILES = 4
 CHUNKS = 16
-PER_STEP = 1
 LEAD = 2
 QUARTERS = 3
 PIECES = 8
 O_PIECES = 2
 GRAD_CHUNKS = 8
-FIRST_X = 5
+FIRST_X = 6
 EARLY = 6
-LATE = ((6, 2), (7, 7))
+LATE = ((6, 4), (7, 9))
 VMEM_BYTES = 67043328
 SIDES = range(2)
 
@@ -807,7 +806,6 @@
                 load.start()
 
     zero(gp)
-    meet([to_core, to_x, to_y] + others("tp", z, n_line) + [{"fsdp": f_diag}])
 
     def finish(chunk, total):
         slot = parity(chunk)
@@ -948,26 +946,25 @@
             load.start()
         w_load.wait()
         line.prepare(0)
+        meet([to_core, to_x, to_y] + others("tp", z, n_line) + [{"fsdp": f_diag}])
 
         @pl.loop(0, line.steps)
         def _(fine):
             line.tick(fine)
-            step = fine // PER_STEP
-            whole = lax.rem(fine, PER_STEP) == 0
-            j, odd = step // 2, parity(step)
-
-            @pl.when(whole & (odd == 0) & (j < GRAD_CHUNKS))
+            j, odd = fine // 2, parity(fine)
+
+            @pl.when((odd == 0) & (j < GRAD_CHUNKS))
             def _():
                 make(j)
 
-            @pl.when(whole & (odd == 1) & (j < GRAD_CHUNKS))
+            @pl.when((odd == 1) & (j < GRAD_CHUNKS))
             def _():
                 meet_core(j)
                 send_x(j)
 
-            k = ((step - FIRST_X) * 2 + 1) // 5
-
-            @pl.when(whole & (k >= 0) & (k < EARLY) & (step == FIRST_X + 5 * k // 2))
+            k = ((fine - FIRST_X) * 2 + 1) // 5
+
+            @pl.when((k >= 0) & (k < EARLY) & (fine == FIRST_X + 5 * k // 2))
             def _():
                 meet_x(k)
                 send_y(k)
@@ -978,8 +975,8 @@
 
             @pl.when(fine > chunks)
             def _():
-                for k in range(PER_STEP):
-                    pass_on((fine - chunks - 1) * PER_STEP + k)
+                for k in range(LEAD):
+                    pass_on((fine - chunks - 1) * LEAD + k)
 
         @pl.when(owner)
         def _():
@@ -1067,7 +1064,7 @@
         gs[...] = ga[0] + ga[1]
         gb_copy().start()
 
-        early = (last - 1) * PER_STEP
+        early = (last - 1) * LEAD
 
         @pl.loop(0, steps - early)
         def _(step):

time: 603 us -> 591 us (0.980)
  Pallas kernels: 591 us -> 579 us
    pallas_call x1, Pallas kernels: 340 us -> 327 us  [close(): pl.pallas_call(functools.partial(close_kernel, n_line, n_fsdp), in_specs=...]
where the time goes in v8:
time: 591 us; the launch traced here: 590 us
  Pallas kernels  579 us (98%)
    pallas_call x1, Pallas kernels, close(): pl.pallas_call(functools.partial(close_kernel, n_line, n_fsdp), in_specs=...  327 us
    pallas_call x1, Pallas kernels, core(): pl.pallas_call(functools.partial(core_kernel, group, n_line), in_specs=[A...  230 us
    pallas_call x1, Pallas kernels, tail(): pl.pallas_call(functools.partial(tail_kernel, head_dim), grid=(GRAD_CHUNK...  21.1 us

profile of v8, /device:TPU:0, one launch (start us, length us, event | category | flops | bytes accessed | tf_op | source)
XLA Modules:
  0.0 589.9 jit_solution(608121773492243068)
XLA Ops:
  0.6 0.0 copy-start
  0.7 0.8 convert_element_type.10
  1.5 1.3 broadcast_in_dim.11.gain_ref
  2.8 1.4 copy_bitcast_fusion.1
  4.1 1.9 fusion
  6.0 1.3 pad_maximum_fusion.1
  7.3 0.0 copy-done
  7.3 0.6 copy.21
  8.0 1.8 pad_maximum_fusion.w_ref
  9.8 230.3 %core.1 = (bf16[1024,1536]{1,0:T(8,128)(2,1)}, bf16[1024,1024]{1,0:T(8,128)(2,1)}, f32[1,4096]{1,0:T(1,128)}, bf16[1024,4096]{1,0:T(8,128)(2,1)}, bf16[4,1024,15...) custom-call(bf16[1024,4096]{1,0:T(8,128)(2,1)} %bitcast.17, ...), custom_call_target="tpu_custom_call" | custom-call | tf_op jit(solution)/shard_map/core/pallas_call | solution.py:677
  240.0 327.5 %close.1 = (bf16[1024,4096]{1,0:T(8,128)(2,1)}, bf16[1024,4096]{1,0:T(8,128)(2,1)}, f32[1,1024]{1,0:T(1,128)}, f32[1024,2560]{1,0:T(8,128)}, f32[1024,2560]{1,0:...) custom-call(bf16[1024,1536]{1,0:T(8,128)(2,1)} %get-tuple-element.25.d_, ...), custom_call_target="tpu_custom_call" | custom-call | tf_op jit(solution)/shard_map/close/pallas_call | solution.py:1151
  567.5 21.1 %tail.1 = (bf16[1024,4096]{1,0:T(8,128)(2,1)}, bf16[1024,4096]{1,0:T(8,128)(2,1)}, f32[1024,8,128]{2,1,0:T(8,128)}, f32[1024,2,128]{2,1,0:T(2,128)}, f32[1024,2,128]{2,1,0:T(2,128)}, /*index=5*/f32[1024,1024]{1,0:T(8,128)}) custom-call(bf16[1024,4096]{1,0:T(8,128)(2,1)} %get-tuple-element.32.blk_ref, bf16[1024,4096]{1,0:T(8,128)(2,1)} %get-tuple-element.33.hid_ref, ...), custom_call_target="tpu_custom_call" | custom-call | tf_op jit(solution)/shard_map/tail/pallas_call | solution.py:1201
  588.7 1.3 copy.23
  (1 shorter events, 0.0 us)
Async XLA Ops:
  0.6 6.7 %copy-start = (bf16[1024,8,128]{2,1,0:T(8,128)(2,1)S(1)}, bf16[1024,8,128]{2,1,0:T(8,128)(2,1)}, u32[]{:S(2)}) copy-start(bf16[1024,8,128]{2,1,0:T(8,128)(2,1)} %param.12) | copy-start | bytes 6291460

commit v9 on v8

--- a/solution.py
+++ b/solution.py
@@ -16,13 +16,14 @@
 TILES = 4
 CHUNKS = 16
 LEAD = 2
+X_LEAD = 4
 QUARTERS = 3
 PIECES = 8
 O_PIECES = 2
 GRAD_CHUNKS = 8
 FIRST_X = 6
 EARLY = 6
-LATE = ((6, 4), (7, 9))
+LATE = ((6, 3), (7, 8))
 VMEM_BYTES = 67043328
 SIDES = range(2)
 
@@ -260,8 +261,8 @@
     for k, where, _ in gains:
         g_copy(k, where, f).start()
     sends = [x_copy(j) for j in range(PIECES)] + [ox_copy(j, f) for j in range(O_PIECES)]
-    for j in range(LEAD):
-        sends[j].start()
+    for copy in sends[:X_LEAD]:
+        copy.start()
     own_copy(f).start()
     all_rows = pl.ds(0, o_rows)
     for up in SIDES:
@@ -307,7 +308,8 @@
         x_in(j).wait_recv()
         y_copy(j, flag).start()
         d_copy(j, flag, f_x).start()
-        sends[j + LEAD].start()
+        for copy in sends[j + X_LEAD:j + X_LEAD + 1]:
+            copy.start()
 
     def y_tick(j):
         y_copy(j, far).wait_recv()

time: 591 us -> 592 us (level)
  no operation moved by 1% of the time
where the time goes in v9:
time: 592 us; the launch traced here: 591 us
  Pallas kernels  580 us (98%)
    pallas_call x1, Pallas kernels, close(): pl.pallas_call(functools.partial(close_kernel, n_line, n_fsdp), in_specs=...  329 us
    pallas_call x1, Pallas kernels, core(): pl.pallas_call(functools.partial(core_kernel, group, n_line), in_specs=[A...  230 us
    pallas_call x1, Pallas kernels, tail(): pl.pallas_call(functools.partial(tail_kernel, head_dim), grid=(GRAD_CHUNK...  21.1 us

profile of v9, /device:TPU:0, one launch (start us, length us, event | category | flops | bytes accessed | tf_op | source)
XLA Modules:
  0.0 591.3 jit_solution(13418810570868542584)
XLA Ops:
  0.6 0.0 copy-start
  0.7 0.8 convert_element_type.10
  1.5 1.3 broadcast_in_dim.11.gain_ref
  2.8 1.4 copy_bitcast_fusion.1
  4.1 1.9 fusion
  6.0 1.3 pad_maximum_fusion.1
  7.3 0.0 copy-done
  7.3 0.6 copy.21
  8.0 1.8 pad_maximum_fusion.w_ref
  9.8 230.3 %core.1 = (bf16[1024,1536]{1,0:T(8,128)(2,1)}, bf16[1024,1024]{1,0:T(8,128)(2,1)}, f32[1,4096]{1,0:T(1,128)}, bf16[1024,4096]{1,0:T(8,128)(2,1)}, bf16[4,1024,15...) custom-call(bf16[1024,4096]{1,0:T(8,128)(2,1)} %bitcast.17, ...), custom_call_target="tpu_custom_call" | custom-call | tf_op jit(solution)/shard_map/core/pallas_call | solution.py:679
  240.0 328.8 %close.1 = (bf16[1024,4096]{1,0:T(8,128)(2,1)}, bf16[1024,4096]{1,0:T(8,128)(2,1)}, f32[1,1024]{1,0:T(1,128)}, f32[1024,2560]{1,0:T(8,128)}, f32[1024,2560]{1,0:...) custom-call(bf16[1024,1536]{1,0:T(8,128)(2,1)} %get-tuple-element.25.d_, ...), custom_call_target="tpu_custom_call" | custom-call | tf_op jit(solution)/shard_map/close/pallas_call | solution.py:1153
  568.8 21.1 %tail.1 = (bf16[1024,4096]{1,0:T(8,128)(2,1)}, bf16[1024,4096]{1,0:T(8,128)(2,1)}, f32[1024,8,128]{2,1,0:T(8,128)}, f32[1024,2,128]{2,1,0:T(2,128)}, f32[1024,2,128]{2,1,0:T(2,128)}, /*index=5*/f32[1024,1024]{1,0:T(8,128)}) custom-call(bf16[1024,4096]{1,0:T(8,128)(2,1)} %get-tuple-element.32.blk_ref, bf16[1024,4096]{1,0:T(8,128)(2,1)} %get-tuple-element.33.hid_ref, ...), custom_call_target="tpu_custom_call" | custom-call | tf_op jit(solution)/shard_map/tail/pallas_call | solution.py:1203
  590.0 1.3 copy.23
  (1 shorter events, 0.0 us)
Async XLA Ops:
  0.6 6.7 %copy-start = (bf16[1024,8,128]{2,1,0:T(8,128)(2,1)S(1)}, bf16[1024,8,128]{2,1,0:T(8,128)(2,1)}, u32[]{:S(2)}) copy-start(bf16[1024,8,128]{2,1,0:T(8,128)(2,1)} %param.12) | copy-start | bytes 6291460

commit v10 on v8

--- a/solution.py
+++ b/solution.py
@@ -22,6 +22,7 @@
 GRAD_CHUNKS = 8
 FIRST_X = 6
 EARLY = 6
+GAIN_AT = 10
 LATE = ((6, 4), (7, 9))
 VMEM_BYTES = 67043328
 SIDES = range(2)
@@ -1076,6 +1077,18 @@
             def _():
                 o_load.wait()
 
+            @pl.when(step == GAIN_AT)
+            def _():
+                gb_copy().wait()
+                for k in range(n_fsdp):
+                    gt[k] = gs[:, blk(k, feat)] + gb[:, blk(k, feat)]
+                gc[f] = gt[f]
+
+            @pl.when(step == GAIN_AT + 1)
+            def _():
+                for k in range(1, n_fsdp):
+                    gc_copy(k, f).start()
+
             @pl.when(step > 0)
             def _():
                 first = (step - 1) * QUARTERS
@@ -1101,10 +1114,6 @@
         pltpu.VMEM((2, d_ref.shape[0], min(512, feat)), BF),
     )
 
-    gb_copy().wait()
-    for k in range(n_fsdp):
-        gt[k] = gs[:, blk(k, feat)] + gb[:, blk(k, feat)]
-    gc[f] = gt[f]
     for side in SIDES:
         @pl.when(dist(side) > 0)
         def _():
@@ -1116,8 +1125,6 @@
     def _(j):
         x_copy(j).wait_send()
 
-    for k in range(1, n_fsdp):
-        gc_copy(k, f).start()
     for k in range(1, n_fsdp):
         gc_copy(k, lax.rem(f + n_fsdp - k, n_fsdp)).wait_recv()
     gg_ref[...] = sum(gc[k] for k in range(n_fsdp))

time: 591 us -> 589 us (level)
  no operation moved by 1% of the time
where the time goes in v10:
time: 589 us; the launch traced here: 588 us
  Pallas kernels  577 us (98%)
    pallas_call x1, Pallas kernels, close(): pl.pallas_call(functools.partial(close_kernel, n_line, n_fsdp), in_specs=...  326 us
    pallas_call x1, Pallas kernels, core(): pl.pallas_call(functools.partial(core_kernel, group, n_line), in_specs=[A...  230 us
    pallas_call x1, Pallas kernels, tail(): pl.pallas_call(functools.partial(tail_kernel, head_dim), grid=(GRAD_CHUNK...  21.1 us

profile of v10, /device:TPU:0, one launch (start us, length us, event | category | flops | bytes accessed | tf_op | source)
XLA Modules:
  0.0 588.4 jit_solution(14855848524737767028)
XLA Ops:
  0.6 0.0 copy-start
  0.7 0.8 convert_element_type.10
  1.5 1.3 broadcast_in_dim.11.gain_ref
  2.8 1.4 copy_bitcast_fusion.1
  4.1 1.9 fusion
  6.0 1.3 pad_maximum_fusion.1
  7.3 0.0 copy-done
  7.3 0.6 copy.21
  8.0 1.8 pad_maximum_fusion.w_ref
  9.8 230.3 %core.1 = (bf16[1024,1536]{1,0:T(8,128)(2,1)}, bf16[1024,1024]{1,0:T(8,128)(2,1)}, f32[1,4096]{1,0:T(1,128)}, bf16[1024,4096]{1,0:T(8,128)(2,1)}, bf16[4,1024,15...) custom-call(bf16[1024,4096]{1,0:T(8,128)(2,1)} %bitcast.17, ...), custom_call_target="tpu_custom_call" | custom-call | tf_op jit(solution)/shard_map/core/pallas_call | solution.py:678
  240.0 326.0 %close.1 = (bf16[1024,4096]{1,0:T(8,128)(2,1)}, bf16[1024,4096]{1,0:T(8,128)(2,1)}, f32[1,1024]{1,0:T(1,128)}, f32[1024,2560]{1,0:T(8,128)}, f32[1024,2560]{1,0:...) custom-call(bf16[1024,1536]{1,0:T(8,128)(2,1)} %get-tuple-element.25.d_, ...), custom_call_target="tpu_custom_call" | custom-call | tf_op jit(solution)/shard_map/close/pallas_call | solution.py:1158
  566.0 21.1 %tail.1 = (bf16[1024,4096]{1,0:T(8,128)(2,1)}, bf16[1024,4096]{1,0:T(8,128)(2,1)}, f32[1024,8,128]{2,1,0:T(8,128)}, f32[1024,2,128]{2,1,0:T(2,128)}, f32[1024,2,128]{2,1,0:T(2,128)}, /*index=5*/f32[1024,1024]{1,0:T(8,128)}) custom-call(bf16[1024,4096]{1,0:T(8,128)(2,1)} %get-tuple-element.32.blk_ref, bf16[1024,4096]{1,0:T(8,128)(2,1)} %get-tuple-element.33.hid_ref, ...), custom_call_target="tpu_custom_call" | custom-call | tf_op jit(solution)/shard_map/tail/pallas_call | solution.py:1208
  587.2 1.3 copy.23
  (1 shorter events, 0.0 us)
Async XLA Ops:
  0.6 6.7 %copy-start = (bf16[1024,8,128]{2,1,0:T(8,128)(2,1)S(1)}, bf16[1024,8,128]{2,1,0:T(8,128)(2,1)}, u32[]{:S(2)}) copy-start(bf16[1024,8,128]{2,1,0:T(8,128)(2,1)} %param.12) | copy-start | bytes 6291460
